TPU v7x, 32 devices: a whole 2x2x4 slice. The times are simulated.
32 devices in a mesh: fsdp: 8 (over y, x, core), tensor: 4 (over z).
Axes of the slice: x: 2, y: 2, z: 4, core: 2. Of those that a mesh axis runs over, the one named last changes fastest.
Arguments:
- block_input: bfloat16 [8192, 2048], P(('fsdp', 'tensor')), may hold values from -6 to 6
- doc_ids: int32 [8, 1024], P('fsdp'), may hold values from 0 to 5, never falling along the last dimension, each value on 1 to 512 neighbouring positions
- w_query: bfloat16 [1, 2048, 2048], P(None, 'fsdp', 'tensor')
- w_keyval: bfloat16 [1, 2048, 8, 128], P(None, 'fsdp', 'tensor')
- w_attn_out: bfloat16 [1, 2048, 2048], P(None, 'tensor', 'fsdp'), may hold values from -0.5 to 0.5
- w_gate_up: bfloat16 [1, 2048, 2, 8192], P(None, 'fsdp', None, 'tensor'), may hold values from -0.125 to 0.125
- w_down: bfloat16 [1, 8192, 2048], P(None, 'tensor', 'fsdp'), may hold values from -0.0625 to 0.0625
- norm_gains: bfloat16 [1, 2, 2048], P(None, None, 'fsdp'), may hold values from 0.5 to 1.5
- out_cotangent: float32 [8192, 2048], P(('fsdp', 'tensor')), may hold values from -6 to 6
Outputs:
- block_output: float32 [8192, 2048], P(('fsdp', 'tensor'))
- grad_input: float32 [8192, 2048], P(('fsdp', 'tensor'))
- grad_w_query: float32 [1, 2048, 2048], P(None, 'fsdp', 'tensor')
- grad_w_keyval: float32 [1, 2048, 8, 128], P(None, 'fsdp', 'tensor')
- grad_w_attn_out: float32 [1, 2048, 2048], P(None, 'tensor', 'fsdp')
- grad_w_gate_up: float32 [1, 2048, 2, 8192], P(None, 'fsdp', None, 'tensor')
- grad_w_down: float32 [1, 8192, 2048], P(None, 'tensor', 'fsdp')
- grad_norm_gains: float32 [1, 2, 2048], P(None, None, 'fsdp')
Inputs may be any that keep to these rules, and one draw needn't show every extreme that they name: `doc_ids`: in each row document numbers never fall, every number of 0 to 5 appears, each document holds 1 to 512 tokens and one holds exactly 512.
All inputs are finite; a program needn't handle non-finite values.
Results may differ from a plain program's by a relative error of at most 0.014.
Values may be sent and summed in bfloat16 or wider, within the bound.
A program may use at most 320 MiB of HBM per device.

v0:
```python
import jax
import jax.numpy as jnp
from jax import lax
from jax.sharding import PartitionSpec as P

MAXLEN = 512


NORM_EPSILON = 1e-05
ROPE_BASE = 500000.0


def norm_apply(residual, gain):
    inverse = lax.rsqrt(jnp.mean(residual * residual, axis=-1, keepdims=True) + NORM_EPSILON)
    return (inverse, (residual * inverse * gain.astype(jnp.float32)).astype(jnp.bfloat16))


def norm_back(residual, inverse, gain, grad_normed):
    scaled = grad_normed * gain.astype(jnp.float32)
    grad_gain = jnp.sum(grad_normed * residual * inverse, axis=0)
    grad_residual = inverse * scaled - residual * inverse * inverse * inverse * jnp.mean(
        scaled * residual, axis=-1, keepdims=True
    )
    return (grad_residual, grad_gain)


def rope_tables(doc_row, head_size):
    places = jnp.arange(doc_row.shape[0], dtype=jnp.int32)
    doc_start = jnp.concatenate([jnp.array([True]), doc_row[1:] != doc_row[:-1]])
    starts = lax.cummax(jnp.where(doc_start, places, 0), axis=0)
    exponent = jnp.arange(head_size // 2, dtype=jnp.float32) * (-2.0 / head_size)
    angles = (places - starts).astype(jnp.float32)[:, None] * jnp.power(ROPE_BASE, exponent)[
        None, :
    ]
    return (jnp.cos(angles), jnp.sin(angles))


def rotate(vectors, cosine, sine_table, direction_sign):
    half_size = vectors.shape[-1] // 2
    table_shape = (vectors.shape[0],) + (1,) * (vectors.ndim - 2) + (half_size,)
    cos_part = cosine.reshape(table_shape)
    sin_part = direction_sign * sine_table.reshape(table_shape)
    first_half = vectors[..., :half_size]
    second = vectors[..., half_size:]
    return jnp.concatenate(
        [first_half * cos_part - second * sin_part, second * cos_part + first_half * sin_part],
        axis=-1,
    )


def block_mask(doc_row, block_start, block_rows, key_low, key_high):
    places = jnp.arange(doc_row.shape[0], dtype=jnp.int32)
    own_docs = doc_row[block_start : block_start + block_rows]
    own_places = places[block_start : block_start + block_rows]
    return (own_docs[:, None] == doc_row[None, key_low:key_high]) & (
        places[None, key_low:key_high] <= own_places[:, None]
    )


def attend_block(query_rows, key_rows, value_rows, allowed, score_scale):
    scores = (
        jnp.einsum("qkgd,skd->kgqs", query_rows, key_rows, preferred_element_type=jnp.float32)
        * score_scale
    )
    scores = jnp.where(allowed[None, None], scores, -jnp.inf)
    row_max = jnp.max(scores, axis=-1, keepdims=True)
    log_total = row_max + jnp.log(jnp.sum(jnp.exp(scores - row_max), axis=-1, keepdims=True))
    probabilities = jnp.exp(scores - log_total).astype(jnp.bfloat16)
    attn_out = jnp.einsum(
        "kgqs,skd->qkgd", probabilities, value_rows, preferred_element_type=jnp.float32
    )
    return (attn_out.astype(jnp.bfloat16), log_total)


def attend_back(
    query_rows, key_rows, value_rows, allowed, log_total, out_rows, grad_out, score_scale
):
    scores = (
        jnp.einsum("qkgd,skd->kgqs", query_rows, key_rows, preferred_element_type=jnp.float32)
        * score_scale
    )
    scores = jnp.where(allowed[None, None], scores, -jnp.inf)
    probabilities = jnp.exp(scores - log_total)
    row_delta = jnp.einsum("qkgd,qkgd->kgq", grad_out, out_rows, preferred_element_type=jnp.float32)
    grad_probs = jnp.einsum(
        "qkgd,skd->kgqs", grad_out, value_rows, preferred_element_type=jnp.float32
    )
    grad_scores = (probabilities * (grad_probs - row_delta[..., None]) * score_scale).astype(
        jnp.bfloat16
    )
    grad_query = jnp.einsum(
        "kgqs,skd->qkgd", grad_scores, key_rows, preferred_element_type=jnp.float32
    )
    grad_key = jnp.einsum(
        "kgqs,qkgd->skd", grad_scores, query_rows, preferred_element_type=jnp.float32
    )
    grad_value = jnp.einsum(
        "kgqs,qkgd->skd",
        probabilities.astype(jnp.bfloat16),
        grad_out,
        preferred_element_type=jnp.float32,
    )
    return (grad_query, grad_key, grad_value)


def per_device(
    block_input,
    doc_ids,
    w_query,
    w_keyval,
    w_attn_out,
    w_gate_up,
    w_down,
    norm_gains,
    out_cotangent,
):
    layers = w_query.shape[0]
    doc_row = doc_ids[0]
    row_count = doc_row.shape[0]
    local_rows = block_input.shape[0]
    kv_local = w_keyval.shape[2]
    head_size = w_keyval.shape[3] // 2
    group_size = w_query.shape[2] // (kv_local * head_size)
    block_rows = min(512, row_count)
    score_scale = head_size ** (-0.5)
    cosine, sine_table = rope_tables(doc_row, head_size)
    block_starts = list(range(0, row_count, block_rows))
    windows = [
        (max(0, block_start - MAXLEN), block_start + block_rows) for block_start in block_starts
    ]
    mask_list = [
        block_mask(
            doc_row, block_start, block_rows, windows[block_index][0], windows[block_index][1]
        )
        for block_index, block_start in enumerate(block_starts)
    ]

    def spread(rows_local):
        return lax.all_gather(rows_local, "tensor", axis=0, tiled=True)

    def collect(term_fn):
        return lax.psum_scatter(
            term_fn(jnp.int32(0), lax.axis_size("tensor") * local_rows),
            "tensor",
            scatter_dimension=0,
            tiled=True,
        )

    def spread_grad(rows_local):
        return lax.all_gather(rows_local, "tensor", axis=0, tiled=True)

    def collect_grad(term_fn):
        return lax.psum_scatter(
            term_fn(jnp.int32(0), lax.axis_size("tensor") * local_rows),
            "tensor",
            scatter_dimension=0,
            tiled=True,
        )

    residual = block_input.astype(jnp.float32)
    layer_index = 0
    weights = (
        lax.all_gather(w_query[layer_index], "fsdp", axis=0, tiled=True),
        lax.all_gather(w_keyval[layer_index], "fsdp", axis=0, tiled=True),
        lax.all_gather(w_attn_out[layer_index], "fsdp", axis=1, tiled=True),
        lax.all_gather(w_gate_up[layer_index], "fsdp", axis=0, tiled=True),
        lax.all_gather(w_down[layer_index], "fsdp", axis=1, tiled=True),
        lax.all_gather(norm_gains[layer_index], "fsdp", axis=1, tiled=True),
    )
    w_query_all, w_keyval_all, w_out_all, w_gate_all, w_down_all, gains_all = weights
    model_width = w_query_all.shape[0]
    inv_attn, normed = norm_apply(residual, gains_all[0])
    normed_all = spread(normed)
    query_full = jnp.dot(normed_all, w_query_all, preferred_element_type=jnp.float32).reshape(
        row_count, kv_local, group_size, head_size
    )
    keyval = jnp.dot(
        normed_all, w_keyval_all.reshape(model_width, -1), preferred_element_type=jnp.float32
    ).reshape(row_count, kv_local, 2 * head_size)
    query_rows = rotate(query_full, cosine, sine_table, 1.0).astype(jnp.bfloat16)
    key_rows = rotate(keyval[..., :head_size], cosine, sine_table, 1.0).astype(jnp.bfloat16)
    value_rows = keyval[..., head_size:].astype(jnp.bfloat16)
    out_list = []
    total_list = []
    for block_index, block_start in enumerate(block_starts):
        key_low, key_high = windows[block_index]
        out_block, log_total = attend_block(
            query_rows[block_start : block_start + block_rows],
            key_rows[key_low:key_high],
            value_rows[key_low:key_high],
            mask_list[block_index],
            score_scale,
        )
        out_list.append(out_block)
        total_list.append(log_total)
    attended = jnp.concatenate(out_list, axis=0).reshape(row_count, -1)

    def attn_term(row_start, row_size):
        return jnp.dot(attended, w_out_all, preferred_element_type=jnp.float32)

    middle = residual + collect(attn_term)
    inv_mlp, normed_mlp = norm_apply(middle, gains_all[1])
    normed_mlp_all = spread(normed_mlp)
    gate_up = jnp.dot(
        normed_mlp_all, w_gate_all.reshape(model_width, -1), preferred_element_type=jnp.float32
    ).reshape(row_count, 2, -1)
    gate_value = gate_up[:, 0]
    up_value = gate_up[:, 1]
    hidden = (jax.nn.silu(gate_value) * up_value).astype(jnp.bfloat16)

    def mlp_term(row_start, row_size):
        return jnp.dot(hidden, w_down_all, preferred_element_type=jnp.float32)

    new_rows = middle + collect(mlp_term)
    stored = [
        (
            residual,
            inv_attn,
            normed_all,
            query_rows,
            key_rows,
            value_rows,
            attended,
            total_list,
            middle,
            inv_mlp,
            normed_mlp_all,
            gate_value,
            up_value,
            hidden,
        )
    ]
    kept_weights = [weights]
    residual = new_rows
    output_rows = residual
    grad_rows = out_cotangent
    layer_grads = [None] * layers
    for layer_index in reversed(range(layers)):
        weights = kept_weights[layer_index]
        w_query_all, w_keyval_all, w_out_all, w_gate_all, w_down_all, gains_all = weights
        model_width = w_query_all.shape[0]
        (
            residual,
            inv_attn,
            normed_all,
            query_rows,
            key_rows,
            value_rows,
            attended,
            total_list,
            middle,
            inv_mlp,
            normed_mlp_all,
            gate_value,
            up_value,
            hidden,
        ) = stored[layer_index]
        grad_all = spread_grad(grad_rows.astype(jnp.bfloat16))
        grad_down = jnp.dot(hidden.T, grad_all, preferred_element_type=jnp.float32)
        grad_hidden = jnp.dot(grad_all, w_down_all.T, preferred_element_type=jnp.float32)
        sigmoid_gate = jax.nn.sigmoid(gate_value)
        grad_gate = (
            grad_hidden * up_value * sigmoid_gate * (1.0 + gate_value * (1.0 - sigmoid_gate))
        )
        grad_up = grad_hidden * jax.nn.silu(gate_value)
        grad_gate_up = (
            jnp.stack([grad_gate, grad_up], axis=1).astype(jnp.bfloat16).reshape(row_count, -1)
        )
        grad_wgu = jnp.dot(
            normed_mlp_all.T, grad_gate_up, preferred_element_type=jnp.float32
        ).reshape(w_gate_all.shape)

        def mlp_back(row_start, row_size):
            return jnp.dot(
                grad_gate_up,
                w_gate_all.reshape(model_width, -1).T,
                preferred_element_type=jnp.float32,
            )

        norm_part, grad_gain_mlp = norm_back(middle, inv_mlp, gains_all[1], collect_grad(mlp_back))
        grad_middle = grad_rows + norm_part
        middle_all = spread_grad(grad_middle.astype(jnp.bfloat16))
        grad_wo = jnp.dot(attended.T, middle_all, preferred_element_type=jnp.float32)
        grad_attended = (
            jnp.dot(middle_all, w_out_all.T, preferred_element_type=jnp.float32)
            .astype(jnp.bfloat16)
            .reshape(row_count, kv_local, group_size, head_size)
        )
        attended_heads = attended.reshape(row_count, kv_local, group_size, head_size)
        grad_keys = jnp.zeros((row_count, kv_local, head_size), jnp.float32)
        grad_values = jnp.zeros((row_count, kv_local, head_size), jnp.float32)
        query_grads = []
        for block_index, block_start in enumerate(block_starts):
            block_stop = block_start + block_rows
            key_low, key_high = windows[block_index]
            grad_query_block, grad_key_part, grad_value_part = attend_back(
                query_rows[block_start:block_stop],
                key_rows[key_low:key_high],
                value_rows[key_low:key_high],
                mask_list[block_index],
                total_list[block_index],
                attended_heads[block_start:block_stop],
                grad_attended[block_start:block_stop],
                score_scale,
            )
            query_grads.append(grad_query_block)
            pad_width = ((key_low, row_count - key_high), (0, 0), (0, 0))
            grad_keys = grad_keys + jnp.pad(grad_key_part, pad_width)
            grad_values = grad_values + jnp.pad(grad_value_part, pad_width)
        grad_query = (
            rotate(jnp.concatenate(query_grads, axis=0), cosine, sine_table, -1.0)
            .astype(jnp.bfloat16)
            .reshape(row_count, -1)
        )
        grad_keyval = (
            jnp.concatenate([rotate(grad_keys, cosine, sine_table, -1.0), grad_values], axis=-1)
            .astype(jnp.bfloat16)
            .reshape(row_count, -1)
        )
        grad_wq = jnp.dot(normed_all.T, grad_query, preferred_element_type=jnp.float32)
        grad_wkv = jnp.dot(normed_all.T, grad_keyval, preferred_element_type=jnp.float32).reshape(
            w_keyval_all.shape
        )

        def attn_back(row_start, row_size):
            return jnp.dot(grad_query, w_query_all.T, preferred_element_type=jnp.float32) + jnp.dot(
                grad_keyval,
                w_keyval_all.reshape(model_width, -1).T,
                preferred_element_type=jnp.float32,
            )

        norm_part, grad_gain_attn = norm_back(
            residual, inv_attn, gains_all[0], collect_grad(attn_back)
        )
        grad_rows = grad_middle + norm_part
        gain_total = lax.psum(jnp.stack([grad_gain_attn, grad_gain_mlp]), "tensor")
        local_set = (grad_wq, grad_wkv, grad_wo, grad_wgu, grad_down, gain_total)
        layer_grads[layer_index] = (
            lax.psum_scatter(local_set[0], "fsdp", scatter_dimension=0, tiled=True),
            lax.psum_scatter(local_set[1], "fsdp", scatter_dimension=0, tiled=True),
            lax.psum_scatter(local_set[2], "fsdp", scatter_dimension=1, tiled=True),
            lax.psum_scatter(local_set[3], "fsdp", scatter_dimension=0, tiled=True),
            lax.psum_scatter(local_set[4], "fsdp", scatter_dimension=1, tiled=True),
            lax.psum_scatter(local_set[5], "fsdp", scatter_dimension=1, tiled=True),
        )
    stacked = tuple((jnp.stack([layer_grads[0][member]]) for member in range(6)))
    return (
        output_rows,
        grad_rows,
        stacked[0],
        stacked[1],
        stacked[2],
        stacked[3],
        stacked[4],
        stacked[5],
    )


def solution(mesh):
    return jax.shard_map(
        per_device,
        mesh=mesh,
        in_specs=(
            P(("fsdp", "tensor"), None),
            P("fsdp", None),
            P(None, "fsdp", "tensor"),
            P(None, "fsdp", "tensor", None),
            P(None, "tensor", "fsdp"),
            P(None, "fsdp", None, "tensor"),
            P(None, "tensor", "fsdp"),
            P(None, None, "fsdp"),
            P(("fsdp", "tensor"), None),
        ),
        out_specs=(
            P(("fsdp", "tensor"), None),
            P(("fsdp", "tensor"), None),
            P(None, "fsdp", "tensor"),
            P(None, "fsdp", "tensor", None),
            P(None, "tensor", "fsdp"),
            P(None, "fsdp", None, "tensor"),
            P(None, "tensor", "fsdp"),
            P(None, None, "fsdp"),
        ),
        check_vma=False,
    )
```

profile of v0, /device:TPU:0, one launch (start us, length us, event | category | flops | bytes accessed | tf_op | source)
XLA Modules:
  0.0 1809.7 jit_solution(13145227916705328422)
XLA Ops:
  8.9 10.6 all-gather
  28.3 8.3 all-gather.24.cloned.1.call-done
  38.1 81.4 %all-gather.16.cloned.1.call-done = bf16[1024,2048]{1,0:T(8,128)(2,1)} async-done(((bf16[256,2048]{1,0:T(8,128)(2,1)}), bf16[1024,2048]{1,0:T(8,128)(2,1)}) %all-gather.16.cloned.1.call-update) | async-done | bytes 4194320 | tf_op jit(solution)/shard_map/all_gather | solution.py:139
  123.1 24.6 %all-gather.26.cloned.1.call-done = bf16[1,2048,512]{2,1,0:T(8,128)(2,1)} async-done(((bf16[1,256,512]{2,1,0:T(8,128)(2,1)}), bf16[1,2048,512]{2,1,0:T(8,128)(2,1)}) %all-gather.26.cloned.1.call-update) | async-done | bytes 2097168 | tf_op jit(solution)/shard_map/all_gather | solution.py:163
  147.7 5.2 fusion.47
  154.8 8.2 fusion.8
  165.1 9.5 exponential_reduce_fusion
  174.6 5.7 convolution_convert_fusion.1
  180.3 8.2 convolution_convert_fusion
  189.5 7.6 fusion.43
  201.0 140.9 %reduce-scatter.13.cloned.1.call-done = f32[256,2048]{1,0:T(8,128)} async-done(((f32[1024,2048]{1,0:T(8,128)}), f32[256,2048]{1,0:T(8,128)}) %reduce-scatter.13.cloned.1.call-update) | async-done | bytes 2097168 | tf_op jit(solution)/shard_map/reduce_scatter | solution.py:142
  348.4 86.2 %all-gather.30.cloned.1.call-done = bf16[1,2048,2,2048]{3,1,2,0:T(8,128)(2,1)} async-done(((bf16[1,256,2,2048]{3,1,2,0:T(8,128)(2,1)}), bf16[1,2048,2,2048]{3,1,2,0:T(8,128)(2,1)}) %all-gather.30.cloned.1.call-update) | async-done | bytes 16777232 | tf_op jit(solution)/shard_map/all_gather | solution.py:166
  434.6 22.6 %copy.56 = bf16[1,2048,2,2048]{1,3,2,0:T(8,128)(2,1)} copy(bf16[1,2048,2,2048]{3,1,2,0:T(8,128)(2,1)} %all-gather.30.cloned.1.call-done) | data formatting | bytes 33554432 | tf_op jit(solution)/shard_map/all_gather | solution.py:166
  457.2 60.3 %all-gather.18.cloned.1.call-done = bf16[1024,2048]{1,0:T(8,128)(2,1)} async-done(((bf16[256,2048]{1,0:T(8,128)(2,1)}), bf16[1024,2048]{1,0:T(8,128)(2,1)}) %all-gather.18.cloned.1.call-update) | async-done | bytes 4194320 | tf_op jit(solution)/shard_map/all_gather | solution.py:139
  517.5 23.7 %fusion = f32[1024,2,2048]{2,0,1:T(8,128)} fusion(bf16[1,2048,2,2048]{1,3,2,0:T(8,128)(2,1)} %copy.56, bf16[1024,2048]{1,0:T(8,128)(2,1)} %all-gather.18.cloned.1.call-done), kind=kOutput, calls=%fused_computation.1 | convolution fusion | flops 17179869184 | bytes 37748736 | tf_op jit(solution)/shard_map/dot_general | solution.py:204
  541.2 57.7 %all-gather.20.cloned.1.call-done = bf16[1024,2048]{1,0:T(8,128)(2,1)} async-done(((bf16[256,2048]{1,0:T(8,128)(2,1)}), bf16[1024,2048]{1,0:T(8,128)(2,1)}) %all-gather.20.cloned.1.call-update) | async-done | bytes 4194320 | tf_op jit(solution)/shard_map/all_gather | solution.py:150
  598.9 56.3 %all-gather.32.cloned.1.call-done = bf16[1,2048,2048]{2,1,0:T(8,128)(2,1)} async-done(((bf16[1,2048,256]{2,1,0:T(8,128)(2,1)}), bf16[1,2048,2048]{2,1,0:T(8,128)(2,1)}) %all-gather.32.cloned.1.call-update) | async-done | bytes 8388624 | tf_op jit(solution)/shard_map/all_gather | solution.py:167
  655.2 19.8 %multiply_bitcast_fusion.1 = (bf16[1024,1,2048]{2,0,1:T(8,128)(2,1)S(1)}, bf16[1024,1,2048]{2,0,1:T(8,128)(2,1)}) fusion(f32[1024,2,2048]{2,0,1:T(8,128)} %fusion, bf16[1024,2048]{1,0:T(8,128)(2,1)} %all-gather.20.cloned.1.call-done, bf16[1,2048,2048]{2,1,0:T(8,128)(2,1)} %all-gather.32.cloned.1.call-done), kind=kOutput, calls=%fused_computation.29 | convolution fusion | flops 8617197568 | bytes 37748736 | tf_op jit(solution)/shard_map/dot_general | solution.py:260
  676.9 23.4 %fusion.21 = f32[1024,2048]{1,0:T(8,128)} fusion(bf16[1,2048,2,2048]{3,1,2,0:T(8,128)(2,1)} %all-gather.30.cloned.1.call-done, bf16[1024,1,2048]{2,0,1:T(8,128)(2,1)} %get-tuple-element.45, bf16[1024,1,2048]{2,0,1:T(8,128)(2,1)S(1)} %get-tuple-element.44), kind=kOutput, calls=%fused_computation.37 | convolution fusion | flops 17184063488 | bytes 33554432 | tf_op jit(solution)/shard_map/dot_general | solution.py:274
  700.4 7.1 multiply_convert_fusion
  709.5 13.2 fusion.16
  722.7 122.4 %reduce-scatter.17.cloned.1.call-done = f32[256,2048]{1,0:T(8,128)} async-done(((f32[1024,2048]{1,0:T(8,128)}), f32[256,2048]{1,0:T(8,128)}) %reduce-scatter.17.cloned.1.call-update) | async-done | bytes 2097168 | tf_op jit(solution)/shard_map/reduce_scatter | solution.py:153
  847.3 145.5 %reduce-scatter.15.cloned.1.call-done = f32[256,2048]{1,0:T(8,128)} async-done(((f32[1024,2048]{1,0:T(8,128)}), f32[256,2048]{1,0:T(8,128)}) %reduce-scatter.15.cloned.1.call-update) | async-done | bytes 2097168 | tf_op jit(solution)/shard_map/reduce_scatter | solution.py:142
  992.7 6.0 fusion.83
  999.3 81.0 %all-gather.22.cloned.1.call-done = bf16[1024,2048]{1,0:T(8,128)(2,1)} async-done(((bf16[256,2048]{1,0:T(8,128)(2,1)}), bf16[1024,2048]{1,0:T(8,128)(2,1)}) %all-gather.22.cloned.1.call-update) | async-done | bytes 4194320 | tf_op jit(solution)/shard_map/all_gather | solution.py:150
  1080.3 5.2 fusion.50
  1087.3 6.3 convolution_bitcast_fusion.4
  1093.6 5.3 fusion.13
  1102.9 6.3 fusion.54
  1109.2 9.6 fusion.4
  1118.9 5.1 convolution_bitcast_fusion.1
  1131.3 4.6 bitcast_add_fusion
  1136.0 4.9 fusion.26
  1141.0 7.6 maximum_convert_fusion
  1148.6 11.9 copy.65
  1160.5 118.7 %reduce-scatter.19.cloned.1.call-done = f32[256,2048]{1,0:T(8,128)} async-done(((f32[1024,2048]{1,0:T(8,128)}), f32[256,2048]{1,0:T(8,128)}) %reduce-scatter.19.cloned.1.call-update) | async-done | bytes 2097168 | tf_op jit(solution)/shard_map/reduce_scatter | solution.py:153
  1282.8 25.5 %fusion.9 = f32[2048,2,2048]{2,0,1:T(8,128)} fusion(bf16[1024,2,2048]{0,2,1:T(8,128)(2,1)} %copy.65, bf16[1024,2048]{1,0:T(8,128)(2,1)} %all-gather.18.cloned.1.call-done), kind=kOutput, calls=%fused_computation.16 | convolution fusion | flops 17179869184 | bytes 46137344 | tf_op jit(solution)/shard_map/dot_general | solution.py:269
  1308.4 15.3 fusion.90
  1324.9 6.6 fusion.89
  1331.9 6.7 fusion.88
  1340.6 3.6 fusion.36
  1344.2 19.5 %reduce-scatter.31.cloned.1.call-done = f32[256,2]{1,0:T(8,128)} async-done(((f32[2048,2]{1,0:T(8,128)}), f32[256,2]{1,0:T(8,128)}) %reduce-scatter.31.cloned.1.call-update) | async-done | bytes 2064
  1364.7 12.3 psum.8
  1377.0 195.7 %reduce-scatter.27.cloned.1.call-done = f32[256,2,2048]{2,0,1:T(8,128)} async-done(((f32[2048,2,2048]{2,0,1:T(8,128)}), f32[256,2,2048]{2,0,1:T(8,128)}) %reduce-scatter.27.cloned.1.call-update) | async-done | bytes 4194320 | tf_op jit(solution)/shard_map/reduce_scatter | solution.py:342
  1572.7 7.4 copy.68
  1580.1 112.6 %reduce-scatter.29.cloned.1.call-done = f32[2048,256]{1,0:T(8,128)} async-done(((f32[2048,2048]{1,0:T(8,128)}), f32[2048,256]{1,0:T(8,128)}) %reduce-scatter.29.cloned.1.call-update) | async-done | bytes 2097168 | tf_op jit(solution)/shard_map/reduce_scatter | solution.py:343
  1692.7 54.9 %reduce-scatter.25.cloned.1.call-done = f32[512,256]{1,0:T(8,128)} async-done(((f32[512,2048]{1,0:T(8,128)}), f32[512,256]{1,0:T(8,128)}) %reduce-scatter.25.cloned.1.call-update) | async-done | bytes 524304 | tf_op jit(solution)/shard_map/reduce_scatter | solution.py:341
  1747.6 55.1 %reduce-scatter.21.cloned.1.call-done = f32[256,512]{1,0:T(8,128)} async-done(((f32[2048,512]{1,0:T(8,128)}), f32[256,512]{1,0:T(8,128)}) %reduce-scatter.21.cloned.1.call-update) | async-done | bytes 524304 | tf_op jit(solution)/shard_map/reduce_scatter | solution.py:339
  (202 shorter events, 58.4 us)
Async XLA Ops:
  7.2 18.3 %copy-start.41 = (s32[1,1024]{1,0:T(1,128)S(1)}, s32[1,1024]{1,0:T(1,128)}, u32[]{:S(2)}) copy-start(s32[1,1024]{1,0:T(1,128)} %param.11) | copy-start | bytes 12292
  7.2 29.4 %all-gather.24.cloned.1.call-start = ((), (), s32[]{:S(2)}) async-start(), calls=%async_computation.23 | async-start | bytes 1179648 | tf_op jit(solution)/shard_map/all_gather | solution.py:164
  8.8 110.7 %all-gather.16.cloned.1.call-start = ((), (), s32[]{:S(2)}) async-start(), calls=%async_computation.10 | async-start | bytes 5242880 | tf_op jit(solution)/shard_map/all_gather | solution.py:139
  21.0 322.8 %copy-start.39 = (f32[1,1,2048]{2,1,0:T(1,128)}, f32[1,1,2048]{2,1,0:T(1,128)S(1)}, u32[]{:S(2)}) copy-start(f32[1,1,2048]{2,1,0:T(1,128)S(1)} %get-tuple-element.57) | copy-start | bytes 24580
  24.1 123.6 %all-gather.26.cloned.1.call-start = ((), (), s32[]{:S(2)}) async-start(), calls=%async_computation.24 | async-start | bytes 2359296 | tf_op jit(solution)/shard_map/all_gather | solution.py:163
  24.9 164.6 %all-gather.28.cloned.1.call-start = ((), (), s32[]{:S(2)}) async-start(), calls=%async_computation.25 | async-start | bytes 2359296 | tf_op jit(solution)/shard_map/all_gather | solution.py:165
  25.4 316.4 %reduce-scatter.13.cloned.1.call-start = ((), (), s32[]{:S(2)}) async-start(), calls=%async_computation.11 | async-start | bytes 10485760 | tf_op jit(solution)/shard_map/reduce_scatter | solution.py:142
  26.6 148.0 %copy-start.31 = (pred[512,512]{0,1:T(8,128)(4,1)}, pred[512,512]{0,1:T(8,128)(4,1)S(1)}, u32[]{:S(2)}) copy-start(pred[512,512]{0,1:T(8,128)(4,1)S(1)} %compare_and_fusion) | copy-start | bytes 786436
  27.8 125.1 %copy-start.17 = (f32[1024,32]{0,1:T(8,128)}, f32[1024,32]{0,1:T(8,128)S(1)}, u32[]{:S(2)}) copy-start(f32[1024,32]{0,1:T(8,128)S(1)} %get-tuple-element.61) | copy-start | bytes 393220
  28.3 152.0 %copy-start.12 = (pred[512,1024]{0,1:T(8,128)(4,1)}, pred[512,1024]{0,1:T(8,128)(4,1)S(1)}, u32[]{:S(2)}) copy-start(pred[512,1024]{0,1:T(8,128)(4,1)S(1)} %fusion.49) | copy-start | bytes 1572868
  123.0 57.4 %copy-start.50 = (bf16[1024,2,128]{0,2,1:T(8,128)(2,1)}, bf16[1024,2,128]{0,2,1:T(8,128)(2,1)S(1)}, u32[]{:S(2)}) copy-start(bf16[1024,2,128]{0,2,1:T(8,128)(2,1)S(1)} %get-tuple-element.64) | copy-start | bytes 1572868
  123.1 31.7 %copy-start.19 = (bf16[1024,2,32]{0,2,1:T(8,128)(2,1)}, bf16[1024,2,32]{0,2,1:T(8,128)(2,1)S(1)}, u32[]{:S(2)}) copy-start(bf16[1024,2,32]{0,2,1:T(8,128)(2,1)S(1)} %get-tuple-element.51) | copy-start | bytes 393220
  123.1 31.7 %copy-start.22 = (bf16[1024,2,32]{0,2,1:T(8,128)(2,1)}, bf16[1024,2,32]{0,2,1:T(8,128)(2,1)S(1)}, u32[]{:S(2)}) copy-start(bf16[1024,2,32]{0,2,1:T(8,128)(2,1)S(1)} %get-tuple-element.52) | copy-start | bytes 393220
  154.8 8.5 copy-start.7
  165.1 9.6 copy-start.45
  180.3 8.2 copy-start.26
  189.5 7.6 copy-start.33
  197.1 144.8 %copy-start.3 = (bf16[256,2048]{1,0:T(8,128)(2,1)S(1)}, bf16[256,2048]{1,0:T(8,128)(2,1)}, u32[]{:S(2)}) copy-start(bf16[256,2048]{1,0:T(8,128)(2,1)} %param.10) | copy-start | bytes 3145732
  197.1 237.5 %all-gather.30.cloned.1.call-start = ((), (), s32[]{:S(2)}) async-start(), calls=%async_computation.26 | async-start | bytes 18874368 | tf_op jit(solution)/shard_map/all_gather | solution.py:166
  200.9 145.5 %copy-start.6 = (f32[256,2048]{1,0:T(8,128)S(1)}, f32[256,2048]{1,0:T(8,128)}, u32[]{:S(2)}) copy-start(f32[256,2048]{1,0:T(8,128)} %param.18) | copy-start | bytes 6291460
  200.9 316.6 %all-gather.18.cloned.1.call-start = ((), (), s32[]{:S(2)}) async-start(), calls=%async_computation.12 | async-start | bytes 5242880 | tf_op jit(solution)/shard_map/all_gather | solution.py:139
  346.4 252.5 %all-gather.20.cloned.1.call-start = ((), (), s32[]{:S(2)}) async-start(), calls=%async_computation.14 | async-start | bytes 5242880 | tf_op jit(solution)/shard_map/all_gather | solution.py:150
  347.6 307.6 %all-gather.32.cloned.1.call-start = ((), (), s32[]{:S(2)}) async-start(), calls=%async_computation.27 | async-start | bytes 9437184 | tf_op jit(solution)/shard_map/all_gather | solution.py:167
  348.3 496.8 %reduce-scatter.17.cloned.1.call-start = ((), (), s32[]{:S(2)}) async-start(), calls=%async_computation.15 | async-start | bytes 10485760 | tf_op jit(solution)/shard_map/reduce_scatter | solution.py:153
  700.4 292.4 %reduce-scatter.15.cloned.1.call-start = ((), (), s32[]{:S(2)}) async-start(), calls=%async_computation.13 | async-start | bytes 10485760 | tf_op jit(solution)/shard_map/reduce_scatter | solution.py:142
  722.7 122.5 %copy-start.2 = (f32[256,2048]{1,0:T(8,128)S(1)}, f32[256,2048]{1,0:T(8,128)}, u32[]{:S(2)}) copy-start(f32[256,2048]{1,0:T(8,128)} %copy-done.1) | copy-start | bytes 6291460
  722.7 122.5 %copy-start.40 = (f32[1,1,2048]{2,1,0:T(1,128)S(1)}, f32[1,1,2048]{2,1,0:T(1,128)}, u32[]{:S(2)}) copy-start(f32[1,1,2048]{2,1,0:T(1,128)} %copy-done.39) | copy-start | bytes 24580
  722.7 122.5 %copy-start.48 = (f32[256]{0:T(256)S(1)}, f32[256]{0:T(256)}, u32[]{:S(2)}) copy-start(f32[256]{0:T(256)} %copy-done.47) | copy-start | bytes 3076
  722.7 357.6 %all-gather.22.cloned.1.call-start = ((), (), s32[]{:S(2)}) async-start(), calls=%async_computation.16 | async-start | bytes 5242880 | tf_op jit(solution)/shard_map/all_gather | solution.py:150
  998.8 86.7 %copy-start.27 = (bf16[2,64,4,512]{3,1,2,0:T(8,128)(2,1)S(1)}, bf16[2,64,4,512]{3,1,2,0:T(8,128)(2,1)}, u32[]{:S(2)}) copy-start(bf16[2,64,4,512]{3,1,2,0:T(8,128)(2,1)} %copy-done.26) | copy-start | bytes 1572868
  998.8 86.7 %copy-start.29 = (bf16[2,64,4,512]{3,1,2,0:T(8,128)(2,1)S(1)}, bf16[2,64,4,512]{3,1,2,0:T(8,128)(2,1)}, u32[]{:S(2)}) copy-start(bf16[2,64,4,512]{3,1,2,0:T(8,128)(2,1)} %copy-done.28) | copy-start | bytes 1572868
  998.8 88.4 %copy-start.32 = (pred[512,512]{0,1:T(8,128)(4,1)S(1)}, pred[512,512]{0,1:T(8,128)(4,1)}, u32[]{:S(2)}) copy-start(pred[512,512]{0,1:T(8,128)(4,1)} %copy-done.31) | copy-start | bytes 786436
  998.8 88.4 %copy-start.46 = (f32[1,8,512]{2,1,0:T(8,128)S(1)}, f32[1,8,512]{2,1,0:T(8,128)}, u32[]{:S(2)}) copy-start(f32[1,8,512]{2,1,0:T(8,128)} %copy-done.45) | copy-start | bytes 49156
  998.8 280.4 %reduce-scatter.19.cloned.1.call-start = ((), (), s32[]{:S(2)}) async-start(), calls=%async_computation.17 | async-start | bytes 10485760 | tf_op jit(solution)/shard_map/reduce_scatter | solution.py:153
  1087.3 15.6 slice-start
  1087.3 15.6 slice-start.1
  1093.6 9.3 slice-start.2
  1109.2 9.6 copy-start.21
  1109.2 9.7 copy-start.24
  1136.0 202.6 %reduce-scatter.23.cloned.1.call-start = ((), (), s32[]{:S(2)}) async-start(), calls=%async_computation.19 | async-start | bytes 2359296 | tf_op jit(solution)/shard_map/reduce_scatter | solution.py:340
  1140.9 222.8 %reduce-scatter.31.cloned.1.call-start = ((), (), s32[]{:S(2)}) async-start(), calls=%async_computation.28 | async-start | bytes 1179648
  1148.6 130.7 %copy-start.4 = (bf16[256,2048]{1,0:T(8,128)(2,1)S(1)}, bf16[256,2048]{1,0:T(8,128)(2,1)}, u32[]{:S(2)}) copy-start(bf16[256,2048]{1,0:T(8,128)(2,1)} %param.10) | copy-start | bytes 3145732
  1148.6 130.7 %copy-start.38 = (f32[1,1,2048]{2,1,0:T(1,128)S(1)}, f32[1,1,2048]{2,1,0:T(1,128)}, u32[]{:S(2)}) copy-start(f32[1,1,2048]{2,1,0:T(1,128)} %copy-done.37) | copy-start | bytes 24580
  1148.6 130.7 %copy-start.43 = (f32[256]{0:T(256)S(1)}, f32[256]{0:T(256)}, u32[]{:S(2)}) copy-start(f32[256]{0:T(256)} %copy-done.42) | copy-start | bytes 3076
  1282.8 289.9 %reduce-scatter.27.cloned.1.call-start = ((), (), s32[]{:S(2)}) async-start(), calls=%async_computation.21 | async-start | bytes 37748736 | tf_op jit(solution)/shard_map/reduce_scatter | solution.py:342
  1308.3 384.4 %reduce-scatter.29.cloned.1.call-start = ((), (), s32[]{:S(2)}) async-start(), calls=%async_computation.22 | async-start | bytes 18874368 | tf_op jit(solution)/shard_map/reduce_scatter | solution.py:343
  1323.7 423.9 %reduce-scatter.25.cloned.1.call-start = ((), (), s32[]{:S(2)}) async-start(), calls=%async_computation.20 | async-start | bytes 4718592 | tf_op jit(solution)/shard_map/reduce_scatter | solution.py:341
  1331.6 471.2 %reduce-scatter.21.cloned.1.call-start = ((), (), s32[]{:S(2)}) async-start(), calls=%async_computation.18 | async-start | bytes 4718592 | tf_op jit(solution)/shard_map/reduce_scatter | solution.py:339
  (26 other events, 71.7 us)
Sparse Core Ops, SparseCore 0:
  10.5 26.0 all-gather.23
  38.7 80.7 all-gather.15
  121.4 26.2 all-gather.25
  149.4 28.0 all-gather.27
  197.2 144.6 reduce-scatter.12
  344.2 90.3 all-gather.29
  436.7 80.7 all-gather.17
  519.6 79.2 all-gather.19
  600.8 54.3 all-gather.31
  700.5 144.6 reduce-scatter.16
  847.5 145.2 reduce-scatter.14
  998.9 81.3 all-gather.21
  1136.1 143.0 reduce-scatter.18
  1282.4 41.7 reduce-scatter.22
  1327.7 35.9 reduce-scatter.30
  1367.2 205.4 reduce-scatter.26
  1576.7 115.9 reduce-scatter.28
  1696.5 51.0 reduce-scatter.24
  1751.5 51.1 reduce-scatter.20
where the time goes:
time: 1820 us; the launch traced here: 1810 us
  waiting for transfers between devices  1420 us (78%)
  matrix products  230 us (13%)
  local copies, waits for them, and re-layouts  63 us (3%)
  other arithmetic  53.5 us (3%)
  blocking collectives  22.8 us (1%)
    reduce_scatter x2, waiting for transfers between devices, collect(): lax.psum_scatter(term_fn(jnp.int32(0), lax.axis_size('tensor') * local_ro...  286 us
    reduce_scatter x2, waiting for transfers between devices, collect_grad(): lax.psum_scatter(term_fn(jnp.int32(0), lax.axis_size('tensor') * local_ro...  241 us
    reduce_scatter x1, waiting for transfers between devices, per_device(): lax.psum_scatter(local_set[3], 'fsdp', scatter_dimension=0, tiled=True)  196 us
    all_gather x2, waiting for transfers between devices, spread(): return lax.all_gather(rows_local, 'tensor', axis=0, tiled=True)  142 us
    all_gather x2, waiting for transfers between devices, spread_grad(): return lax.all_gather(rows_local, 'tensor', axis=0, tiled=True)  139 us
    reduce_scatter x1, waiting for transfers between devices, per_device(): lax.psum_scatter(local_set[4], 'fsdp', scatter_dimension=1, tiled=True)  113 us
    all_gather x1, waiting for transfers between devices, per_device(): lax.all_gather(w_gate_up[layer_index], 'fsdp', axis=0, tiled=True)  86.2 us
    all_gather x1, waiting for transfers between devices, per_device(): lax.all_gather(w_down[layer_index], 'fsdp', axis=1, tiled=True)  56.3 us
  transfers between devices with their start and end apart: 19, of which 17 were waited for; matrix products, arithmetic and copies ran while one was open for 12% of the time, Pallas kernels for 0%

commit v1 on v0

--- a/solution.py
+++ b/solution.py
@@ -140,22 +140,22 @@
 
     def collect(term_fn):
         return lax.psum_scatter(
-            term_fn(jnp.int32(0), lax.axis_size("tensor") * local_rows),
+            term_fn(jnp.int32(0), lax.axis_size("tensor") * local_rows).astype(jnp.bfloat16),
             "tensor",
             scatter_dimension=0,
             tiled=True,
-        )
+        ).astype(jnp.float32)
 
     def spread_grad(rows_local):
         return lax.all_gather(rows_local, "tensor", axis=0, tiled=True)
 
     def collect_grad(term_fn):
         return lax.psum_scatter(
-            term_fn(jnp.int32(0), lax.axis_size("tensor") * local_rows),
+            term_fn(jnp.int32(0), lax.axis_size("tensor") * local_rows).astype(jnp.bfloat16),
             "tensor",
             scatter_dimension=0,
             tiled=True,
-        )
+        ).astype(jnp.float32)
 
     residual = block_input.astype(jnp.float32)
     layer_index = 0
@@ -336,11 +336,11 @@
         gain_total = lax.psum(jnp.stack([grad_gain_attn, grad_gain_mlp]), "tensor")
         local_set = (grad_wq, grad_wkv, grad_wo, grad_wgu, grad_down, gain_total)
         layer_grads[layer_index] = (
-            lax.psum_scatter(local_set[0], "fsdp", scatter_dimension=0, tiled=True),
-            lax.psum_scatter(local_set[1], "fsdp", scatter_dimension=0, tiled=True),
-            lax.psum_scatter(local_set[2], "fsdp", scatter_dimension=1, tiled=True),
-            lax.psum_scatter(local_set[3], "fsdp", scatter_dimension=0, tiled=True),
-            lax.psum_scatter(local_set[4], "fsdp", scatter_dimension=1, tiled=True),
+            lax.psum_scatter(local_set[0].astype(jnp.bfloat16), "fsdp", scatter_dimension=0, tiled=True).astype(jnp.float32),
+            lax.psum_scatter(local_set[1].astype(jnp.bfloat16), "fsdp", scatter_dimension=0, tiled=True).astype(jnp.float32),
+            lax.psum_scatter(local_set[2].astype(jnp.bfloat16), "fsdp", scatter_dimension=1, tiled=True).astype(jnp.float32),
+            lax.psum_scatter(local_set[3].astype(jnp.bfloat16), "fsdp", scatter_dimension=0, tiled=True).astype(jnp.float32),
+            lax.psum_scatter(local_set[4].astype(jnp.bfloat16), "fsdp", scatter_dimension=1, tiled=True).astype(jnp.float32),
             lax.psum_scatter(local_set[5], "fsdp", scatter_dimension=1, tiled=True),
         )
     stacked = tuple((jnp.stack([layer_grads[0][member]]) for member in range(6)))

time: 1820 us -> 1390 us (0.76)
  waiting for transfers between devices: 1420 us -> 1000 us
    reduce_scatter x2, waiting for transfers between devices: 241 us -> 80.4 us  [collect_grad(): lax.psum_scatter(term_fn(jnp.int32(0), lax.axis_size('tensor') * local_ro...]
    reduce_scatter x5, waiting for transfers between devices: 418 us -> 276 us  [the longest x1 106 us: per_device(): lax.psum_scatter(local_set[3].astype(jnp.bfloat16), 'fsdp', scatter_dimen...]
    reduce_scatter x2, waiting for transfers between devices: 286 us -> 150 us  [collect(): lax.psum_scatter(term_fn(jnp.int32(0), lax.axis_size('tensor') * local_ro...]
  transfers between devices with their start and end apart: 19 -> 19, of which waited for: 17 -> 18; matrix products, arithmetic and copies ran while one was open for 12% -> 16% of each run, Pallas kernels for 0% -> 0%
where the time goes in v1:
time: 1390 us; the launch traced here: 1380 us
  waiting for transfers between devices  1000 us (72%)
  matrix products  222 us (16%)
  other arithmetic  67 us (5%)
  local copies, waits for them, and re-layouts  55.7 us (4%)
  blocking collectives  23 us (2%)
  between operations  15 us (1%)
    reduce_scatter x2, waiting for transfers between devices, collect(): lax.psum_scatter(term_fn(jnp.int32(0), lax.axis_size('tensor') * local_ro...  150 us
    all_gather x2, waiting for transfers between devices, spread(): return lax.all_gather(rows_local, 'tensor', axis=0, tiled=True)  142 us
    all_gather x2, waiting for transfers between devices, spread_grad(): return lax.all_gather(rows_local, 'tensor', axis=0, tiled=True)  139 us
    reduce_scatter x1, waiting for transfers between devices, per_device(): lax.psum_scatter(local_set[3].astype(jnp.bfloat16), 'fsdp', scatter_dimen...  106 us
    all_gather x1, waiting for transfers between devices, per_device(): lax.all_gather(w_gate_up[layer_index], 'fsdp', axis=0, tiled=True)  86.3 us
    reduce_scatter x2, waiting for transfers between devices, collect_grad(): lax.psum_scatter(term_fn(jnp.int32(0), lax.axis_size('tensor') * local_ro...  80.4 us
    all_gather x1, waiting for transfers between devices, per_device(): lax.all_gather(w_down[layer_index], 'fsdp', axis=1, tiled=True)  56.3 us
    reduce_scatter x1, waiting for transfers between devices, per_device(): lax.psum_scatter(local_set[4].astype(jnp.bfloat16), 'fsdp', scatter_dimen...  46.8 us
  transfers between devices with their start and end apart: 19, of which 18 were waited for; matrix products, arithmetic and copies ran while one was open for 16% of the time, Pallas kernels for 0%

profile of v1, /device:TPU:0, one launch (start us, length us, event | category | flops | bytes accessed | tf_op | source)
XLA Modules:
  0.0 1383.2 jit_solution(8392175093084249237)
XLA Ops:
  8.9 10.6 all-gather
  27.7 8.9 all-gather.24.cloned.1.call-done
  38.1 81.4 %all-gather.16.cloned.1.call-done = bf16[1024,2048]{1,0:T(8,128)(2,1)} async-done(((bf16[256,2048]{1,0:T(8,128)(2,1)}), bf16[1024,2048]{1,0:T(8,128)(2,1)}) %all-gather.16.cloned.1.call-update) | async-done | bytes 4194320 | tf_op jit(solution)/shard_map/all_gather | solution.py:139
  119.5 3.5 fusion.97
  123.1 24.6 %all-gather.26.cloned.1.call-done = bf16[1,2048,512]{2,1,0:T(8,128)(2,1)} async-done(((bf16[1,256,512]{2,1,0:T(8,128)(2,1)}), bf16[1,2048,512]{2,1,0:T(8,128)(2,1)}) %all-gather.26.cloned.1.call-update) | async-done | bytes 2097168 | tf_op jit(solution)/shard_map/all_gather | solution.py:163
  147.7 5.2 fusion.59
  153.3 7.9 fusion.8
  161.3 9.2 exponential_reduce_fusion
  176.3 6.3 convolution_convert_fusion.6
  182.7 4.2 convolution_convert_fusion.5
  188.1 6.0 convolution_convert_fusion.2
  198.0 73.2 %reduce-scatter.13.cloned.1.call-done = bf16[256,2048]{1,0:T(8,128)(2,1)} async-done(((bf16[1024,2048]{1,0:T(8,128)(2,1)}), bf16[256,2048]{1,0:T(8,128)(2,1)}) %reduce-scatter.13.cloned.1.call-update) | async-done | bytes 1048592 | tf_op jit(solution)/shard_map/reduce_scatter | solution.py:142
  277.5 86.3 %all-gather.30.cloned.1.call-done = bf16[1,2048,2,2048]{3,1,2,0:T(8,128)(2,1)} async-done(((bf16[1,256,2,2048]{3,1,2,0:T(8,128)(2,1)}), bf16[1,2048,2,2048]{3,1,2,0:T(8,128)(2,1)}) %all-gather.30.cloned.1.call-update) | async-done | bytes 16777232 | tf_op jit(solution)/shard_map/all_gather | solution.py:166
  363.8 22.6 %copy.56 = bf16[1,2048,2,2048]{1,3,2,0:T(8,128)(2,1)} copy(bf16[1,2048,2,2048]{3,1,2,0:T(8,128)(2,1)} %all-gather.30.cloned.1.call-done) | data formatting | bytes 33554432 | tf_op jit(solution)/shard_map/all_gather | solution.py:166
  386.4 60.3 %all-gather.18.cloned.1.call-done = bf16[1024,2048]{1,0:T(8,128)(2,1)} async-done(((bf16[256,2048]{1,0:T(8,128)(2,1)}), bf16[1024,2048]{1,0:T(8,128)(2,1)}) %all-gather.18.cloned.1.call-update) | async-done | bytes 4194320 | tf_op jit(solution)/shard_map/all_gather | solution.py:139
  446.7 23.7 %fusion = f32[1024,2,2048]{2,0,1:T(8,128)} fusion(bf16[1,2048,2,2048]{1,3,2,0:T(8,128)(2,1)} %copy.56, bf16[1024,2048]{1,0:T(8,128)(2,1)} %all-gather.18.cloned.1.call-done), kind=kOutput, calls=%fused_computation.1 | convolution fusion | flops 17179869184 | bytes 37748736 | tf_op jit(solution)/shard_map/dot_general | solution.py:204
  470.4 57.7 %all-gather.20.cloned.1.call-done = bf16[1024,2048]{1,0:T(8,128)(2,1)} async-done(((bf16[256,2048]{1,0:T(8,128)(2,1)}), bf16[1024,2048]{1,0:T(8,128)(2,1)}) %all-gather.20.cloned.1.call-update) | async-done | bytes 4194320 | tf_op jit(solution)/shard_map/all_gather | solution.py:150
  528.1 56.3 %all-gather.32.cloned.1.call-done = bf16[1,2048,2048]{2,1,0:T(8,128)(2,1)} async-done(((bf16[1,2048,256]{2,1,0:T(8,128)(2,1)}), bf16[1,2048,2048]{2,1,0:T(8,128)(2,1)}) %all-gather.32.cloned.1.call-update) | async-done | bytes 8388624 | tf_op jit(solution)/shard_map/all_gather | solution.py:167
  584.4 20.5 %multiply_bitcast_fusion.1 = (bf16[1024,1,2048]{2,0,1:T(8,128)(2,1)}, bf16[1024,1,2048]{2,0,1:T(8,128)(2,1)}) fusion(f32[1024,2,2048]{2,0,1:T(8,128)} %fusion, bf16[1024,2048]{1,0:T(8,128)(2,1)} %all-gather.20.cloned.1.call-done, bf16[1,2048,2048]{2,1,0:T(8,128)(2,1)} %all-gather.32.cloned.1.call-done), kind=kOutput, calls=%fused_computation.31 | convolution fusion | flops 8617197568 | bytes 37748736 | tf_op jit(solution)/shard_map/dot_general | solution.py:260
  604.9 24.0 %bitcast_convert_fusion = bf16[1024,2048]{1,0:T(8,128)(2,1)} fusion(bf16[1,2048,2,2048]{3,1,2,0:T(8,128)(2,1)} %all-gather.30.cloned.1.call-done, bf16[1024,1,2048]{2,0,1:T(8,128)(2,1)} %get-tuple-element.41, bf16[1024,1,2048]{2,0,1:T(8,128)(2,1)} %get-tuple-element.40), kind=kOutput, calls=%fused_computation.24 | convolution fusion | flops 17186160640 | bytes 29360128 | tf_op jit(solution)/shard_map/dot_general | solution.py:274
  629.0 76.9 %reduce-scatter.17.cloned.1.call-done = bf16[256,2048]{1,0:T(8,128)(2,1)} async-done(((bf16[1024,2048]{1,0:T(8,128)(2,1)}), bf16[256,2048]{1,0:T(8,128)(2,1)}) %reduce-scatter.17.cloned.1.call-update) | async-done | bytes 1048592 | tf_op jit(solution)/shard_map/reduce_scatter | solution.py:153
  711.3 81.3 %all-gather.22.cloned.1.call-done = bf16[1024,2048]{1,0:T(8,128)(2,1)} async-done(((bf16[256,2048]{1,0:T(8,128)(2,1)}), bf16[1024,2048]{1,0:T(8,128)(2,1)}) %all-gather.22.cloned.1.call-update) | async-done | bytes 4194320 | tf_op jit(solution)/shard_map/all_gather | solution.py:150
  792.7 5.2 fusion.62
  799.7 6.3 convolution_bitcast_fusion.4
  806.0 5.7 fusion.13
  815.7 9.3 fusion.4
  825.0 6.2 convolution_bitcast_fusion.1
  834.6 6.4 fusion.66
  850.8 8.0 multiply_convert_fusion
  860.9 11.5 convolution_convert_fusion.1
  872.4 4.6 fusion.32
  877.3 5.8 convolution_convert_fusion.3
  883.2 6.0 convolution_convert_fusion.4
  889.3 13.9 %fusion.29 = bf16[1024,2048]{1,0:T(8,128)(2,1)} fusion(bf16[1024,2048]{1,0:T(8,128)(2,1)} %copy-done.14, bf16[1,2048,2048]{2,1,0:T(8,128)(2,1)} %all-gather.32.cloned.1.call-done), kind=kOutput, calls=%fused_computation.51 | convolution fusion | flops 8592031744 | bytes 16777216 | tf_op jit(solution)/shard_map/dot_general | solution.py:212
  903.3 7.5 maximum_convert_fusion
  910.8 11.9 copy.65
  922.7 3.5 reduce-scatter.19.cloned.1.call-done
  930.0 24.7 %convolution_convert_fusion = bf16[2048,2,2048]{2,0,1:T(8,128)(2,1)} fusion(bf16[1024,2,2048]{0,2,1:T(8,128)(2,1)} %copy.65, bf16[1024,2048]{1,0:T(8,128)(2,1)} %all-gather.18.cloned.1.call-done), kind=kOutput, calls=%fused_computation.14 | convolution fusion | flops 17188257792 | bytes 29360128 | tf_op jit(solution)/shard_map/dot_general | solution.py:269
  954.7 46.8 %reduce-scatter.29.cloned.1.call-done = bf16[2048,256]{1,0:T(8,128)(2,1)} async-done(((bf16[2048,2048]{1,0:T(8,128)(2,1)}), bf16[2048,256]{1,0:T(8,128)(2,1)}) %reduce-scatter.29.cloned.1.call-update) | async-done | bytes 1048592 | tf_op jit(solution)/shard_map/reduce_scatter | solution.py:343
  1004.2 36.3 %reduce-scatter.23.cloned.1.call-done = bf16[256,2,128]{2,0,1:T(8,128)(2,1)} async-done(((bf16[2048,2,128]{2,0,1:T(8,128)(2,1)}), bf16[256,2,128]{2,0,1:T(8,128)(2,1)}) %reduce-scatter.23.cloned.1.call-update) | async-done | bytes 131088 | tf_op jit(solution)/shard_map/reduce_scatter | solution.py:340
  1042.3 43.0 %reduce-scatter.25.cloned.1.call-done = bf16[512,256]{1,0:T(8,128)(2,1)} async-done(((bf16[512,2048]{1,0:T(8,128)(2,1)}), bf16[512,256]{1,0:T(8,128)(2,1)}) %reduce-scatter.25.cloned.1.call-update) | async-done | bytes 262160 | tf_op jit(solution)/shard_map/reduce_scatter | solution.py:341
  1087.2 43.1 %reduce-scatter.21.cloned.1.call-done = bf16[256,512]{1,0:T(8,128)(2,1)} async-done(((bf16[2048,512]{1,0:T(8,128)(2,1)}), bf16[256,512]{1,0:T(8,128)(2,1)}) %reduce-scatter.21.cloned.1.call-update) | async-done | bytes 262160 | tf_op jit(solution)/shard_map/reduce_scatter | solution.py:339
  1132.1 77.2 %reduce-scatter.15.cloned.1.call-done = bf16[256,2048]{1,0:T(8,128)(2,1)} async-done(((bf16[1024,2048]{1,0:T(8,128)(2,1)}), bf16[256,2048]{1,0:T(8,128)(2,1)}) %reduce-scatter.15.cloned.1.call-update) | async-done | bytes 1048592 | tf_op jit(solution)/shard_map/reduce_scatter | solution.py:142
  1209.2 6.0 fusion.44
  1215.2 34.2 %reduce-scatter.31.cloned.1.call-done = f32[256,2]{1,0:T(8,128)} async-done(((f32[2048,2]{1,0:T(8,128)}), f32[256,2]{1,0:T(8,128)}) %reduce-scatter.31.cloned.1.call-update) | async-done | bytes 2064
  1250.4 12.4 psum.8
  1262.8 106.4 %reduce-scatter.27.cloned.1.call-done = bf16[256,2,2048]{2,0,1:T(8,128)(2,1)} async-done(((bf16[2048,2,2048]{2,0,1:T(8,128)(2,1)}), bf16[256,2,2048]{2,0,1:T(8,128)(2,1)}) %reduce-scatter.27.cloned.1.call-update) | async-done | bytes 2097168 | tf_op jit(solution)/shard_map/reduce_scatter | solution.py:342
  1371.3 5.3 copy.68
  (212 shorter events, 70.3 us)
Async XLA Ops:
  7.2 17.8 %copy-start.36 = (s32[1,1024]{1,0:T(1,128)S(1)}, s32[1,1024]{1,0:T(1,128)}, u32[]{:S(2)}) copy-start(s32[1,1024]{1,0:T(1,128)} %param.11) | copy-start | bytes 12292
  7.2 29.4 %all-gather.24.cloned.1.call-start = ((), (), s32[]{:S(2)}) async-start(), calls=%async_computation.23 | async-start | bytes 1179648 | tf_op jit(solution)/shard_map/all_gather | solution.py:164
  8.8 110.7 %all-gather.16.cloned.1.call-start = ((), (), s32[]{:S(2)}) async-start(), calls=%async_computation.10 | async-start | bytes 5242880 | tf_op jit(solution)/shard_map/all_gather | solution.py:139
  21.0 687.0 %copy-start.32 = (f32[1,1,2048]{2,1,0:T(1,128)}, f32[1,1,2048]{2,1,0:T(1,128)S(1)}, u32[]{:S(2)}) copy-start(f32[1,1,2048]{2,1,0:T(1,128)S(1)} %get-tuple-element.54) | copy-start | bytes 24580
  23.6 124.1 %all-gather.26.cloned.1.call-start = ((), (), s32[]{:S(2)}) async-start(), calls=%async_computation.24 | async-start | bytes 2359296 | tf_op jit(solution)/shard_map/all_gather | solution.py:163
  24.3 162.9 %all-gather.28.cloned.1.call-start = ((), (), s32[]{:S(2)}) async-start(), calls=%async_computation.25 | async-start | bytes 2359296 | tf_op jit(solution)/shard_map/all_gather | solution.py:165
  24.9 246.3 %reduce-scatter.13.cloned.1.call-start = ((), (), s32[]{:S(2)}) async-start(), calls=%async_computation.11 | async-start | bytes 5242880 | tf_op jit(solution)/shard_map/reduce_scatter | solution.py:142
  26.9 126.0 %copy-start.16 = (f32[1024,32]{0,1:T(8,128)}, f32[1024,32]{0,1:T(8,128)S(1)}, u32[]{:S(2)}) copy-start(f32[1024,32]{0,1:T(8,128)S(1)} %get-tuple-element.58) | copy-start | bytes 393220
  27.2 149.1 %copy-start.26 = (pred[512,512]{0,1:T(8,128)(4,1)}, pred[512,512]{0,1:T(8,128)(4,1)S(1)}, u32[]{:S(2)}) copy-start(pred[512,512]{0,1:T(8,128)(4,1)S(1)} %compare_and_fusion) | copy-start | bytes 786436
  27.7 155.0 %copy-start.12 = (pred[512,1024]{0,1:T(8,128)(4,1)}, pred[512,1024]{0,1:T(8,128)(4,1)S(1)}, u32[]{:S(2)}) copy-start(pred[512,1024]{0,1:T(8,128)(4,1)S(1)} %fusion.61) | copy-start | bytes 1572868
  123.0 59.7 %copy-start.48 = (bf16[1024,2,128]{0,2,1:T(8,128)(2,1)}, bf16[1024,2,128]{0,2,1:T(8,128)(2,1)S(1)}, u32[]{:S(2)}) copy-start(bf16[1024,2,128]{0,2,1:T(8,128)(2,1)S(1)} %get-tuple-element.61) | copy-start | bytes 1572868
  123.1 47.4 %copy-start.17 = (bf16[1024,2,32]{0,2,1:T(8,128)(2,1)}, bf16[1024,2,32]{0,2,1:T(8,128)(2,1)S(1)}, u32[]{:S(2)}) copy-start(bf16[1024,2,32]{0,2,1:T(8,128)(2,1)S(1)} %get-tuple-element.48) | copy-start | bytes 393220
  123.1 47.4 %copy-start.19 = (bf16[1024,2,32]{0,2,1:T(8,128)(2,1)}, bf16[1024,2,32]{0,2,1:T(8,128)(2,1)S(1)}, u32[]{:S(2)}) copy-start(bf16[1024,2,32]{0,2,1:T(8,128)(2,1)S(1)} %get-tuple-element.49) | copy-start | bytes 393220
  153.3 17.2 %copy-start.8 = (bf16[1024,2,4,32]{0,3,2,1:T(8,128)(2,1)}, bf16[1024,2,4,32]{0,3,2,1:T(8,128)(2,1)S(1)}, u32[]{:S(2)}) copy-start(bf16[1024,2,4,32]{0,3,2,1:T(8,128)(2,1)S(1)} %get-tuple-element.44) | copy-start | bytes 1572868
  153.3 17.2 %copy-start.10 = (bf16[1024,2,4,32]{0,3,2,1:T(8,128)(2,1)}, bf16[1024,2,4,32]{0,3,2,1:T(8,128)(2,1)S(1)}, u32[]{:S(2)}) copy-start(bf16[1024,2,4,32]{0,3,2,1:T(8,128)(2,1)S(1)} %get-tuple-element.45) | copy-start | bytes 1572868
  170.5 12.2 copy-start.39
  194.1 77.1 %copy-start = (bf16[256,2048]{1,0:T(8,128)(2,1)S(1)}, bf16[256,2048]{1,0:T(8,128)(2,1)}, u32[]{:S(2)}) copy-start(bf16[256,2048]{1,0:T(8,128)(2,1)} %param.10) | copy-start | bytes 3145732
  194.2 169.7 %all-gather.30.cloned.1.call-start = ((), (), s32[]{:S(2)}) async-start(), calls=%async_computation.26 | async-start | bytes 18874368 | tf_op jit(solution)/shard_map/all_gather | solution.py:166
  197.9 77.6 %copy-start.4 = (f32[256,2048]{1,0:T(8,128)S(1)}, f32[256,2048]{1,0:T(8,128)}, u32[]{:S(2)}) copy-start(f32[256,2048]{1,0:T(8,128)} %param.18) | copy-start | bytes 6291460
  197.9 248.8 %all-gather.18.cloned.1.call-start = ((), (), s32[]{:S(2)}) async-start(), calls=%async_computation.12 | async-start | bytes 5242880 | tf_op jit(solution)/shard_map/all_gather | solution.py:139
  272.9 435.1 %copy-start.37 = (f32[256]{0:T(256)}, f32[256]{0:T(256)S(1)}, u32[]{:S(2)}) copy-start(f32[256]{0:T(256)S(1)} %add_rsqrt_fusion) | copy-start | bytes 3076
  275.5 252.6 %all-gather.20.cloned.1.call-start = ((), (), s32[]{:S(2)}) async-start(), calls=%async_computation.14 | async-start | bytes 5242880 | tf_op jit(solution)/shard_map/all_gather | solution.py:150
  276.7 307.7 %all-gather.32.cloned.1.call-start = ((), (), s32[]{:S(2)}) async-start(), calls=%async_computation.27 | async-start | bytes 9437184 | tf_op jit(solution)/shard_map/all_gather | solution.py:167
  277.4 428.4 %reduce-scatter.17.cloned.1.call-start = ((), (), s32[]{:S(2)}) async-start(), calls=%async_computation.15 | async-start | bytes 5242880 | tf_op jit(solution)/shard_map/reduce_scatter | solution.py:153
  628.9 77.0 %copy-start.2 = (bf16[256,2048]{1,0:T(8,128)(2,1)S(1)}, bf16[256,2048]{1,0:T(8,128)(2,1)}, u32[]{:S(2)}) copy-start(bf16[256,2048]{1,0:T(8,128)(2,1)} %reduce-scatter.13.cloned.1.call-done) | copy-start | bytes 3145732
  628.9 163.7 %all-gather.22.cloned.1.call-start = ((), (), s32[]{:S(2)}) async-start(), calls=%async_computation.16 | async-start | bytes 5242880 | tf_op jit(solution)/shard_map/all_gather | solution.py:150
  708.0 89.9 %copy-start.44 = (f32[256]{0:T(256)}, f32[256]{0:T(256)S(1)}, u32[]{:S(2)}) copy-start(f32[256]{0:T(256)S(1)} %broadcast_multiply_fusion.2) | copy-start | bytes 3076
  711.2 86.7 %copy-start.23 = (bf16[2,64,4,512]{3,1,2,0:T(8,128)(2,1)S(1)}, bf16[2,64,4,512]{3,1,2,0:T(8,128)(2,1)}, u32[]{:S(2)}) copy-start(bf16[2,64,4,512]{3,1,2,0:T(8,128)(2,1)} %copy-done.22) | copy-start | bytes 1572868
  711.3 86.7 %copy-start.25 = (bf16[2,64,4,512]{3,1,2,0:T(8,128)(2,1)S(1)}, bf16[2,64,4,512]{3,1,2,0:T(8,128)(2,1)}, u32[]{:S(2)}) copy-start(bf16[2,64,4,512]{3,1,2,0:T(8,128)(2,1)} %copy-done.24) | copy-start | bytes 1572868
  711.3 88.4 %copy-start.27 = (pred[512,512]{0,1:T(8,128)(4,1)S(1)}, pred[512,512]{0,1:T(8,128)(4,1)}, u32[]{:S(2)}) copy-start(pred[512,512]{0,1:T(8,128)(4,1)} %copy-done.26) | copy-start | bytes 786436
  711.3 88.4 %copy-start.41 = (f32[1,8,512]{2,1,0:T(8,128)S(1)}, f32[1,8,512]{2,1,0:T(8,128)}, u32[]{:S(2)}) copy-start(f32[1,8,512]{2,1,0:T(8,128)} %copy-done.40) | copy-start | bytes 49156
  711.3 214.9 %reduce-scatter.19.cloned.1.call-start = ((), (), s32[]{:S(2)}) async-start(), calls=%async_computation.17 | async-start | bytes 5242880 | tf_op jit(solution)/shard_map/reduce_scatter | solution.py:153
  799.7 16.0 %slice-start.4 = ((s8[16777216]{0:T(1024)(128)(4,1)}), s8[4194304]{0:T(1024)(128)(4,1)S(1)}, s32[]{:S(2)}) async-start(s8[16777216]{0:T(1024)(128)(4,1)} %bitcast.277), calls=%async_computation.33 | async-start | bytes 8388608
  799.7 16.0 %slice-start.5 = ((s8[16777216]{0:T(1024)(128)(4,1)}), s8[4194304]{0:T(1024)(128)(4,1)S(1)}, s32[]{:S(2)}) async-start(s8[16777216]{0:T(1024)(128)(4,1)} %bitcast.277), calls=%async_computation.34 | async-start | bytes 8388608
  850.8 150.7 %reduce-scatter.29.cloned.1.call-start = ((), (), s32[]{:S(2)}) async-start(), calls=%async_computation.22 | async-start | bytes 9437184 | tf_op jit(solution)/shard_map/reduce_scatter | solution.py:343
  872.4 168.2 %reduce-scatter.23.cloned.1.call-start = ((), (), s32[]{:S(2)}) async-start(), calls=%async_computation.19 | async-start | bytes 1179648 | tf_op jit(solution)/shard_map/reduce_scatter | solution.py:340
  877.0 208.3 %reduce-scatter.25.cloned.1.call-start = ((), (), s32[]{:S(2)}) async-start(), calls=%async_computation.20 | async-start | bytes 2359296 | tf_op jit(solution)/shard_map/reduce_scatter | solution.py:341
  883.2 247.1 %reduce-scatter.21.cloned.1.call-start = ((), (), s32[]{:S(2)}) async-start(), calls=%async_computation.18 | async-start | bytes 2359296 | tf_op jit(solution)/shard_map/reduce_scatter | solution.py:339
  889.3 320.0 %reduce-scatter.15.cloned.1.call-start = ((), (), s32[]{:S(2)}) async-start(), calls=%async_computation.13 | async-start | bytes 5242880 | tf_op jit(solution)/shard_map/reduce_scatter | solution.py:142
  903.2 346.1 %reduce-scatter.31.cloned.1.call-start = ((), (), s32[]{:S(2)}) async-start(), calls=%async_computation.28 | async-start | bytes 1179648
  910.8 15.4 %copy-start.35 = (f32[1,1,2048]{2,1,0:T(1,128)S(1)}, f32[1,1,2048]{2,1,0:T(1,128)}, u32[]{:S(2)}) copy-start(f32[1,1,2048]{2,1,0:T(1,128)} %copy-done.34) | copy-start | bytes 24580
  910.8 15.4 %copy-start.43 = (f32[256]{0:T(256)S(1)}, f32[256]{0:T(256)}, u32[]{:S(2)}) copy-start(f32[256]{0:T(256)} %copy-done.42) | copy-start | bytes 3076
  929.5 439.7 %reduce-scatter.27.cloned.1.call-start = ((), (), s32[]{:S(2)}) async-start(), calls=%async_computation.21 | async-start | bytes 18874368 | tf_op jit(solution)/shard_map/reduce_scatter | solution.py:342
  954.7 254.5 %copy-start.3 = (bf16[256,2048]{1,0:T(8,128)(2,1)S(1)}, bf16[256,2048]{1,0:T(8,128)(2,1)}, u32[]{:S(2)}) copy-start(bf16[256,2048]{1,0:T(8,128)(2,1)} %reduce-scatter.13.cloned.1.call-done) | copy-start | bytes 3145732
  954.7 254.5 %copy-start.6 = (bf16[256,2048]{1,0:T(8,128)(2,1)S(1)}, bf16[256,2048]{1,0:T(8,128)(2,1)}, u32[]{:S(2)}) copy-start(bf16[256,2048]{1,0:T(8,128)(2,1)} %reduce-scatter.17.cloned.1.call-done) | copy-start | bytes 3145732
  954.7 254.5 %copy-start.33 = (f32[1,1,2048]{2,1,0:T(1,128)S(1)}, f32[1,1,2048]{2,1,0:T(1,128)}, u32[]{:S(2)}) copy-start(f32[1,1,2048]{2,1,0:T(1,128)} %copy-done.32) | copy-start | bytes 24580
  954.7 254.5 %copy-start.38 = (f32[256]{0:T(256)S(1)}, f32[256]{0:T(256)}, u32[]{:S(2)}) copy-start(f32[256]{0:T(256)} %copy-done.37) | copy-start | bytes 3076
  954.7 254.5 %copy-start.45 = (f32[256]{0:T(256)S(1)}, f32[256]{0:T(256)}, u32[]{:S(2)}) copy-start(f32[256]{0:T(256)} %copy-done.44) | copy-start | bytes 3076
  (28 other events, 153.1 us)
Sparse Core Ops, SparseCore 0:
  10.5 26.0 all-gather.23
  38.7 80.7 all-gather.15
  121.4 26.2 all-gather.25
  149.4 28.0 all-gather.27
  194.3 76.8 reduce-scatter.12
  273.5 90.2 all-gather.29
  365.9 80.7 all-gather.17
  448.9 79.2 all-gather.19
  530.0 54.3 all-gather.31
  629.1 76.7 reduce-scatter.16
  711.4 81.2 all-gather.21
  850.9 75.2 reduce-scatter.18
  929.7 71.7 reduce-scatter.28
  1004.5 35.9 reduce-scatter.22
  1044.2 41.1 reduce-scatter.24
  1089.1 41.1 reduce-scatter.20
  1132.4 76.7 reduce-scatter.14
  1212.8 36.5 reduce-scatter.30
  1252.9 116.1 reduce-scatter.26

commit v2 on v1

v2 whole, which is shorter than its diff:
```python
import jax
import jax.numpy as jnp
from jax import lax
from jax.sharding import PartitionSpec as P


MAXLEN = 512


NORM_EPSILON = 1e-05
ROPE_BASE = 500000.0


def norm_apply(residual, gain):
    inverse = lax.rsqrt(jnp.mean(residual * residual, axis=-1, keepdims=True) + NORM_EPSILON)
    return (inverse, (residual * inverse * gain.astype(jnp.float32)).astype(jnp.bfloat16))


def norm_back(residual, inverse, gain, grad_normed):
    scaled = grad_normed * gain.astype(jnp.float32)
    grad_gain = jnp.sum(grad_normed * residual * inverse, axis=0)
    grad_residual = inverse * scaled - residual * inverse * inverse * inverse * jnp.mean(
        scaled * residual, axis=-1, keepdims=True
    )
    return (grad_residual, grad_gain)


def rope_tables(doc_row, head_size):
    places = jnp.arange(doc_row.shape[0], dtype=jnp.int32)
    doc_start = jnp.concatenate([jnp.array([True]), doc_row[1:] != doc_row[:-1]])
    starts = lax.cummax(jnp.where(doc_start, places, 0), axis=0)
    exponent = jnp.arange(head_size // 2, dtype=jnp.float32) * (-2.0 / head_size)
    angles = (places - starts).astype(jnp.float32)[:, None] * jnp.power(ROPE_BASE, exponent)[
        None, :
    ]
    return (jnp.cos(angles), jnp.sin(angles))


def rotate(vectors, cosine, sine_table, direction_sign):
    half_size = vectors.shape[-1] // 2
    table_shape = (vectors.shape[0],) + (1,) * (vectors.ndim - 2) + (half_size,)
    cos_part = cosine.reshape(table_shape)
    sin_part = direction_sign * sine_table.reshape(table_shape)
    first_half = vectors[..., :half_size]
    second = vectors[..., half_size:]
    return jnp.concatenate(
        [first_half * cos_part - second * sin_part, second * cos_part + first_half * sin_part],
        axis=-1,
    )


def block_mask(doc_row, block_start, block_rows, key_low, key_high):
    places = jnp.arange(doc_row.shape[0], dtype=jnp.int32)
    own_docs = doc_row[block_start : block_start + block_rows]
    own_places = places[block_start : block_start + block_rows]
    return (own_docs[:, None] == doc_row[None, key_low:key_high]) & (
        places[None, key_low:key_high] <= own_places[:, None]
    )


def attend_block(query_rows, key_rows, value_rows, allowed, score_scale):
    scores = (
        jnp.einsum("qkgd,skd->kgqs", query_rows, key_rows, preferred_element_type=jnp.float32)
        * score_scale
    )
    scores = jnp.where(allowed[None, None], scores, -jnp.inf)
    row_max = jnp.max(scores, axis=-1, keepdims=True)
    log_total = row_max + jnp.log(jnp.sum(jnp.exp(scores - row_max), axis=-1, keepdims=True))
    probabilities = jnp.exp(scores - log_total).astype(jnp.bfloat16)
    attn_out = jnp.einsum(
        "kgqs,skd->qkgd", probabilities, value_rows, preferred_element_type=jnp.float32
    )
    return (attn_out.astype(jnp.bfloat16), log_total)


def attend_back(
    query_rows, key_rows, value_rows, allowed, log_total, out_rows, grad_out, score_scale
):
    scores = (
        jnp.einsum("qkgd,skd->kgqs", query_rows, key_rows, preferred_element_type=jnp.float32)
        * score_scale
    )
    scores = jnp.where(allowed[None, None], scores, -jnp.inf)
    probabilities = jnp.exp(scores - log_total)
    row_delta = jnp.einsum("qkgd,qkgd->kgq", grad_out, out_rows, preferred_element_type=jnp.float32)
    grad_probs = jnp.einsum(
        "qkgd,skd->kgqs", grad_out, value_rows, preferred_element_type=jnp.float32
    )
    grad_scores = (probabilities * (grad_probs - row_delta[..., None]) * score_scale).astype(
        jnp.bfloat16
    )
    grad_query = jnp.einsum(
        "kgqs,skd->qkgd", grad_scores, key_rows, preferred_element_type=jnp.float32
    )
    grad_key = jnp.einsum(
        "kgqs,qkgd->skd", grad_scores, query_rows, preferred_element_type=jnp.float32
    )
    grad_value = jnp.einsum(
        "kgqs,qkgd->skd",
        probabilities.astype(jnp.bfloat16),
        grad_out,
        preferred_element_type=jnp.float32,
    )
    return (grad_query, grad_key, grad_value)


def per_device(
    block_input,
    doc_ids,
    w_query,
    w_keyval,
    w_attn_out,
    w_gate_up,
    w_down,
    norm_gains,
    out_cotangent,
):
    f32, bf16 = jnp.float32, jnp.bfloat16
    ring = lax.axis_size("tensor")
    place = lax.axis_index("tensor")
    ring_pairs = [(i, (i + 1) % ring) for i in range(ring)]
    doc_row = doc_ids[0]
    row_count = doc_row.shape[0]
    local_rows, _ = block_input.shape
    kv_local = w_keyval.shape[2]
    head_size = w_keyval.shape[3] // 2
    query_width = w_query.shape[2]
    group_size = query_width // (kv_local * head_size)
    block_rows = min(512, row_count)
    score_scale = head_size ** (-0.5)

    def dot(a, b):
        return jnp.dot(a, b, preferred_element_type=f32)

    def dot_nt(a, b):
        return lax.dot_general(a, b, (((1,), (1,)), ((), ())), preferred_element_type=f32)

    def dot_tn(a, b):
        return lax.dot_general(a, b, (((0,), (0,)), ((), ())), preferred_element_type=f32)

    def shift(rows):
        return lax.ppermute(rows, "tensor", ring_pairs)

    def after(value, gate):
        return lax.optimization_barrier((value, gate))[0]

    def block_start_of(step):
        return lax.rem(place - step + ring, ring) * local_rows

    def spread(rows):
        blocks = [rows]
        for _ in range(ring - 1):
            blocks.append(shift(blocks[-1]))
        return blocks

    def in_order(blocks):
        whole = jnp.zeros((ring * local_rows,) + blocks[0].shape[1:], blocks[0].dtype)
        for step, block in enumerate(blocks):
            whole = lax.dynamic_update_slice_in_dim(whole, block, block_start_of(step), 0)
        return whole

    def rows_of(whole, step):
        return lax.dynamic_slice_in_dim(whole, block_start_of(step), local_rows, 0)

    def scatter_sum(grad):
        return lax.psum_scatter(grad, "fsdp", scatter_dimension=0, tiled=True).astype(f32)

    def collect(parts, last_gate=None):
        total = parts[1 % ring].astype(f32)
        for step in range(2, ring + 1):
            if step == ring and last_gate is not None:
                total = after(total, last_gate)
            total = shift(total.astype(bf16)).astype(f32) + parts[step % ring]
        return total

    w_qkv_local = jnp.concatenate(
        [w_query[0], w_keyval[0].reshape(w_keyval.shape[1], -1)], axis=1
    )
    w_qkv = lax.all_gather(w_qkv_local, "fsdp", axis=0, tiled=True)
    gains_all = lax.all_gather(norm_gains[0], "fsdp", axis=1, tiled=True)
    w_out_all = lax.all_gather(w_attn_out[0], "fsdp", axis=1, tiled=True)
    w_gu_all = lax.all_gather(
        jnp.swapaxes(w_gate_up[0], 0, 1), "fsdp", axis=1, tiled=True
    )
    w_down_all = lax.all_gather(w_down[0], "fsdp", axis=1, tiled=True)
    w_gate, w_up = w_gu_all[0], w_gu_all[1]

    cosine, sine_table = rope_tables(doc_row, head_size)
    block_starts = list(range(0, row_count, block_rows))
    windows = [
        (max(0, start - MAXLEN), start + block_rows) for start in block_starts
    ]
    mask_list = [
        block_mask(doc_row, start, block_rows, windows[index][0], windows[index][1])
        for index, start in enumerate(block_starts)
    ]

    input_blocks = spread(block_input)
    grad_blocks = spread(after(out_cotangent.astype(bf16), input_blocks[-1]))
    normed_pairs = [norm_apply(block.astype(f32), gains_all[0]) for block in input_blocks]
    residual = block_input.astype(f32)
    inv_attn = normed_pairs[0][0]
    normed_all = in_order([pair[1] for pair in normed_pairs])
    qkv = dot(normed_all, w_qkv)
    query_rows = rotate(
        qkv[:, :query_width].reshape(row_count, kv_local, group_size, head_size),
        cosine, sine_table, 1.0,
    ).astype(bf16)
    keyval = qkv[:, query_width:].reshape(row_count, kv_local, 2 * head_size)
    key_rows = rotate(keyval[..., :head_size], cosine, sine_table, 1.0).astype(bf16)
    value_rows = keyval[..., head_size:].astype(bf16)
    out_list = []
    total_list = []
    for block_index, block_start in enumerate(block_starts):
        key_low, key_high = windows[block_index]
        attend_inputs = (
            query_rows[block_start : block_start + block_rows],
            key_rows[key_low:key_high],
            value_rows[key_low:key_high],
        )
        if block_index == len(block_starts) - 1:
            attend_inputs = after(attend_inputs, grad_blocks[1 % ring])
        out_block, log_total = attend_block(
            *attend_inputs,
            mask_list[block_index],
            score_scale,
        )
        out_list.append(out_block)
        total_list.append(log_total)
    attended = jnp.concatenate(out_list, axis=0).reshape(row_count, -1)
    attended = after(attended, grad_blocks[2 % ring])
    middle = residual + collect(
        [dot(rows_of(attended, step), w_out_all) for step in range(ring)]
    )
    inv_mlp, normed_mlp = norm_apply(middle, gains_all[1])

    normed_mlp_blocks = [normed_mlp]
    hidden_blocks, dgate_blocks, dup_blocks, back_parts = [], [], [], []
    for step in range(ring):
        if step == 1:
            normed_mlp_blocks.append(shift(normed_mlp))
        elif step > 1:
            gate = dup_blocks[0] if step == 2 else back_parts[step - 2]
            normed_mlp_blocks.append(shift(after(normed_mlp_blocks[-1], gate)))
        rows = normed_mlp_blocks[step]
        if step == 1:
            rows = after(rows, (dgate_blocks[0], dup_blocks[0]))
        elif step > 1:
            rows = after(rows, back_parts[step - 1])
        gate = dot(rows, w_gate)
        up = dot(rows, w_up)
        grad_hidden = dot_nt(grad_blocks[step], w_down_all)
        sigmoid_gate = jax.nn.sigmoid(gate)
        silu_gate = gate * sigmoid_gate
        hidden_blocks.append((silu_gate * up).astype(bf16))
        dgate = (grad_hidden * up * sigmoid_gate * (1.0 + gate * (1.0 - sigmoid_gate))).astype(bf16)
        dup = (grad_hidden * silu_gate).astype(bf16)
        dgate_blocks.append(dgate)
        dup_blocks.append(dup)
        back_parts.append(dot_nt(dgate, w_gate) + dot_nt(dup, w_up))
    grad_normed_mlp = collect(back_parts)
    grad_down = dot_tn(in_order(grad_blocks), in_order(hidden_blocks)).astype(bf16)
    normed_mlp_all = in_order(normed_mlp_blocks)
    grad_wgate = dot_tn(normed_mlp_all, in_order(dgate_blocks)).astype(bf16)
    grad_wup = dot_tn(normed_mlp_all, in_order(dup_blocks)).astype(bf16)
    grad_normed_mlp = after(grad_normed_mlp, (grad_down, grad_wgate))
    grad_down = jnp.swapaxes(scatter_sum(grad_down), 0, 1)
    grad_wgate = scatter_sum(grad_wgate)
    norm_part, grad_gain_mlp = norm_back(middle, inv_mlp, gains_all[1], grad_normed_mlp)
    grad_middle = out_cotangent + norm_part

    middle_blocks = spread(grad_middle.astype(bf16))
    do_parts = [dot_nt(block, w_out_all).astype(bf16) for block in middle_blocks]
    grad_attended = in_order(do_parts).reshape(row_count, kv_local, group_size, head_size)
    middle_all = in_order(middle_blocks)

    grad_attended = after(grad_attended, grad_wup)
    grad_wup = scatter_sum(grad_wup)
    grad_wgu = jnp.stack([grad_wgate, grad_wup], axis=1)
    grad_wo = jnp.swapaxes(scatter_sum(dot_tn(middle_all, attended).astype(bf16)), 0, 1)

    out_parts = [dot(hidden, w_down_all) for hidden in hidden_blocks]
    out_totals = [after(out_parts[1 % ring], middle_blocks[-1]).astype(bf16)]
    for step in range(2, ring + 1):
        out_totals.append((shift(out_totals[-1]).astype(f32) + out_parts[step % ring]))
        if step < ring:
            out_totals[-1] = out_totals[-1].astype(bf16)
    output_rows = middle + out_totals[-1]

    attended_heads = attended.reshape(row_count, kv_local, group_size, head_size)
    grad_keys = jnp.zeros((row_count, kv_local, head_size), f32)
    grad_values = jnp.zeros((row_count, kv_local, head_size), f32)
    query_grads = []
    for block_index, block_start in enumerate(block_starts):
        block_stop = block_start + block_rows
        key_low, key_high = windows[block_index]
        grad_out = after(grad_attended[block_start:block_stop], out_totals[block_index])
        grad_query_block, grad_key_part, grad_value_part = attend_back(
            query_rows[block_start:block_stop],
            key_rows[key_low:key_high],
            value_rows[key_low:key_high],
            mask_list[block_index],
            total_list[block_index],
            attended_heads[block_start:block_stop],
            grad_out,
            score_scale,
        )
        query_grads.append(grad_query_block)
        pad_width = ((key_low, row_count - key_high), (0, 0), (0, 0))
        grad_keys = grad_keys + jnp.pad(grad_key_part, pad_width)
        grad_values = grad_values + jnp.pad(grad_value_part, pad_width)
    grad_query = (
        rotate(jnp.concatenate(query_grads, axis=0), cosine, sine_table, -1.0)
        .astype(bf16)
        .reshape(row_count, -1)
    )
    grad_keyval = (
        jnp.concatenate([rotate(grad_keys, cosine, sine_table, -1.0), grad_values], axis=-1)
        .astype(bf16)
        .reshape(row_count, -1)
    )
    grad_qkv = jnp.concatenate([grad_query, grad_keyval], axis=1)
    grad_qkv = after(grad_qkv, out_totals[-2])
    in_parts = [dot_nt(rows_of(grad_qkv, step), w_qkv) for step in range(ring)]
    grad_normed = collect(in_parts, output_rows)
    norm_part, _ = norm_back(residual, inv_attn, gains_all[0], grad_normed)
    grad_rows = grad_middle + norm_part

    grad_gain_attn = sum(
        jnp.sum(part * block.astype(f32) * pair[0], axis=0)
        for part, block, pair in zip(in_parts, input_blocks, normed_pairs)
    )
    grad_wqkv = dot_tn(normed_all, grad_qkv).astype(bf16)
    gain_columns = jnp.stack([grad_gain_attn, grad_gain_mlp], axis=1).astype(bf16)
    gain_columns = jnp.pad(gain_columns, ((0, 0), (0, 126)))
    packed = scatter_sum(jnp.concatenate([grad_wqkv, gain_columns], axis=1))
    qkv_width = grad_wqkv.shape[1]
    grad_wq = packed[:, :query_width]
    grad_wkv = packed[:, query_width:qkv_width].reshape(-1, kv_local, 2 * head_size)
    gain_part = packed[:, qkv_width : qkv_width + 2]
    gain_total = gain_part
    for _ in range(ring - 1):
        gain_part = shift(gain_part)
        gain_total = gain_total + gain_part
    return (
        output_rows,
        grad_rows,
        grad_wq[None],
        grad_wkv[None],
        grad_wo[None],
        grad_wgu[None],
        grad_down[None],
        gain_total.T[None],
    )


def solution(mesh):
    return jax.shard_map(
        per_device,
        mesh=mesh,
        in_specs=(
            P(("fsdp", "tensor"), None),
            P("fsdp", None),
            P(None, "fsdp", "tensor"),
            P(None, "fsdp", "tensor", None),
            P(None, "tensor", "fsdp"),
            P(None, "fsdp", None, "tensor"),
            P(None, "tensor", "fsdp"),
            P(None, None, "fsdp"),
            P(("fsdp", "tensor"), None),
        ),
        out_specs=(
            P(("fsdp", "tensor"), None),
            P(("fsdp", "tensor"), None),
            P(None, "fsdp", "tensor"),
            P(None, "fsdp", "tensor", None),
            P(None, "tensor", "fsdp"),
            P(None, "fsdp", None, "tensor"),
            P(None, "tensor", "fsdp"),
            P(None, None, "fsdp"),
        ),
        check_vma=False,
    )
```

time: 1390 us -> 1010 us (0.73)
  waiting for transfers between devices: 1000 us -> 523 us
  matrix products: 222 us -> 310 us
  starting transfers between devices: 1.4 us -> 30.8 us
  blocking collectives: 23 us -> 9.07 us
    all_gather x9 -> x4, waiting for transfers between devices: 457 us -> 0.04 us  [the longest x1 0.02 us: per_device(): w_out_all = lax.all_gather(w_attn_out[0], 'fsdp', axis=1, tiled=True)]
    ppermute x0 -> x27, waiting for transfers between devices: none -> 263 us  [shift(): return lax.ppermute(rows, 'tensor', ring_pairs)]
    reduce_scatter x9 -> x5, waiting for transfers between devices: 506 us -> 257 us  [scatter_sum(): lax.psum_scatter(grad, 'fsdp', scatter_dimension=0, tiled=True).astype(f32)]
    dot_general x15 -> x43, matrix products: 160 us -> 256 us  [the longest x20 109 us: dot_nt(): lax.dot_general(a, b, (((1,), (1,)), ((), ())), preferred_element_type=f32)]
    unnamed x20 -> x9, waiting for transfers between devices: 36.3 us -> 3.26 us
    ppermute x0 -> x27, starting transfers between devices: none -> 30.2 us  [shift(): return lax.ppermute(rows, 'tensor', ring_pairs)]
    all_gather x2 -> x0, local copies, waits for them, and re-layouts: 24.1 us -> none  [the longest x1 22.6 us: per_device(): lax.all_gather(w_gate_up[layer_index], 'fsdp', axis=0, tiled=True)]
    convert_element_type x6 -> x5, other arithmetic: 25 us -> 6.51 us  [the longest x2 4.06 us: per_device(): out_totals[-1] = out_totals[-1].astype(bf16)]
  transfers between devices with their start and end apart: 19 -> 36, of which waited for: 18 -> 22; matrix products, arithmetic and copies ran while one was open for 16% -> 38% of each run, Pallas kernels for 0% -> 0%
where the time goes in v2:
time: 1010 us; the launch traced here: 1000 us
  waiting for transfers between devices  523 us (52%)
  matrix products  310 us (31%)
  local copies, waits for them, and re-layouts  57.3 us (6%)
  other arithmetic  55.6 us (6%)
  starting transfers between devices  30.8 us (3%)
  between operations  16 us (2%)
    ppermute x27, waiting for transfers between devices, shift(): return lax.ppermute(rows, 'tensor', ring_pairs)  263 us
    reduce_scatter x5, waiting for transfers between devices, scatter_sum(): lax.psum_scatter(grad, 'fsdp', scatter_dimension=0, tiled=True).astype(f32)  257 us
    dot_general x20, matrix products, dot_nt(): lax.dot_general(a, b, (((1,), (1,)), ((), ())), preferred_element_type=f32)  109 us
    dot_general x17, matrix products, dot(): return jnp.dot(a, b, preferred_element_type=f32)  90.2 us
    dot_general x5, matrix products, dot_tn(): lax.dot_general(a, b, (((0,), (0,)), ((), ())), preferred_element_type=f32)  48.5 us
    ppermute x27, starting transfers between devices, shift(): return lax.ppermute(rows, 'tensor', ring_pairs)  30.2 us
    unnamed x197, local copies, waits for them, and re-layouts  26.7 us
  transfers between devices with their start and end apart: 36, of which 22 were waited for; matrix products, arithmetic and copies ran while one was open for 38% of the time, Pallas kernels for 0%

profile of v2, /device:TPU:0, one launch (start us, length us, event | category | flops | bytes accessed | tf_op | source)
XLA Modules:
  0.0 1002.0 jit_solution(6746093098654824694)
XLA Ops:
  20.7 9.1 all-gather
  32.6 11.3 %collective-permute-done = bf16[256,2048]{1,0:T(8,128)(2,1)} collective-permute-done((bf16[256,2048]{1,0:T(8,128)(2,1)S(1)}, bf16[256,2048]{1,0:T(8,128)(2,1)}, u32[]{:S(2)}, u32[]{:S(2)}) %collective-permute-start) | collective-permute-done | bytes 1048608 | tf_op jit(solution)/shard_map/ppermute | solution.py:142
  46.3 23.9 %collective-permute-done.1 = bf16[256,2048]{1,0:T(8,128)(2,1)S(1)} collective-permute-done((bf16[256,2048]{1,0:T(8,128)(2,1)}, bf16[256,2048]{1,0:T(8,128)(2,1)S(1)}, u32[]{:S(2)}, u32[]{:S(2)}) %collective-permute-start.1) | collective-permute-done | bytes 1048608 | tf_op jit(solution)/shard_map/ppermute | solution.py:142
  72.5 23.0 %collective-permute-done.2 = bf16[256,2048]{1,0:T(8,128)(2,1)S(1)} collective-permute-done((bf16[256,2048]{1,0:T(8,128)(2,1)S(1)}, bf16[256,2048]{1,0:T(8,128)(2,1)S(1)}, u32[]{:S(2)}, u32[]{:S(2)}) %collective-permute-start.2) | collective-permute-done | bytes 1048608 | tf_op jit(solution)/shard_map/ppermute | solution.py:142
  96.8 23.2 %collective-permute-done.3 = bf16[256,2048]{1,0:T(8,128)(2,1)} collective-permute-done((bf16[256,2048]{1,0:T(8,128)(2,1)S(1)}, bf16[256,2048]{1,0:T(8,128)(2,1)}, u32[]{:S(2)}, u32[]{:S(2)}) %collective-permute-start.3) | collective-permute-done | bytes 1048608 | tf_op jit(solution)/shard_map/ppermute | solution.py:142
  120.0 6.2 fusion.173
  130.2 7.5 fusion.5
  137.7 10.1 %exponential_reduce_fusion = f32[2,4,512]{2,1,0:T(4,128)S(1)} fusion(f32[2,1024,512,4]{2,1,3,0:T(8,128)} %get-tuple-element.125, f32[2,4,512]{2,1,0:T(4,128)S(1)} %get-tuple-element.124, pred[512,1024]{0,1:T(8,128)(4,1)S(1)} %fusion.78), kind=kLoop, calls=%fused_computation.9 | loop fusion | flops 16773120 | bytes 17334272 | tf_op jit(solution)/shard_map/reduce_sum | solution.py:68
  167.4 10.2 %collective-permute-start.5 = (bf16[256,2048]{1,0:T(8,128)(2,1)S(1)}, bf16[256,2048]{1,0:T(8,128)(2,1)S(1)}, u32[]{:S(2)}, u32[]{:S(2)}) collective-permute-start(bf16[256,2048]{1,0:T(8,128)(2,1)S(1)} %convolution_convert_fusion.5), channel_id=1, source_target_pairs={{0,1},{1,2},{2,3},{3,0},{4,5},{5,6},{6,7},{7,4},{8,9},{9,10},{10,1... | collective-permute-start | bytes 3145736 | tf_op jit(solution)/shard_map/ppermute | solution.py:142
  177.7 23.7 %collective-permute-done.5 = bf16[256,2048]{1,0:T(8,128)(2,1)S(1)} collective-permute-done((bf16[256,2048]{1,0:T(8,128)(2,1)S(1)}, bf16[256,2048]{1,0:T(8,128)(2,1)S(1)}, u32[]{:S(2)}, u32[]{:S(2)}) %collective-permute-start.5) | collective-permute-done | bytes 1048608 | tf_op jit(solution)/shard_map/ppermute | solution.py:142
  202.2 22.8 %collective-permute-done.6 = bf16[256,2048]{1,0:T(8,128)(2,1)S(1)} collective-permute-done((bf16[256,2048]{1,0:T(8,128)(2,1)S(1)}, bf16[256,2048]{1,0:T(8,128)(2,1)S(1)}, u32[]{:S(2)}, u32[]{:S(2)}) %collective-permute-start.6) | collective-permute-done | bytes 1048608 | tf_op jit(solution)/shard_map/ppermute | solution.py:142
  232.5 21.1 %collective-permute-done.7 = bf16[256,2048]{1,0:T(8,128)(2,1)S(1)} collective-permute-done((bf16[256,2048]{1,0:T(8,128)(2,1)S(1)}, bf16[256,2048]{1,0:T(8,128)(2,1)S(1)}, u32[]{:S(2)}, u32[]{:S(2)}) %collective-permute-start.7) | collective-permute-done | bytes 1048608 | tf_op jit(solution)/shard_map/ppermute | solution.py:142
  261.4 8.2 fusion.140
  269.6 6.6 collective-permute-done.12
  277.2 15.5 %collective-permute-done.8 = bf16[256,2048]{1,0:T(8,128)(2,1)S(1)} collective-permute-done((bf16[256,2048]{1,0:T(8,128)(2,1)S(1)}, bf16[256,2048]{1,0:T(8,128)(2,1)S(1)}, u32[]{:S(2)}, u32[]{:S(2)}) %collective-permute-start.8) | collective-permute-done | bytes 1048608 | tf_op jit(solution)/shard_map/ppermute | solution.py:142
  300.6 6.0 fusion.82
  307.9 7.4 constant_dynamic-update-slice_fusion.15
  319.6 7.1 fusion.89
  326.7 7.1 fusion.81
  333.7 9.3 constant_dynamic-update-slice_fusion.6
  360.7 7.2 convolution_add_fusion.3
  369.3 7.0 fusion.87
  376.3 7.0 fusion.80
  383.3 9.3 constant_dynamic-update-slice_fusion.5
  392.7 6.1 fusion.86
  398.8 7.2 add_convert_fusion.4
  410.9 7.0 fusion.85
  418.0 7.1 fusion.79
  425.1 9.2 constant_dynamic-update-slice_fusion.4
  434.3 9.0 fusion.84
  450.5 13.5 %convolution_convert_fusion.2 = bf16[2048,2048]{1,0:T(8,128)(2,1)} fusion(bf16[1024,2048]{1,0:T(8,128)(2,1)} %constant_dynamic-update-slice_fusion.24, bf16[1024,2048]{1,0:T(8,128)(2,1)S(1)} %get-tuple-element.93), kind=kOutput, calls=%fused_computation.43 | convolution fusion | flops 8594128896 | bytes 16777216 | tf_op jit(solution)/shard_map/dot_general | solution.py:139
  465.1 14.0 %convolution_convert_fusion.1 = bf16[2048,2048]{1,0:T(8,128)(2,1)} fusion(bf16[1024,2048]{1,0:T(8,128)(2,1)} %constant_dynamic-update-slice_fusion.16, bf16[1024,2048]{1,0:T(8,128)(2,1)} %copy-done.28), kind=kOutput, calls=%fused_computation.42 | convolution fusion | flops 8594128896 | bytes 16777216 | tf_op jit(solution)/shard_map/dot_general | solution.py:139
  486.2 8.0 fusion.22
  497.9 11.3 %collective-permute-done.15 = bf16[256,2048]{1,0:T(8,128)(2,1)} collective-permute-done((bf16[256,2048]{1,0:T(8,128)(2,1)S(1)}, bf16[256,2048]{1,0:T(8,128)(2,1)}, u32[]{:S(2)}, u32[]{:S(2)}) %collective-permute-start.15) | collective-permute-done | bytes 1048608 | tf_op jit(solution)/shard_map/ppermute | solution.py:142
  509.2 13.5 %convolution_convert_fusion = bf16[2048,2048]{1,0:T(8,128)(2,1)} fusion(bf16[1024,2048]{1,0:T(8,128)(2,1)} %constant_dynamic-update-slice_fusion.16, bf16[1024,2048]{1,0:T(8,128)(2,1)S(1)} %copy-done.30), kind=kOutput, calls=%fused_computation.41 | convolution fusion | flops 8594128896 | bytes 16777216 | tf_op jit(solution)/shard_map/dot_general | solution.py:139
  522.7 7.5 fusion.12
  544.3 11.6 %collective-permute-done.17 = bf16[256,2048]{1,0:T(8,128)(2,1)} collective-permute-done((bf16[256,2048]{1,0:T(8,128)(2,1)}, bf16[256,2048]{1,0:T(8,128)(2,1)}, u32[]{:S(2)}, u32[]{:S(2)}) %collective-permute-start.17) | collective-permute-done | bytes 1048608 | tf_op jit(solution)/shard_map/ppermute | solution.py:142
  567.9 10.0 collective-permute-done.18
  587.9 8.0 fusion.113
  595.9 9.4 fusion.2
  628.8 16.5 %collective-permute-done.21 = bf16[256,2048]{1,0:T(8,128)(2,1)S(1)} collective-permute-done((bf16[256,2048]{1,0:T(8,128)(2,1)S(1)}, bf16[256,2048]{1,0:T(8,128)(2,1)S(1)}, u32[]{:S(2)}, u32[]{:S(2)}) %collective-permute-start.21) | collective-permute-done | bytes 1048608 | tf_op jit(solution)/shard_map/ppermute | solution.py:142
  655.0 8.8 collective-permute-done.20
  666.9 17.1 %collective-permute-done.22 = bf16[256,2048]{1,0:T(8,128)(2,1)} collective-permute-done((bf16[256,2048]{1,0:T(8,128)(2,1)}, bf16[256,2048]{1,0:T(8,128)(2,1)}, u32[]{:S(2)}, u32[]{:S(2)}) %collective-permute-start.22) | collective-permute-done | bytes 1048608 | tf_op jit(solution)/shard_map/ppermute | solution.py:142
  690.4 11.9 %collective-permute-done.23 = bf16[256,2048]{1,0:T(8,128)(2,1)S(1)} collective-permute-done((bf16[256,2048]{1,0:T(8,128)(2,1)S(1)}, bf16[256,2048]{1,0:T(8,128)(2,1)S(1)}, u32[]{:S(2)}, u32[]{:S(2)}) %collective-permute-start.23) | collective-permute-done | bytes 1048608 | tf_op jit(solution)/shard_map/ppermute | solution.py:142
  717.9 37.2 %reduce-scatter.6.cloned.1.call-done = bf16[256,896]{0,1:T(8,128)(2,1)} async-done(((bf16[2048,896]{0,1:T(8,128)(2,1)}), bf16[256,896]{0,1:T(8,128)(2,1)}) %reduce-scatter.6.cloned.1.call-update) | async-done | bytes 458768 | tf_op jit(solution)/shard_map/reduce_scatter | solution.py:166
  757.2 72.8 %reduce-scatter.14.cloned.1.call-done = bf16[256,2048]{1,0:T(8,128)(2,1)} async-done(((bf16[2048,2048]{1,0:T(8,128)(2,1)}), bf16[256,2048]{1,0:T(8,128)(2,1)}) %reduce-scatter.14.cloned.1.call-update) | async-done | bytes 1048592 | tf_op jit(solution)/shard_map/reduce_scatter | solution.py:166
  833.0 72.0 %reduce-scatter.12.cloned.1.call-done = bf16[256,2048]{1,0:T(8,128)(2,1)} async-done(((bf16[2048,2048]{1,0:T(8,128)(2,1)}), bf16[256,2048]{1,0:T(8,128)(2,1)}) %reduce-scatter.12.cloned.1.call-update) | async-done | bytes 1048592 | tf_op jit(solution)/shard_map/reduce_scatter | solution.py:166
  905.0 75.0 %reduce-scatter.10.cloned.1.call-done = bf16[256,2048]{1,0:T(8,128)(2,1)} async-done(((bf16[2048,2048]{1,0:T(8,128)(2,1)}), bf16[256,2048]{1,0:T(8,128)(2,1)}) %reduce-scatter.10.cloned.1.call-update) | async-done | bytes 1048592 | tf_op jit(solution)/shard_map/reduce_scatter | solution.py:166
  (396 shorter events, 232.6 us)
Async XLA Ops:
  7.2 112.8 %all-gather.8.cloned.1.call-start = ((), (), s32[]{:S(2)}) async-start(), calls=%async_computation.5 | async-start | bytes 3538944 | tf_op jit(solution)/shard_map/all_gather | solution.py:179
  9.9 154.8 %all-gather.12.cloned.1.call-start = ((), (), s32[]{:S(2)}) async-start(), calls=%async_computation.12 | async-start | bytes 2359296 | tf_op jit(solution)/shard_map/all_gather | solution.py:181
  10.6 284.2 %all-gather.14.cloned.1.call-start = ((), (), s32[]{:S(2)}) async-start(), calls=%async_computation.13 | async-start | bytes 9437184 | tf_op jit(solution)/shard_map/all_gather | solution.py:185
  11.4 289.2 %all-gather.10.cloned.1.call-start = ((), (), s32[]{:S(2)}) async-start(), calls=%async_computation.6 | async-start | bytes 18874368 | tf_op jit(solution)/shard_map/all_gather | solution.py:182
  15.4 694.2 %reduce-scatter.8.cloned.1.call-start = ((), (), s32[]{:S(2)}) async-start(), calls=%async_computation.8 | async-start | bytes 2359296 | tf_op jit(solution)/shard_map/reduce_scatter | solution.py:166
  15.5 28.4 %collective-permute-start = (bf16[256,2048]{1,0:T(8,128)(2,1)S(1)}, bf16[256,2048]{1,0:T(8,128)(2,1)}, u32[]{:S(2)}, u32[]{:S(2)}) collective-permute-start(bf16[256,2048]{1,0:T(8,128)(2,1)S(1)} %copy-done.4), channel_id=1, source_target_pairs={{0,1},{1,2},{2,3},{3,0},{4,5},{5,6},{6,7},{7,4},{8,9},{9,10},{10,1... | collective-permute-start | bytes 3145736 | tf_op jit(solution)/shard_map/ppermute | solution.py:142
  32.1 96.7 %copy-start.39 = (f32[1024,32]{0,1:T(8,128)}, f32[1024,32]{0,1:T(8,128)S(1)}, u32[]{:S(2)}) copy-start(f32[1024,32]{0,1:T(8,128)S(1)} %get-tuple-element.121) | copy-start | bytes 393220
  32.6 127.8 %copy-start.17 = (pred[512,1024]{0,1:T(8,128)(4,1)}, pred[512,1024]{0,1:T(8,128)(4,1)S(1)}, u32[]{:S(2)}) copy-start(pred[512,1024]{0,1:T(8,128)(4,1)S(1)} %fusion.78) | copy-start | bytes 1572868
  43.9 26.3 %collective-permute-start.1 = (bf16[256,2048]{1,0:T(8,128)(2,1)}, bf16[256,2048]{1,0:T(8,128)(2,1)S(1)}, u32[]{:S(2)}, u32[]{:S(2)}) collective-permute-start(bf16[256,2048]{1,0:T(8,128)(2,1)} %collective-permute-done), channel_id=1, source_target_pairs={{0,1},{1,2},{2,3},{3,0},{4,5},{5,6},{6,7},{7,4},{8,9},{9,10},{10,1... | collective-permute-start | bytes 3145736 | tf_op jit(solution)/shard_map/ppermute | solution.py:142
  43.9 52.2 %copy-start.63 = (f32[1,1,2048]{2,1,0:T(1,128)}, f32[1,1,2048]{2,1,0:T(1,128)S(1)}, u32[]{:S(2)}) copy-start(f32[1,1,2048]{2,1,0:T(1,128)S(1)} %get-tuple-element.118) | copy-start | bytes 24580
  43.9 213.5 %copy-start.65 = (f32[1,1,2048]{2,1,0:T(1,128)}, f32[1,1,2048]{2,1,0:T(1,128)S(1)}, u32[]{:S(2)}) copy-start(f32[1,1,2048]{2,1,0:T(1,128)S(1)} %get-tuple-element.117) | copy-start | bytes 24580
  44.5 51.0 %copy-start.23 = (bf16[256,2048]{1,0:T(8,128)(2,1)S(1)}, bf16[256,2048]{1,0:T(8,128)(2,1)}, u32[]{:S(2)}) copy-start(bf16[256,2048]{1,0:T(8,128)(2,1)} %convert_element_type.255) | copy-start | bytes 3145732
  70.2 25.3 %collective-permute-start.2 = (bf16[256,2048]{1,0:T(8,128)(2,1)S(1)}, bf16[256,2048]{1,0:T(8,128)(2,1)S(1)}, u32[]{:S(2)}, u32[]{:S(2)}) collective-permute-start(bf16[256,2048]{1,0:T(8,128)(2,1)S(1)} %collective-permute-done.1), channel_id=1, source_target_pairs={{0,1},{1,2},{2,3},{3,0},{4,5},{5,6},{6,7},{7,4},{8,9},{9,10},{10,1... | collective-permute-start | bytes 3145736 | tf_op jit(solution)/shard_map/ppermute | solution.py:142
  95.5 24.5 %collective-permute-start.3 = (bf16[256,2048]{1,0:T(8,128)(2,1)S(1)}, bf16[256,2048]{1,0:T(8,128)(2,1)}, u32[]{:S(2)}, u32[]{:S(2)}) collective-permute-start(bf16[256,2048]{1,0:T(8,128)(2,1)S(1)} %copy-done.23), channel_id=1, source_target_pairs={{0,1},{1,2},{2,3},{3,0},{4,5},{5,6},{6,7},{7,4},{8,9},{9,10},{10,1... | collective-permute-start | bytes 3145736 | tf_op jit(solution)/shard_map/ppermute | solution.py:142
  96.5 29.8 %copy-start.68 = (f32[256]{0:T(256)}, f32[256]{0:T(256)S(1)}, u32[]{:S(2)}) copy-start(f32[256]{0:T(256)S(1)} %add_rsqrt_fusion.1) | copy-start | bytes 3076
  120.0 44.7 %collective-permute-start.4 = (bf16[256,2048]{1,0:T(8,128)(2,1)}, bf16[256,2048]{1,0:T(8,128)(2,1)}, u32[]{:S(2)}, u32[]{:S(2)}) collective-permute-start(bf16[256,2048]{1,0:T(8,128)(2,1)} %collective-permute-done.3), channel_id=1, source_target_pairs={{0,1},{1,2},{2,3},{3,0},{4,5},{5,6},{6,7},{7,4},{8,9},{9,10},{10,1... | collective-permute-start | bytes 3145736 | tf_op jit(solution)/shard_map/ppermute | solution.py:142
  128.1 133.3 %copy-start.35 = (bf16[1024,2,32]{0,2,1:T(8,128)(2,1)}, bf16[1024,2,32]{0,2,1:T(8,128)(2,1)S(1)}, u32[]{:S(2)}) copy-start(bf16[1024,2,32]{0,2,1:T(8,128)(2,1)S(1)} %get-tuple-element.111) | copy-start | bytes 393220
  128.1 133.3 %copy-start.37 = (bf16[1024,2,32]{0,2,1:T(8,128)(2,1)}, bf16[1024,2,32]{0,2,1:T(8,128)(2,1)S(1)}, u32[]{:S(2)}) copy-start(bf16[1024,2,32]{0,2,1:T(8,128)(2,1)S(1)} %get-tuple-element.112) | copy-start | bytes 393220
  130.2 131.2 %copy-start.15 = (bf16[512,2,4,64]{0,3,2,1:T(8,128)(2,1)}, bf16[512,2,4,64]{0,3,2,1:T(8,128)(2,1)S(1)}, u32[]{:S(2)}) copy-start(bf16[512,2,4,64]{0,3,2,1:T(8,128)(2,1)S(1)} %pad_maximum_fusion.5) | copy-start | bytes 1572868
  164.7 89.0 %copy-start.6 = (bf16[1024,2,4,64]{0,3,2,1:T(8,128)(2,1)}, bf16[1024,2,4,64]{0,3,2,1:T(8,128)(2,1)S(1)}, u32[]{:S(2)}) copy-start(bf16[1024,2,4,64]{0,3,2,1:T(8,128)(2,1)S(1)} %pad_maximum_fusion.3) | copy-start | bytes 3145732
  164.7 36.7 %copy-start.2 = (bf16[1,512,2048]{2,1,0:T(8,128)(2,1)S(1)}, bf16[1,512,2048]{2,1,0:T(8,128)(2,1)}, u32[]{:S(2)}) copy-start(bf16[1,512,2048]{2,1,0:T(8,128)(2,1)} %all-gather.12.cloned.1.call-done) | copy-start | bytes 6291460
  167.4 33.9 %collective-permute-start.5 = (bf16[256,2048]{1,0:T(8,128)(2,1)S(1)}, bf16[256,2048]{1,0:T(8,128)(2,1)S(1)}, u32[]{:S(2)}, u32[]{:S(2)}) collective-permute-start(bf16[256,2048]{1,0:T(8,128)(2,1)S(1)} %convolution_convert_fusion.5), channel_id=1, source_target_pairs={{0,1},{1,2},{2,3},{3,0},{4,5},{5,6},{6,7},{7,4},{8,9},{9,10},{10,1... | collective-permute-start | bytes 3145736 | tf_op jit(solution)/shard_map/ppermute | solution.py:142
  202.1 22.9 %collective-permute-start.6 = (bf16[256,2048]{1,0:T(8,128)(2,1)S(1)}, bf16[256,2048]{1,0:T(8,128)(2,1)S(1)}, u32[]{:S(2)}, u32[]{:S(2)}) collective-permute-start(bf16[256,2048]{1,0:T(8,128)(2,1)S(1)} %fusion.33), channel_id=1, source_target_pairs={{0,1},{1,2},{2,3},{3,0},{4,5},{5,6},{6,7},{7,4},{8,9},{9,10},{10,1... | collective-permute-start | bytes 3145736 | tf_op jit(solution)/shard_map/ppermute | solution.py:142
  225.8 27.9 %collective-permute-start.7 = (bf16[256,2048]{1,0:T(8,128)(2,1)S(1)}, bf16[256,2048]{1,0:T(8,128)(2,1)S(1)}, u32[]{:S(2)}, u32[]{:S(2)}) collective-permute-start(bf16[256,2048]{1,0:T(8,128)(2,1)S(1)} %fusion.34), channel_id=1, source_target_pairs={{0,1},{1,2},{2,3},{3,0},{4,5},{5,6},{6,7},{7,4},{8,9},{9,10},{10,1... | collective-permute-start | bytes 3145736 | tf_op jit(solution)/shard_map/ppermute | solution.py:142
  231.8 44.3 %collective-permute-start.12 = (bf16[256,2048]{1,0:T(8,128)(2,1)}, bf16[256,2048]{1,0:T(8,128)(2,1)S(1)}, u32[]{:S(2)}, u32[]{:S(2)}) collective-permute-start(bf16[256,2048]{1,0:T(8,128)(2,1)} %collective-permute-done.4), channel_id=1, source_target_pairs={{0,1},{1,2},{2,3},{3,0},{4,5},{5,6},{6,7},{7,4},{8,9},{9,10},{10,1... | collective-permute-start | bytes 3145736 | tf_op jit(solution)/shard_map/ppermute | solution.py:142
  258.6 34.1 %collective-permute-start.8 = (bf16[256,2048]{1,0:T(8,128)(2,1)S(1)}, bf16[256,2048]{1,0:T(8,128)(2,1)S(1)}, u32[]{:S(2)}, u32[]{:S(2)}) collective-permute-start(bf16[256,2048]{1,0:T(8,128)(2,1)S(1)} %get-tuple-element.82), channel_id=1, source_target_pairs={{0,1},{1,2},{2,3},{3,0},{4,5},{5,6},{6,7},{7,4},{8,9},{9,10},{10,1... | collective-permute-start | bytes 3145736 | tf_op jit(solution)/shard_map/ppermute | solution.py:142
  319.2 48.7 %collective-permute-start.10 = (bf16[256,2048]{1,0:T(8,128)(2,1)S(1)}, bf16[256,2048]{1,0:T(8,128)(2,1)S(1)}, u32[]{:S(2)}, u32[]{:S(2)}) collective-permute-start(bf16[256,2048]{1,0:T(8,128)(2,1)S(1)} %copy-done.59), channel_id=1, source_target_pairs={{0,1},{1,2},{2,3},{3,0},{4,5},{5,6},{6,7},{7,4},{8,9},{9,10},{10,1... | collective-permute-start | bytes 3145736 | tf_op jit(solution)/shard_map/ppermute | solution.py:142
  354.7 44.0 %collective-permute-start.9 = (bf16[256,2048]{1,0:T(8,128)(2,1)S(1)}, bf16[256,2048]{1,0:T(8,128)(2,1)}, u32[]{:S(2)}, u32[]{:S(2)}) collective-permute-start(bf16[256,2048]{1,0:T(8,128)(2,1)S(1)} %convolution_add_fusion.6), channel_id=1, source_target_pairs={{0,1},{1,2},{2,3},{3,0},{4,5},{5,6},{6,7},{7,4},{8,9},{9,10},{10,1... | collective-permute-start | bytes 3145736 | tf_op jit(solution)/shard_map/ppermute | solution.py:142
  367.9 43.0 %collective-permute-start.13 = (bf16[256,2048]{1,0:T(8,128)(2,1)S(1)}, bf16[256,2048]{1,0:T(8,128)(2,1)S(1)}, u32[]{:S(2)}, u32[]{:S(2)}) collective-permute-start(bf16[256,2048]{1,0:T(8,128)(2,1)S(1)} %collective-permute-done.10), channel_id=1, source_target_pairs={{0,1},{1,2},{2,3},{3,0},{4,5},{5,6},{6,7},{7,4},{8,9},{9,10},{10,1... | collective-permute-start | bytes 3145736 | tf_op jit(solution)/shard_map/ppermute | solution.py:142
  405.9 43.1 %collective-permute-start.11 = (bf16[256,2048]{1,0:T(8,128)(2,1)}, bf16[256,2048]{1,0:T(8,128)(2,1)S(1)}, u32[]{:S(2)}, u32[]{:S(2)}) collective-permute-start(bf16[256,2048]{1,0:T(8,128)(2,1)} %add_convert_fusion.4), channel_id=1, source_target_pairs={{0,1},{1,2},{2,3},{3,0},{4,5},{5,6},{6,7},{7,4},{8,9},{9,10},{10,1... | collective-permute-start | bytes 3145736 | tf_op jit(solution)/shard_map/ppermute | solution.py:142
  450.3 28.8 %collective-permute-start.14 = (bf16[256,2048]{1,0:T(8,128)(2,1)}, bf16[256,2048]{1,0:T(8,128)(2,1)S(1)}, u32[]{:S(2)}, u32[]{:S(2)}) collective-permute-start(bf16[256,2048]{1,0:T(8,128)(2,1)} %add_convert_fusion.3), channel_id=1, source_target_pairs={{0,1},{1,2},{2,3},{3,0},{4,5},{5,6},{6,7},{7,4},{8,9},{9,10},{10,1... | collective-permute-start | bytes 3145736 | tf_op jit(solution)/shard_map/ppermute | solution.py:142
  485.7 23.5 %collective-permute-start.15 = (bf16[256,2048]{1,0:T(8,128)(2,1)S(1)}, bf16[256,2048]{1,0:T(8,128)(2,1)}, u32[]{:S(2)}, u32[]{:S(2)}) collective-permute-start(bf16[256,2048]{1,0:T(8,128)(2,1)S(1)} %get-tuple-element.63), channel_id=1, source_target_pairs={{0,1},{1,2},{2,3},{3,0},{4,5},{5,6},{6,7},{7,4},{8,9},{9,10},{10,1... | collective-permute-start | bytes 3145736 | tf_op jit(solution)/shard_map/ppermute | solution.py:142
  509.2 23.3 %collective-permute-start.16 = (bf16[256,2048]{1,0:T(8,128)(2,1)}, bf16[256,2048]{1,0:T(8,128)(2,1)}, u32[]{:S(2)}, u32[]{:S(2)}) collective-permute-start(bf16[256,2048]{1,0:T(8,128)(2,1)} %collective-permute-done.15), channel_id=1, source_target_pairs={{0,1},{1,2},{2,3},{3,0},{4,5},{5,6},{6,7},{7,4},{8,9},{9,10},{10,1... | collective-permute-start | bytes 3145736 | tf_op jit(solution)/shard_map/ppermute | solution.py:142
  532.6 23.3 %collective-permute-start.17 = (bf16[256,2048]{1,0:T(8,128)(2,1)}, bf16[256,2048]{1,0:T(8,128)(2,1)}, u32[]{:S(2)}, u32[]{:S(2)}) collective-permute-start(bf16[256,2048]{1,0:T(8,128)(2,1)} %collective-permute-done.16), channel_id=1, source_target_pairs={{0,1},{1,2},{2,3},{3,0},{4,5},{5,6},{6,7},{7,4},{8,9},{9,10},{10,1... | collective-permute-start | bytes 3145736 | tf_op jit(solution)/shard_map/ppermute | solution.py:142
  555.9 21.9 %collective-permute-start.18 = (bf16[256,2048]{1,0:T(8,128)(2,1)}, bf16[256,2048]{1,0:T(8,128)(2,1)}, u32[]{:S(2)}, u32[]{:S(2)}) collective-permute-start(bf16[256,2048]{1,0:T(8,128)(2,1)} %fusion.22), channel_id=1, source_target_pairs={{0,1},{1,2},{2,3},{3,0},{4,5},{5,6},{6,7},{7,4},{8,9},{9,10},{10,1... | collective-permute-start | bytes 3145736 | tf_op jit(solution)/shard_map/ppermute | solution.py:142
  579.4 30.9 %collective-permute-start.19 = (bf16[256,2048]{1,0:T(8,128)(2,1)S(1)}, bf16[256,2048]{1,0:T(8,128)(2,1)}, u32[]{:S(2)}, u32[]{:S(2)}) collective-permute-start(bf16[256,2048]{1,0:T(8,128)(2,1)S(1)} %add_convert_fusion.2), channel_id=1, source_target_pairs={{0,1},{1,2},{2,3},{3,0},{4,5},{5,6},{6,7},{7,4},{8,9},{9,10},{10,1... | collective-permute-start | bytes 3145736 | tf_op jit(solution)/shard_map/ppermute | solution.py:142
  610.3 35.1 %copy-start.43 = (bf16[1024,768]{0,1:T(8,128)(2,1)}, bf16[1024,768]{0,1:T(8,128)(2,1)S(1)}, u32[]{:S(2)}) copy-start(bf16[1024,768]{0,1:T(8,128)(2,1)S(1)} %pad_maximum_fusion.1) | copy-start | bytes 4718596
  617.2 28.1 %collective-permute-start.21 = (bf16[256,2048]{1,0:T(8,128)(2,1)S(1)}, bf16[256,2048]{1,0:T(8,128)(2,1)S(1)}, u32[]{:S(2)}, u32[]{:S(2)}) collective-permute-start(bf16[256,2048]{1,0:T(8,128)(2,1)S(1)} %get-tuple-element.108), channel_id=1, source_target_pairs={{0,1},{1,2},{2,3},{3,0},{4,5},{5,6},{6,7},{7,4},{8,9},{9,10},{10,1... | collective-permute-start | bytes 3145736 | tf_op jit(solution)/shard_map/ppermute | solution.py:142
  626.3 37.5 %collective-permute-start.20 = (bf16[256,2048]{1,0:T(8,128)(2,1)}, bf16[256,2048]{1,0:T(8,128)(2,1)}, u32[]{:S(2)}, u32[]{:S(2)}) collective-permute-start(bf16[256,2048]{1,0:T(8,128)(2,1)} %add_convert_fusion.1), channel_id=1, source_target_pairs={{0,1},{1,2},{2,3},{3,0},{4,5},{5,6},{6,7},{7,4},{8,9},{9,10},{10,1... | collective-permute-start | bytes 3145736 | tf_op jit(solution)/shard_map/ppermute | solution.py:142
  647.6 36.5 %collective-permute-start.22 = (bf16[256,2048]{1,0:T(8,128)(2,1)}, bf16[256,2048]{1,0:T(8,128)(2,1)}, u32[]{:S(2)}, u32[]{:S(2)}) collective-permute-start(bf16[256,2048]{1,0:T(8,128)(2,1)} %get-tuple-element.110), channel_id=1, source_target_pairs={{0,1},{1,2},{2,3},{3,0},{4,5},{5,6},{6,7},{7,4},{8,9},{9,10},{10,1... | collective-permute-start | bytes 3145736 | tf_op jit(solution)/shard_map/ppermute | solution.py:142
  651.5 103.6 %reduce-scatter.6.cloned.1.call-start = ((), (), s32[]{:S(2)}) async-start(), calls=%async_computation.7 | async-start | bytes 4128768 | tf_op jit(solution)/shard_map/reduce_scatter | solution.py:166
  685.7 16.7 %collective-permute-start.23 = (bf16[256,2048]{1,0:T(8,128)(2,1)S(1)}, bf16[256,2048]{1,0:T(8,128)(2,1)S(1)}, u32[]{:S(2)}, u32[]{:S(2)}) collective-permute-start(bf16[256,2048]{1,0:T(8,128)(2,1)S(1)} %convert_add_fusion.1), channel_id=1, source_target_pairs={{0,1},{1,2},{2,3},{3,0},{4,5},{5,6},{6,7},{7,4},{8,9},{9,10},{10,1... | collective-permute-start | bytes 3145736 | tf_op jit(solution)/shard_map/ppermute | solution.py:142
  707.3 122.7 %reduce-scatter.14.cloned.1.call-start = ((), (), s32[]{:S(2)}) async-start(), calls=%async_computation.11 | async-start | bytes 9437184 | tf_op jit(solution)/shard_map/reduce_scatter | solution.py:166
  708.1 196.9 %reduce-scatter.12.cloned.1.call-start = ((), (), s32[]{:S(2)}) async-start(), calls=%async_computation.10 | async-start | bytes 9437184 | tf_op jit(solution)/shard_map/reduce_scatter | solution.py:166
  708.8 271.2 %reduce-scatter.10.cloned.1.call-start = ((), (), s32[]{:S(2)}) async-start(), calls=%async_computation.9 | async-start | bytes 9437184 | tf_op jit(solution)/shard_map/reduce_scatter | solution.py:166
  755.7 75.8 %collective-permute-start.24 = (f32[256,2]{0,1:T(2,128)S(1)}, f32[256,2]{0,1:T(2,128)S(1)}, u32[]{:S(2)}, u32[]{:S(2)}) collective-permute-start(f32[256,2]{0,1:T(2,128)S(1)} %slice.190), channel_id=1, source_target_pairs={{0,1},{1,2},{2,3},{3,0},{4,5},{5,6},{6,7},{7,4},{8,9},{9,10},{10,1... | collective-permute-start | bytes 6152 | tf_op jit(solution)/shard_map/ppermute | solution.py:142
  831.5 157.5 %collective-permute-start.25 = (f32[256,2]{0,1:T(2,128)S(1)}, f32[256,2]{0,1:T(2,128)S(1)}, u32[]{:S(2)}, u32[]{:S(2)}) collective-permute-start(f32[256,2]{0,1:T(2,128)S(1)} %collective-permute-done.24), channel_id=1, source_target_pairs={{0,1},{1,2},{2,3},{3,0},{4,5},{5,6},{6,7},{7,4},{8,9},{9,10},{10,1... | collective-permute-start | bytes 6152 | tf_op jit(solution)/shard_map/ppermute | solution.py:142
  989.0 5.4 collective-permute-start.26
  (85 other events, 744.7 us)
Sparse Core Ops, SparseCore 0:
  10.4 34.9 all-gather.7
  47.3 28.0 all-gather.11
  77.3 55.8 all-gather.13
  135.5 89.7 all-gather.9
  651.6 41.9 reduce-scatter.7
  707.5 47.5 reduce-scatter.5
  758.5 71.4 reduce-scatter.13
  833.5 71.5 reduce-scatter.11
  908.5 71.5 reduce-scatter.9

commit v3 on v2

--- a/solution.py
+++ b/solution.py
@@ -1,6 +1,10 @@
+import functools
+
 import jax
 import jax.numpy as jnp
 from jax import lax
+from jax.experimental import pallas as pl
+from jax.experimental.pallas import tpu as pltpu
 from jax.sharding import PartitionSpec as P
 
 
@@ -102,6 +106,78 @@
         preferred_element_type=jnp.float32,
     )
     return (grad_query, grad_key, grad_value)
+
+
+def mlp_kernel(reused, *refs):
+    x_ref, g_ref, w_gu_ref, w_down_ref = refs[:4]
+    hidden_ref, dgate_ref, dup_ref, x_all_ref, g_all_ref, back_ref, out_ref = refs[4 + reused :]
+    first = pl.program_id(0) == 0
+    dims = (((1,), (1,)), ((), ()))
+    x = x_ref[...]
+    g = g_ref[...]
+    w_gate = w_gu_ref[0]
+    w_up = w_gu_ref[1]
+    w_down = w_down_ref[...]
+    gate = jnp.dot(x, w_gate, preferred_element_type=jnp.float32)
+    up = jnp.dot(x, w_up, preferred_element_type=jnp.float32)
+    grad_hidden = lax.dot_general(g, w_down, dims, preferred_element_type=jnp.float32)
+    sigmoid_gate = 1.0 / (1.0 + jnp.exp(-gate))
+    silu_gate = gate * sigmoid_gate
+    hidden = (silu_gate * up).astype(jnp.bfloat16)
+    dgate = (grad_hidden * up * sigmoid_gate * (1.0 + gate * (1.0 - sigmoid_gate))).astype(
+        jnp.bfloat16
+    )
+    dup = (grad_hidden * silu_gate).astype(jnp.bfloat16)
+    hidden_ref[...] = hidden
+    dgate_ref[...] = dgate
+    dup_ref[...] = dup
+
+    @pl.when(first)
+    def _():
+        x_all_ref[...] = x
+        g_all_ref[...] = g
+        out_ref[...] = jnp.zeros_like(out_ref)
+        back_ref[...] = jnp.zeros_like(back_ref)
+
+    out_ref[...] += jnp.dot(hidden, w_down, preferred_element_type=jnp.float32)
+    back_ref[...] += lax.dot_general(
+        dgate, w_gate, dims, preferred_element_type=jnp.float32
+    ) + lax.dot_general(dup, w_up, dims, preferred_element_type=jnp.float32)
+
+
+def mlp_block(step, ring, x, g, w_gu, w_down, kept):
+    rows, width = x.shape
+    hidden_width = w_down.shape[0]
+    tile = min(512, hidden_width)
+    bf16, f32 = jnp.bfloat16, jnp.float32
+    wide = jax.ShapeDtypeStruct((ring * rows, hidden_width), bf16)
+    whole = jax.ShapeDtypeStruct((ring * rows, width), bf16)
+    part = jax.ShapeDtypeStruct((rows, width), f32)
+    wide_spec = pl.BlockSpec((rows, tile), lambda t: (step, t))
+    whole_spec = pl.BlockSpec((rows, width), lambda t: (step, 0))
+    block_spec = pl.BlockSpec((rows, width), lambda t: (0, 0))
+    reused = len(kept)
+    return pl.pallas_call(
+        functools.partial(mlp_kernel, reused),
+        grid=(hidden_width // tile,),
+        out_shape=(wide, wide, wide, whole, whole, part, part),
+        in_specs=[
+            block_spec,
+            block_spec,
+            pl.BlockSpec((2, width, tile), lambda t: (0, 0, t)),
+            pl.BlockSpec((tile, width), lambda t: (t, 0)),
+        ]
+        + [pl.BlockSpec(memory_space=pl.ANY)] * reused,
+        out_specs=(wide_spec, wide_spec, wide_spec, whole_spec, whole_spec, block_spec, block_spec),
+        input_output_aliases={4 + i: i for i in range(reused)},
+        cost_estimate=pl.CostEstimate(
+            flops=12 * rows * width * hidden_width,
+            bytes_accessed=6 * width * hidden_width + 12 * rows * width,
+            transcendentals=rows * hidden_width,
+        ),
+        compiler_params=pltpu.CompilerParams(vmem_limit_bytes=44 << 20),
+        name="mlp_block",
+    )(x, g, w_gu, w_down, *kept)
 
 
 def per_device(
@@ -149,7 +225,7 @@
 
     def spread(rows):
         blocks = [rows]
-        for _ in range(ring - 1):
+        for _ in range(1, ring):
             blocks.append(shift(blocks[-1]))
         return blocks
 
@@ -161,9 +237,6 @@
 
     def rows_of(whole, step):
         return lax.dynamic_slice_in_dim(whole, block_start_of(step), local_rows, 0)
-
-    def scatter_sum(grad):
-        return lax.psum_scatter(grad, "fsdp", scatter_dimension=0, tiled=True).astype(f32)
 
     def collect(parts, last_gate=None):
         total = parts[1 % ring].astype(f32)
@@ -183,7 +256,6 @@
         jnp.swapaxes(w_gate_up[0], 0, 1), "fsdp", axis=1, tiled=True
     )
     w_down_all = lax.all_gather(w_down[0], "fsdp", axis=1, tiled=True)
-    w_gate, w_up = w_gu_all[0], w_gu_all[1]
 
     cosine, sine_table = rope_tables(doc_row, head_size)
     block_starts = list(range(0, row_count, block_rows))
@@ -218,8 +290,8 @@
             key_rows[key_low:key_high],
             value_rows[key_low:key_high],
         )
-        if block_index == len(block_starts) - 1:
-            attend_inputs = after(attend_inputs, grad_blocks[1 % ring])
+        if block_index > 0:
+            attend_inputs = after(attend_inputs, out_list[-1])
         out_block, log_total = attend_block(
             *attend_inputs,
             mask_list[block_index],
@@ -228,44 +300,37 @@
         out_list.append(out_block)
         total_list.append(log_total)
     attended = jnp.concatenate(out_list, axis=0).reshape(row_count, -1)
-    attended = after(attended, grad_blocks[2 % ring])
-    middle = residual + collect(
-        [dot(rows_of(attended, step), w_out_all) for step in range(ring)]
-    )
+    middle = residual + collect([dot(rows_of(attended, step), w_out_all) for step in range(ring)])
     inv_mlp, normed_mlp = norm_apply(middle, gains_all[1])
 
     normed_mlp_blocks = [normed_mlp]
-    hidden_blocks, dgate_blocks, dup_blocks, back_parts = [], [], [], []
+    kept, back_parts, out_parts = (), [], []
     for step in range(ring):
-        if step == 1:
-            normed_mlp_blocks.append(shift(normed_mlp))
-        elif step > 1:
-            gate = dup_blocks[0] if step == 2 else back_parts[step - 2]
-            normed_mlp_blocks.append(shift(after(normed_mlp_blocks[-1], gate)))
+        if step > 0:
+            source = normed_mlp_blocks[-1]
+            if step > 1:
+                source = after(source, back_parts[step - 2])
+            normed_mlp_blocks.append(shift(source))
         rows = normed_mlp_blocks[step]
-        if step == 1:
-            rows = after(rows, (dgate_blocks[0], dup_blocks[0]))
-        elif step > 1:
+        if step > 0:
             rows = after(rows, back_parts[step - 1])
-        gate = dot(rows, w_gate)
-        up = dot(rows, w_up)
-        grad_hidden = dot_nt(grad_blocks[step], w_down_all)
-        sigmoid_gate = jax.nn.sigmoid(gate)
-        silu_gate = gate * sigmoid_gate
-        hidden_blocks.append((silu_gate * up).astype(bf16))
-        dgate = (grad_hidden * up * sigmoid_gate * (1.0 + gate * (1.0 - sigmoid_gate))).astype(bf16)
-        dup = (grad_hidden * silu_gate).astype(bf16)
-        dgate_blocks.append(dgate)
-        dup_blocks.append(dup)
-        back_parts.append(dot_nt(dgate, w_gate) + dot_nt(dup, w_up))
+        *kept, back_part, out_part = mlp_block(
+            step, ring, rows, grad_blocks[step], w_gu_all, w_down_all, tuple(kept)
+        )
+        back_parts.append(back_part)
+        out_parts.append(out_part)
+    hidden_all, dgate_all, dup_all, normed_mlp_all, grad_all = kept
     grad_normed_mlp = collect(back_parts)
-    grad_down = dot_tn(in_order(grad_blocks), in_order(hidden_blocks)).astype(bf16)
-    normed_mlp_all = in_order(normed_mlp_blocks)
-    grad_wgate = dot_tn(normed_mlp_all, in_order(dgate_blocks)).astype(bf16)
-    grad_wup = dot_tn(normed_mlp_all, in_order(dup_blocks)).astype(bf16)
-    grad_normed_mlp = after(grad_normed_mlp, (grad_down, grad_wgate))
-    grad_down = jnp.swapaxes(scatter_sum(grad_down), 0, 1)
-    grad_wgate = scatter_sum(grad_wgate)
+    weight_grads = []
+    for left, right in (
+        (grad_all, hidden_all), (normed_mlp_all, dgate_all), (normed_mlp_all, dup_all)
+    ):
+        weight_grads.append(dot_tn(left, right).astype(bf16))
+    grad_mlp = jnp.stack(weight_grads)
+    grad_mlp = lax.psum_scatter(grad_mlp, "fsdp", scatter_dimension=1, tiled=True)
+    grad_mlp = grad_mlp.astype(f32)
+    grad_down = jnp.swapaxes(grad_mlp[0], 0, 1)
+    grad_wgu = jnp.swapaxes(grad_mlp[1:], 0, 1)
     norm_part, grad_gain_mlp = norm_back(middle, inv_mlp, gains_all[1], grad_normed_mlp)
     grad_middle = out_cotangent + norm_part
 
@@ -274,12 +339,8 @@
     grad_attended = in_order(do_parts).reshape(row_count, kv_local, group_size, head_size)
     middle_all = in_order(middle_blocks)
 
-    grad_attended = after(grad_attended, grad_wup)
-    grad_wup = scatter_sum(grad_wup)
-    grad_wgu = jnp.stack([grad_wgate, grad_wup], axis=1)
-    grad_wo = jnp.swapaxes(scatter_sum(dot_tn(middle_all, attended).astype(bf16)), 0, 1)
-
-    out_parts = [dot(hidden, w_down_all) for hidden in hidden_blocks]
+    grad_wo = dot_tn(middle_all, attended).astype(bf16)
+
     out_totals = [after(out_parts[1 % ring], middle_blocks[-1]).astype(bf16)]
     for step in range(2, ring + 1):
         out_totals.append((shift(out_totals[-1]).astype(f32) + out_parts[step % ring]))
@@ -333,15 +394,22 @@
     grad_wqkv = dot_tn(normed_all, grad_qkv).astype(bf16)
     gain_columns = jnp.stack([grad_gain_attn, grad_gain_mlp], axis=1).astype(bf16)
     gain_columns = jnp.pad(gain_columns, ((0, 0), (0, 126)))
-    packed = scatter_sum(jnp.concatenate([grad_wqkv, gain_columns], axis=1))
+    packed = lax.psum_scatter(
+        jnp.concatenate([grad_wqkv, grad_wo, gain_columns], axis=1),
+        "fsdp", scatter_dimension=0, tiled=True,
+    )
+    packed = packed.astype(f32)
     qkv_width = grad_wqkv.shape[1]
+    gain_start = qkv_width + grad_wo.shape[1]
     grad_wq = packed[:, :query_width]
     grad_wkv = packed[:, query_width:qkv_width].reshape(-1, kv_local, 2 * head_size)
-    gain_part = packed[:, qkv_width : qkv_width + 2]
+    grad_wo = jnp.swapaxes(packed[:, qkv_width:gain_start], 0, 1)
+    gain_part = packed[:, gain_start : gain_start + 2]
     gain_total = gain_part
-    for _ in range(ring - 1):
-        gain_part = shift(gain_part)
-        gain_total = gain_total + gain_part
+    for distance in range(1, ring):
+        gain_total = gain_total + lax.ppermute(
+            gain_part, "tensor", [(i, (i + distance) % ring) for i in range(ring)]
+        )
     return (
         output_rows,
         grad_rows,

time: 1010 us -> 883 us (0.87)
  matrix products: 310 us -> 132 us
  Pallas kernels: 0 us -> 78.5 us
  starting transfers between devices: 30.8 us -> 10.5 us
    ppermute x27 -> x24, waiting for transfers between devices: 263 us -> 368 us  [shift(): return lax.ppermute(rows, 'tensor', ring_pairs)]
    reduce_scatter x5 -> x2, waiting for transfers between devices: 257 us -> 153 us  [the longest x1 148 us: per_device(): lax.psum_scatter(grad_mlp, 'fsdp', scatter_dimension=1, tiled=True)]
    dot_general x20 -> x8, matrix products: 109 us -> 16.1 us  [dot_nt(): lax.dot_general(a, b, (((1,), (1,)), ((), ())), preferred_element_type=f32)]
    dot_general x17 -> x5, matrix products: 90.2 us -> 11.5 us  [dot(): return jnp.dot(a, b, preferred_element_type=f32)]
    pallas_call x0 -> x4, Pallas kernels: none -> 78.5 us  [mlp_block(): pl.pallas_call(functools.partial(mlp_kernel, reused), grid=(hidden_width...]
    ppermute x27 -> x24, starting transfers between devices: 30.2 us -> 4.55 us  [shift(): return lax.ppermute(rows, 'tensor', ring_pairs)]
    another operation x8 -> x9, other arithmetic: 1.19 us -> 15.4 us  [the longest x1 14.2 us: per_device(): grad_mlp = jnp.stack(weight_grads)]
    unnamed x197 -> x160, local copies, waits for them, and re-layouts: 26.7 us -> 27.5 us
  transfers between devices with their start and end apart: 36 -> 33, of which waited for: 22 -> 23; matrix products, arithmetic and copies ran while one was open for 38% -> 21% of each run, Pallas kernels for 0% -> 9%
where the time goes in v3:
time: 883 us; the launch traced here: 878 us
  waiting for transfers between devices  523 us (59%)
  matrix products  132 us (15%)
  Pallas kernels  78.5 us (9%)
  other arithmetic  62 us (7%)
  local copies, waits for them, and re-layouts  47.5 us (5%)
  between operations  15.8 us (2%)
  starting transfers between devices  10.5 us (1%)
  blocking collectives  9.05 us (1%)
    ppermute x24, waiting for transfers between devices, shift(): return lax.ppermute(rows, 'tensor', ring_pairs)  368 us
    reduce_scatter x1, waiting for transfers between devices, per_device(): lax.psum_scatter(grad_mlp, 'fsdp', scatter_dimension=1, tiled=True)  148 us
    pallas_call x4, Pallas kernels, mlp_block(): pl.pallas_call(functools.partial(mlp_kernel, reused), grid=(hidden_width...  78.5 us
    dot_general x5, matrix products, dot_tn(): lax.dot_general(a, b, (((0,), (0,)), ((), ())), preferred_element_type=f32)  44.6 us
    unnamed x160, local copies, waits for them, and re-layouts  27.5 us
  transfers between devices with their start and end apart: 33, of which 23 were waited for; matrix products, arithmetic and copies ran while one was open for 21% of the time, Pallas kernels for 9%

profile of v3, /device:TPU:0, one launch (start us, length us, event | category | flops | bytes accessed | tf_op | source)
XLA Modules:
  0.0 878.2 jit_solution(13724529618133578440)
XLA Ops:
  13.9 3.1 collective-permute-start
  19.1 9.1 %all-gather = bf16[1,2,2048]{2,1,0:T(2,128)(2,1)S(1)} all-gather(bf16[1,2,256]{2,1,0:T(2,128)(2,1)S(1)} %copy-done.74), channel_id=2, replica_groups=mesh['fsdp'=8,'tensor'=4] {'fsdp'}, dimensions={2}, use_global_device_ids=true | all-gather | bytes 9216 | tf_op jit(solution)/shard_map/all_gather | solution.py:253
  29.9 12.3 %collective-permute-done = bf16[256,2048]{1,0:T(8,128)(2,1)S(1)} collective-permute-done((bf16[256,2048]{1,0:T(8,128)(2,1)S(1)}, bf16[256,2048]{1,0:T(8,128)(2,1)S(1)}, u32[]{:S(2)}, u32[]{:S(2)}) %collective-permute-start) | collective-permute-done | bytes 1048608 | tf_op jit(solution)/shard_map/ppermute | solution.py:218
  46.3 22.0 %collective-permute-done.1 = bf16[256,2048]{1,0:T(8,128)(2,1)S(1)} collective-permute-done((bf16[256,2048]{1,0:T(8,128)(2,1)S(1)}, bf16[256,2048]{1,0:T(8,128)(2,1)S(1)}, u32[]{:S(2)}, u32[]{:S(2)}) %collective-permute-start.1) | collective-permute-done | bytes 1048608 | tf_op jit(solution)/shard_map/ppermute | solution.py:218
  71.7 22.4 %collective-permute-done.2 = bf16[256,2048]{1,0:T(8,128)(2,1)S(1)} collective-permute-done((bf16[256,2048]{1,0:T(8,128)(2,1)S(1)}, bf16[256,2048]{1,0:T(8,128)(2,1)S(1)}, u32[]{:S(2)}, u32[]{:S(2)}) %collective-permute-start.2) | collective-permute-done | bytes 1048608 | tf_op jit(solution)/shard_map/ppermute | solution.py:218
  96.3 6.2 fusion.143
  111.9 3.1 convolution_convert_fusion.3
  115.0 7.6 fusion.5
  122.6 9.2 %exponential_reduce_fusion = f32[2,4,512]{2,1,0:T(4,128)S(1)} fusion(f32[2,1024,512,4]{2,1,3,0:T(8,128)} %get-tuple-element.139, f32[2,4,512]{2,1,0:T(4,128)S(1)} %get-tuple-element.138, pred[512,1024]{0,1:T(8,128)(4,1)S(1)} %fusion.58), kind=kLoop, calls=%fused_computation.10 | loop fusion | flops 16773120 | bytes 17334272 | tf_op jit(solution)/shard_map/reduce_sum | solution.py:72
  132.4 8.1 fusion.59
  142.4 3.0 convolution_convert_fusion.2
  145.8 27.6 %collective-permute-done.3 = bf16[256,2048]{1,0:T(8,128)(2,1)S(1)} collective-permute-done((bf16[256,2048]{1,0:T(8,128)(2,1)S(1)}, bf16[256,2048]{1,0:T(8,128)(2,1)S(1)}, u32[]{:S(2)}, u32[]{:S(2)}) %collective-permute-start.3) | collective-permute-done | bytes 1048608 | tf_op jit(solution)/shard_map/ppermute | solution.py:218
  174.2 21.6 %collective-permute-done.7.refs_1_ = bf16[256,2048]{1,0:T(8,128)(2,1)S(1)} collective-permute-done((bf16[256,2048]{1,0:T(8,128)(2,1)S(1)}, bf16[256,2048]{1,0:T(8,128)(2,1)S(1)}, u32[]{:S(2)}, u32[]{:S(2)}) %collective-permute-start.7) | collective-permute-done | bytes 1048608 | tf_op jit(solution)/shard_map/ppermute | solution.py:218
  196.6 21.7 %collective-permute-done.4 = bf16[256,2048]{1,0:T(8,128)(2,1)S(1)} collective-permute-done((bf16[256,2048]{1,0:T(8,128)(2,1)S(1)}, bf16[256,2048]{1,0:T(8,128)(2,1)S(1)}, u32[]{:S(2)}, u32[]{:S(2)}) %collective-permute-start.4) | collective-permute-done | bytes 1048608 | tf_op jit(solution)/shard_map/ppermute | solution.py:218
  218.7 22.1 %collective-permute-done.10.refs_1_ = bf16[256,2048]{1,0:T(8,128)(2,1)S(1)} collective-permute-done((bf16[256,2048]{1,0:T(8,128)(2,1)S(1)}, bf16[256,2048]{1,0:T(8,128)(2,1)S(1)}, u32[]{:S(2)}, u32[]{:S(2)}) %collective-permute-start.10) | collective-permute-done | bytes 1048608 | tf_op jit(solution)/shard_map/ppermute | solution.py:218
  241.5 21.7 %collective-permute-done.5 = bf16[256,2048]{1,0:T(8,128)(2,1)S(1)} collective-permute-done((bf16[256,2048]{1,0:T(8,128)(2,1)S(1)}, bf16[256,2048]{1,0:T(8,128)(2,1)S(1)}, u32[]{:S(2)}, u32[]{:S(2)}) %collective-permute-start.5) | collective-permute-done | bytes 1048608 | tf_op jit(solution)/shard_map/ppermute | solution.py:218
  267.6 20.1 %mlp_block.4 = (bf16[1024,2048]{1,0:T(8,128)(2,1)}, bf16[1024,2048]{1,0:T(8,128)(2,1)}, bf16[1024,2048]{1,0:T(8,128)(2,1)}, bf16[1024,2048]{1,0:T(8,128)(2,1)}, ...) custom-call(bf16[256,2048]{1,0:T(8,128)(2,1)} %multiply_convert_fusion.refs_0_, ...), custom_call_target="tpu_custom_call" | custom-call | flops 12884901888 | bytes 31457280 | tf_op jit(solution)/shard_map/mlp_block/pallas_call | solution.py:160
  287.7 16.5 %collective-permute-done.6.refs_0_ = bf16[256,2048]{1,0:T(8,128)(2,1)} collective-permute-done((bf16[256,2048]{1,0:T(8,128)(2,1)}, bf16[256,2048]{1,0:T(8,128)(2,1)}, u32[]{:S(2)}, u32[]{:S(2)}) %collective-permute-start.6) | collective-permute-done | bytes 1048608 | tf_op jit(solution)/shard_map/ppermute | solution.py:218
  304.2 19.8 %mlp_block.5 = (bf16[1024,2048]{1,0:T(8,128)(2,1)}, bf16[1024,2048]{1,0:T(8,128)(2,1)}, bf16[1024,2048]{1,0:T(8,128)(2,1)}, bf16[1024,2048]{1,0:T(8,128)(2,1)}, ...) custom-call(bf16[256,2048]{1,0:T(8,128)(2,1)} %collective-permute-do, ...), custom_call_target="tpu_custom_call", output_to_operand_aliasing={{0}: (4, {}), {1}: (5, {}), {2}: (6, {}), {3}: (7, {}), {4}... | custom-call | flops 12884901888 | bytes 31457280 | tf_op jit(solution)/shard_map/mlp_block/pallas_call | solution.py:160
  325.6 3.1 collective-permute-done.9.refs_0_
  328.7 18.4 %mlp_block.6 = (bf16[1024,2048]{1,0:T(8,128)(2,1)}, bf16[1024,2048]{1,0:T(8,128)(2,1)}, bf16[1024,2048]{1,0:T(8,128)(2,1)}, bf16[1024,2048]{1,0:T(8,128)(2,1)}, ...) custom-call(bf16[256,2048]{1,0:T(8,128)(2,1)S(1)} %collective-permut, ...), custom_call_target="tpu_custom_call", output_to_operand_aliasing={{0}: (4, {}), {1}: (5, {}), {2}: (6, {}), {3}: (7, {}), {4}... | custom-call | flops 12884901888 | bytes 31457280 | tf_op jit(solution)/shard_map/mlp_block/pallas_call | solution.py:160
  347.1 6.3 collective-permute-done.8
  353.8 22.1 %collective-permute-done.12.refs_0_ = bf16[256,2048]{1,0:T(8,128)(2,1)S(1)} collective-permute-done((bf16[256,2048]{1,0:T(8,128)(2,1)S(1)}, bf16[256,2048]{1,0:T(8,128)(2,1)S(1)}, u32[]{:S(2)}, u32[]{:S(2)}) %collective-permute-start.12) | collective-permute-done | bytes 1048608 | tf_op jit(solution)/shard_map/ppermute | solution.py:218
  375.9 20.2 %mlp_block.7 = (bf16[1024,2048]{1,0:T(8,128)(2,1)}, bf16[1024,2048]{1,0:T(8,128)(2,1)}, bf16[1024,2048]{1,0:T(8,128)(2,1)}, bf16[1024,2048]{1,0:T(8,128)(2,1)}, ...) custom-call(bf16[256,2048]{1,0:T(8,128)(2,1)S(1)} %collective-permut, ...), custom_call_target="tpu_custom_call", output_to_operand_aliasing={{0}: (4, {}), {1}: (5, {}), {2}: (6, {}), {3}: (7, {}), {4}... | custom-call | flops 12884901888 | bytes 31457280 | tf_op jit(solution)/shard_map/mlp_block/pallas_call | solution.py:160
  396.5 22.0 %collective-permute-done.14 = bf16[256,2048]{1,0:T(8,128)(2,1)S(1)} collective-permute-done((bf16[256,2048]{1,0:T(8,128)(2,1)S(1)}, bf16[256,2048]{1,0:T(8,128)(2,1)S(1)}, u32[]{:S(2)}, u32[]{:S(2)}) %collective-permute-start.14) | collective-permute-done | bytes 1048608 | tf_op jit(solution)/shard_map/ppermute | solution.py:218
  423.2 23.3 %collective-permute-done.15 = bf16[256,2048]{1,0:T(8,128)(2,1)S(1)} collective-permute-done((bf16[256,2048]{1,0:T(8,128)(2,1)S(1)}, bf16[256,2048]{1,0:T(8,128)(2,1)S(1)}, u32[]{:S(2)}, u32[]{:S(2)}) %collective-permute-start.15) | collective-permute-done | bytes 1048608 | tf_op jit(solution)/shard_map/ppermute | solution.py:218
  446.6 8.2 fusion.106
  454.7 14.9 %collective-permute-done.16 = bf16[256,2048]{1,0:T(8,128)(2,1)} collective-permute-done((bf16[256,2048]{1,0:T(8,128)(2,1)S(1)}, bf16[256,2048]{1,0:T(8,128)(2,1)}, u32[]{:S(2)}, u32[]{:S(2)}) %collective-permute-start.16) | collective-permute-done | bytes 1048608 | tf_op jit(solution)/shard_map/ppermute | solution.py:218
  479.6 9.8 %collective-permute-done.17 = bf16[256,2048]{1,0:T(8,128)(2,1)} collective-permute-done((bf16[256,2048]{1,0:T(8,128)(2,1)}, bf16[256,2048]{1,0:T(8,128)(2,1)}, u32[]{:S(2)}, u32[]{:S(2)}) %collective-permute-start.17) | collective-permute-done | bytes 1048608 | tf_op jit(solution)/shard_map/ppermute | solution.py:218
  489.4 3.4 fusion.76
  498.4 5.8 fusion.9
  508.7 12.3 %collective-permute-done.18 = bf16[256,2048]{1,0:T(8,128)(2,1)S(1)} collective-permute-done((bf16[256,2048]{1,0:T(8,128)(2,1)S(1)}, bf16[256,2048]{1,0:T(8,128)(2,1)S(1)}, u32[]{:S(2)}, u32[]{:S(2)}) %collective-permute-start.18) | collective-permute-done | bytes 1048608 | tf_op jit(solution)/shard_map/ppermute | solution.py:218
  521.6 9.4 %fusion.2 = bf16[2,4,512,1024]{2,3,1,0:T(8,128)(2,1)S(1)} fusion(f32[2,1024,512,4]{2,1,3,0:T(8,128)} %fusion.106, f32[2,4,512]{2,1,0:T(4,128)S(1)} %fusion.89, f32[2,4,512]{2,1,0:T(4,128)S(1)} %bitcast.304, pred[512,1024]{0,1:T(8,128)(4,1)S(1)} %copy-done.32, bf16[512,2,4,64]{0,3,2,1:T(8,128)(2,1)S(1)} %bitcast.278, bf16[1024,2,128]{0,2,1:T(8,128)(2,1)S(1)} %copy-done.52), kind=kOutput, calls=%fused_computation.4 | convolution fusion | flops 566231040 | bytes 26509312 | tf_op jit(solution)/shard_map/qkgd,skd->kgqs/dot_general | solution.py:90
  531.0 8.0 fusion.79
  550.6 25.1 %collective-permute-done.21 = bf16[256,2048]{1,0:T(8,128)(2,1)S(1)} collective-permute-done((bf16[256,2048]{1,0:T(8,128)(2,1)S(1)}, bf16[256,2048]{1,0:T(8,128)(2,1)S(1)}, u32[]{:S(2)}, u32[]{:S(2)}) %collective-permute-start.21) | collective-permute-done | bytes 1048608 | tf_op jit(solution)/shard_map/ppermute | solution.py:218
  580.0 15.4 %collective-permute-done.20 = bf16[256,2048]{1,0:T(8,128)(2,1)S(1)} collective-permute-done((bf16[256,2048]{1,0:T(8,128)(2,1)S(1)}, bf16[256,2048]{1,0:T(8,128)(2,1)S(1)}, u32[]{:S(2)}, u32[]{:S(2)}) %collective-permute-start.20) | collective-permute-done | bytes 1048608 | tf_op jit(solution)/shard_map/ppermute | solution.py:218
  597.2 18.6 %collective-permute-done.22 = bf16[256,2048]{1,0:T(8,128)(2,1)S(1)} collective-permute-done((bf16[256,2048]{1,0:T(8,128)(2,1)S(1)}, bf16[256,2048]{1,0:T(8,128)(2,1)S(1)}, u32[]{:S(2)}, u32[]{:S(2)}) %collective-permute-start.22) | collective-permute-done | bytes 1048608 | tf_op jit(solution)/shard_map/ppermute | solution.py:218
  618.6 7.1 convolution_convert_fusion
  625.6 7.1 collective-permute-done.23
  635.6 5.3 pad_maximum_fusion.1
  641.3 12.2 %convert_bitcast_fusion.1 = bf16[1,2048,2048]{2,1,0:T(8,128)(2,1)S(1)} fusion(bf16[1024,2048]{1,0:T(8,128)(2,1)} %get-tuple-element.85, bf16[1024,2048]{1,0:T(8,128)(2,1)} %get-tuple-element.86), kind=kOutput, calls=%fused_computation.19 | convolution fusion | flops 8594128896 | bytes 16777216 | tf_op jit(solution)/shard_map/dot_general | solution.py:215
  653.6 11.5 %convert_bitcast_fusion = bf16[1,2048,2048]{2,1,0:T(8,128)(2,1)} fusion(bf16[1024,2048]{1,0:T(8,128)(2,1)S(1)} %copy-done.15, bf16[1024,2048]{1,0:T(8,128)(2,1)S(1)} %copy-done.14), kind=kOutput, calls=%fused_computation.18 | convolution fusion | flops 8594128896 | bytes 16777216 | tf_op jit(solution)/shard_map/dot_general | solution.py:215
  665.0 11.6 %convert_bitcast_fusion.2 = bf16[1,2048,2048]{2,1,0:T(8,128)(2,1)} fusion(bf16[1024,2048]{1,0:T(8,128)(2,1)S(1)} %copy-done.16, bf16[1024,2048]{1,0:T(8,128)(2,1)S(1)} %copy-done.13), kind=kOutput, calls=%fused_computation.20 | convolution fusion | flops 8594128896 | bytes 16777216 | tf_op jit(solution)/shard_map/dot_general | solution.py:215
  676.6 14.2 %pad_maximum_fusion = bf16[3,2048,2048]{2,1,0:T(8,128)(2,1)} fusion(bf16[1,2048,2048]{2,1,0:T(8,128)(2,1)S(1)} %copy-done.27, bf16[1,2048,2048]{2,1,0:T(8,128)(2,1)S(1)} %convert_bitcast_fusion.1, bf16[1,2048,2048]{2,1,0:T(8,128)(2,1)} %convert_bitcast_fusion.2), kind=kLoop, calls=%fused_computation | loop fusion | flops 25165824 | bytes 50331648 | tf_op jit(solution)/shard_map/stack | solution.py:329
  692.4 4.0 fusion.23
  696.5 4.9 reduce-scatter.3.cloned.1.call-done
  712.9 148.1 %reduce-scatter.5.cloned.1.call-done = bf16[3,256,2048]{2,1,0:T(8,128)(2,1)} async-done(((bf16[3,2048,2048]{2,1,0:T(8,128)(2,1)}), bf16[3,256,2048]{2,1,0:T(8,128)(2,1)}) %reduce-scatter.5.cloned.1.call-update) | async-done | bytes 3145744 | tf_op jit(solution)/shard_map/reduce_scatter | solution.py:330
  864.2 5.2 copy.65
  (320 shorter events, 107.7 us)
Async XLA Ops:
  7.2 89.1 %all-gather.8.cloned.1.call-start = ((), (), s32[]{:S(2)}) async-start(), calls=%async_computation.2 | async-start | bytes 3538944 | tf_op jit(solution)/shard_map/all_gather | solution.py:252
  10.0 132.4 %all-gather.12.cloned.1.call-start = ((), (), s32[]{:S(2)}) async-start(), calls=%async_computation.6 | async-start | bytes 2359296 | tf_op jit(solution)/shard_map/all_gather | solution.py:254
  10.8 255.6 %all-gather.14.cloned.1.call-start = ((), (), s32[]{:S(2)}) async-start(), calls=%async_computation.7 | async-start | bytes 9437184 | tf_op jit(solution)/shard_map/all_gather | solution.py:258
  11.6 254.8 %all-gather.10.cloned.1.call-start = ((), (), s32[]{:S(2)}) async-start(), calls=%async_computation.3 | async-start | bytes 18874368 | tf_op jit(solution)/shard_map/all_gather | solution.py:255
  13.8 687.5 %reduce-scatter.3.cloned.1.call-start = ((), (), s32[]{:S(2)}) async-start(), calls=%async_computation.4 | async-start | bytes 6488064 | tf_op jit(solution)/shard_map/reduce_scatter | solution.py:397
  13.9 28.3 %collective-permute-start = (bf16[256,2048]{1,0:T(8,128)(2,1)S(1)}, bf16[256,2048]{1,0:T(8,128)(2,1)S(1)}, u32[]{:S(2)}, u32[]{:S(2)}) collective-permute-start(bf16[256,2048]{1,0:T(8,128)(2,1)S(1)} %copy-done.19), channel_id=1, source_target_pairs={{0,1},{1,2},{2,3},{3,0},{4,5},{5,6},{6,7},{7,4},{8,9},{9,10},{10,1... | collective-permute-start | bytes 3145736 | tf_op jit(solution)/shard_map/ppermute | solution.py:218
  29.9 102.0 %copy-start.31 = (pred[512,1024]{0,1:T(8,128)(4,1)}, pred[512,1024]{0,1:T(8,128)(4,1)S(1)}, u32[]{:S(2)}) copy-start(pred[512,1024]{0,1:T(8,128)(4,1)S(1)} %fusion.58) | copy-start | bytes 1572868
  29.9 64.5 %copy-start.59 = (f32[1,1,2048]{2,1,0:T(1,128)}, f32[1,1,2048]{2,1,0:T(1,128)S(1)}, u32[]{:S(2)}) copy-start(f32[1,1,2048]{2,1,0:T(1,128)S(1)} %get-tuple-element.130) | copy-start | bytes 24580
  42.2 26.6 %copy-start.41 = (bf16[256,2048]{1,0:T(8,128)(2,1)}, bf16[256,2048]{1,0:T(8,128)(2,1)S(1)}, u32[]{:S(2)}) copy-start(bf16[256,2048]{1,0:T(8,128)(2,1)S(1)} %collective-permute-done) | copy-start | bytes 3145732
  42.2 26.1 %collective-permute-start.1 = (bf16[256,2048]{1,0:T(8,128)(2,1)S(1)}, bf16[256,2048]{1,0:T(8,128)(2,1)S(1)}, u32[]{:S(2)}, u32[]{:S(2)}) collective-permute-start(bf16[256,2048]{1,0:T(8,128)(2,1)S(1)} %collective-permute-done), channel_id=1, source_target_pairs={{0,1},{1,2},{2,3},{3,0},{4,5},{5,6},{6,7},{7,4},{8,9},{9,10},{10,1... | collective-permute-start | bytes 3145736 | tf_op jit(solution)/shard_map/ppermute | solution.py:218
  68.3 26.0 %copy-start.43 = (bf16[256,2048]{1,0:T(8,128)(2,1)}, bf16[256,2048]{1,0:T(8,128)(2,1)S(1)}, u32[]{:S(2)}) copy-start(bf16[256,2048]{1,0:T(8,128)(2,1)S(1)} %collective-permute-done.1) | copy-start | bytes 3145732
  68.3 25.7 %collective-permute-start.2 = (bf16[256,2048]{1,0:T(8,128)(2,1)S(1)}, bf16[256,2048]{1,0:T(8,128)(2,1)S(1)}, u32[]{:S(2)}, u32[]{:S(2)}) collective-permute-start(bf16[256,2048]{1,0:T(8,128)(2,1)S(1)} %collective-permute-done.1), channel_id=1, source_target_pairs={{0,1},{1,2},{2,3},{3,0},{4,5},{5,6},{6,7},{7,4},{8,9},{9,10},{10,1... | collective-permute-start | bytes 3145736 | tf_op jit(solution)/shard_map/ppermute | solution.py:218
  142.4 30.9 %copy-start.17 = (bf16[1,512,2048]{2,1,0:T(8,128)(2,1)S(1)}, bf16[1,512,2048]{2,1,0:T(8,128)(2,1)}, u32[]{:S(2)}) copy-start(bf16[1,512,2048]{2,1,0:T(8,128)(2,1)} %all-gather.12.cloned.1.call-done) | copy-start | bytes 6291460
  142.4 30.9 %copy-start.37 = (bf16[1024,2,4,64]{0,3,2,1:T(8,128)(2,1)S(1)}, bf16[1024,2,4,64]{0,3,2,1:T(8,128)(2,1)}, u32[]{:S(2)}) copy-start(bf16[1024,2,4,64]{0,3,2,1:T(8,128)(2,1)} %pad_maximum_fusion.4) | copy-start | bytes 3145732
  145.5 27.9 %collective-permute-start.3 = (bf16[256,2048]{1,0:T(8,128)(2,1)S(1)}, bf16[256,2048]{1,0:T(8,128)(2,1)S(1)}, u32[]{:S(2)}, u32[]{:S(2)}) collective-permute-start(bf16[256,2048]{1,0:T(8,128)(2,1)S(1)} %convolution_convert_fusion.2), channel_id=1, source_target_pairs={{0,1},{1,2},{2,3},{3,0},{4,5},{5,6},{6,7},{7,4},{8,9},{9,10},{10,1... | collective-permute-start | bytes 3145736 | tf_op jit(solution)/shard_map/ppermute | solution.py:218
  145.7 50.9 %copy-start.8 = (bf16[256,2048]{1,0:T(8,128)(2,1)}, bf16[256,2048]{1,0:T(8,128)(2,1)S(1)}, u32[]{:S(2)}) copy-start(bf16[256,2048]{1,0:T(8,128)(2,1)S(1)} %convert_element_type.228.refs_1_) | copy-start | bytes 3145732
  145.7 50.1 %collective-permute-start.7 = (bf16[256,2048]{1,0:T(8,128)(2,1)S(1)}, bf16[256,2048]{1,0:T(8,128)(2,1)S(1)}, u32[]{:S(2)}, u32[]{:S(2)}) collective-permute-start(bf16[256,2048]{1,0:T(8,128)(2,1)S(1)} %convert_element_type.228.refs_1_), channel_id=1, source_target_pairs={{0,1},{1,2},{2,3},{3,0},{4,5},{5,6},{6,7},{7,4},{8,9},{9,10},{10,1... | collective-permute-start | bytes 3145736 | tf_op jit(solution)/shard_map/ppermute | solution.py:218
  174.1 44.2 %collective-permute-start.4 = (bf16[256,2048]{1,0:T(8,128)(2,1)S(1)}, bf16[256,2048]{1,0:T(8,128)(2,1)S(1)}, u32[]{:S(2)}, u32[]{:S(2)}) collective-permute-start(bf16[256,2048]{1,0:T(8,128)(2,1)S(1)} %add_convert_fusion.6), channel_id=1, source_target_pairs={{0,1},{1,2},{2,3},{3,0},{4,5},{5,6},{6,7},{7,4},{8,9},{9,10},{10,1... | collective-permute-start | bytes 3145736 | tf_op jit(solution)/shard_map/ppermute | solution.py:218
  195.8 44.9 %collective-permute-start.10 = (bf16[256,2048]{1,0:T(8,128)(2,1)S(1)}, bf16[256,2048]{1,0:T(8,128)(2,1)S(1)}, u32[]{:S(2)}, u32[]{:S(2)}) collective-permute-start(bf16[256,2048]{1,0:T(8,128)(2,1)S(1)} %collective-permute-done.7.refs_1_), channel_id=1, source_target_pairs={{0,1},{1,2},{2,3},{3,0},{4,5},{5,6},{6,7},{7,4},{8,9},{9,10},{10,1... | collective-permute-start | bytes 3145736 | tf_op jit(solution)/shard_map/ppermute | solution.py:218
  218.6 44.6 %collective-permute-start.5 = (bf16[256,2048]{1,0:T(8,128)(2,1)S(1)}, bf16[256,2048]{1,0:T(8,128)(2,1)S(1)}, u32[]{:S(2)}, u32[]{:S(2)}) collective-permute-start(bf16[256,2048]{1,0:T(8,128)(2,1)S(1)} %add_convert_fusion.5), channel_id=1, source_target_pairs={{0,1},{1,2},{2,3},{3,0},{4,5},{5,6},{6,7},{7,4},{8,9},{9,10},{10,1... | collective-permute-start | bytes 3145736 | tf_op jit(solution)/shard_map/ppermute | solution.py:218
  240.7 135.1 %collective-permute-start.13 = (bf16[256,2048]{1,0:T(8,128)(2,1)S(1)}, bf16[256,2048]{1,0:T(8,128)(2,1)}, u32[]{:S(2)}, u32[]{:S(2)}) collective-permute-start(bf16[256,2048]{1,0:T(8,128)(2,1)S(1)} %collective-permute-done.10.refs_1_), channel_id=1, source_target_pairs={{0,1},{1,2},{2,3},{3,0},{4,5},{5,6},{6,7},{7,4},{8,9},{9,10},{10,1... | collective-permute-start | bytes 3145736 | tf_op jit(solution)/shard_map/ppermute | solution.py:218
  266.4 37.8 %collective-permute-start.6 = (bf16[256,2048]{1,0:T(8,128)(2,1)}, bf16[256,2048]{1,0:T(8,128)(2,1)}, u32[]{:S(2)}, u32[]{:S(2)}) collective-permute-start(bf16[256,2048]{1,0:T(8,128)(2,1)} %multiply_convert_fusion.refs_0_), channel_id=1, source_target_pairs={{0,1},{1,2},{2,3},{3,0},{4,5},{5,6},{6,7},{7,4},{8,9},{9,10},{10,1... | collective-permute-start | bytes 3145736 | tf_op jit(solution)/shard_map/ppermute | solution.py:218
  267.6 36.6 %copy-start.7 = (bf16[256,2048]{1,0:T(8,128)(2,1)S(1)}, bf16[256,2048]{1,0:T(8,128)(2,1)}, u32[]{:S(2)}) copy-start(bf16[256,2048]{1,0:T(8,128)(2,1)} %copy-done.6) | copy-start | bytes 3145732
  304.2 24.5 %collective-permute-start.9 = (bf16[256,2048]{1,0:T(8,128)(2,1)}, bf16[256,2048]{1,0:T(8,128)(2,1)S(1)}, u32[]{:S(2)}, u32[]{:S(2)}) collective-permute-start(bf16[256,2048]{1,0:T(8,128)(2,1)} %collective-permute-done.6.refs_0_), channel_id=1, source_target_pairs={{0,1},{1,2},{2,3},{3,0},{4,5},{5,6},{6,7},{7,4},{8,9},{9,10},{10,1... | collective-permute-start | bytes 3145736 | tf_op jit(solution)/shard_map/ppermute | solution.py:218
  325.5 27.9 %collective-permute-start.8 = (bf16[256,2048]{1,0:T(8,128)(2,1)S(1)}, bf16[256,2048]{1,0:T(8,128)(2,1)S(1)}, u32[]{:S(2)}, u32[]{:S(2)}) collective-permute-start(bf16[256,2048]{1,0:T(8,128)(2,1)S(1)} %convert_element_type.229), channel_id=1, source_target_pairs={{0,1},{1,2},{2,3},{3,0},{4,5},{5,6},{6,7},{7,4},{8,9},{9,10},{10,1... | collective-permute-start | bytes 3145736 | tf_op jit(solution)/shard_map/ppermute | solution.py:218
  328.7 47.2 %collective-permute-start.12 = (bf16[256,2048]{1,0:T(8,128)(2,1)S(1)}, bf16[256,2048]{1,0:T(8,128)(2,1)S(1)}, u32[]{:S(2)}, u32[]{:S(2)}) collective-permute-start(bf16[256,2048]{1,0:T(8,128)(2,1)S(1)} %collective-permute-done.9.refs_0_), channel_id=1, source_target_pairs={{0,1},{1,2},{2,3},{3,0},{4,5},{5,6},{6,7},{7,4},{8,9},{9,10},{10,1... | collective-permute-start | bytes 3145736 | tf_op jit(solution)/shard_map/ppermute | solution.py:218
  347.1 28.8 %copy-start.4 = (f32[256,2048]{1,0:T(8,128)}, f32[256,2048]{1,0:T(8,128)S(1)}, u32[]{:S(2)}) copy-start(f32[256,2048]{1,0:T(8,128)S(1)} %get-tuple-element.76) | copy-start | bytes 6291460
  353.7 42.5 %collective-permute-start.11 = (bf16[256,2048]{1,0:T(8,128)(2,1)S(1)}, bf16[256,2048]{1,0:T(8,128)(2,1)S(1)}, u32[]{:S(2)}, u32[]{:S(2)}) collective-permute-start(bf16[256,2048]{1,0:T(8,128)(2,1)S(1)} %add_convert_fusion.4), channel_id=1, source_target_pairs={{0,1},{1,2},{2,3},{3,0},{4,5},{5,6},{6,7},{7,4},{8,9},{9,10},{10,1... | collective-permute-start | bytes 3145736 | tf_op jit(solution)/shard_map/ppermute | solution.py:218
  396.5 22.1 %collective-permute-start.14 = (bf16[256,2048]{1,0:T(8,128)(2,1)S(1)}, bf16[256,2048]{1,0:T(8,128)(2,1)S(1)}, u32[]{:S(2)}, u32[]{:S(2)}) collective-permute-start(bf16[256,2048]{1,0:T(8,128)(2,1)S(1)} %add_convert_fusion.3), channel_id=1, source_target_pairs={{0,1},{1,2},{2,3},{3,0},{4,5},{5,6},{6,7},{7,4},{8,9},{9,10},{10,1... | collective-permute-start | bytes 3145736 | tf_op jit(solution)/shard_map/ppermute | solution.py:218
  423.2 31.5 %copy-start.39 = (bf16[1024,2048]{1,0:T(8,128)(2,1)}, bf16[1024,2048]{1,0:T(8,128)(2,1)S(1)}, u32[]{:S(2)}) copy-start(bf16[1024,2048]{1,0:T(8,128)(2,1)S(1)} %get-tuple-element.108) | copy-start | bytes 12582916
  423.2 46.4 %copy-start.18 = (bf16[1,512,2048]{2,1,0:T(8,128)(2,1)S(1)}, bf16[1,512,2048]{2,1,0:T(8,128)(2,1)}, u32[]{:S(2)}) copy-start(bf16[1,512,2048]{2,1,0:T(8,128)(2,1)} %all-gather.12.cloned.1.call-done) | copy-start | bytes 6291460
  423.2 23.3 %collective-permute-start.15 = (bf16[256,2048]{1,0:T(8,128)(2,1)S(1)}, bf16[256,2048]{1,0:T(8,128)(2,1)S(1)}, u32[]{:S(2)}, u32[]{:S(2)}) collective-permute-start(bf16[256,2048]{1,0:T(8,128)(2,1)S(1)} %get-tuple-element.109), channel_id=1, source_target_pairs={{0,1},{1,2},{2,3},{3,0},{4,5},{5,6},{6,7},{7,4},{8,9},{9,10},{10,1... | collective-permute-start | bytes 3145736 | tf_op jit(solution)/shard_map/ppermute | solution.py:218
  446.6 23.1 %collective-permute-start.16 = (bf16[256,2048]{1,0:T(8,128)(2,1)S(1)}, bf16[256,2048]{1,0:T(8,128)(2,1)}, u32[]{:S(2)}, u32[]{:S(2)}) collective-permute-start(bf16[256,2048]{1,0:T(8,128)(2,1)S(1)} %collective-permute-done.15), channel_id=1, source_target_pairs={{0,1},{1,2},{2,3},{3,0},{4,5},{5,6},{6,7},{7,4},{8,9},{9,10},{10,1... | collective-permute-start | bytes 3145736 | tf_op jit(solution)/shard_map/ppermute | solution.py:218
  469.7 19.8 %collective-permute-start.17 = (bf16[256,2048]{1,0:T(8,128)(2,1)}, bf16[256,2048]{1,0:T(8,128)(2,1)}, u32[]{:S(2)}, u32[]{:S(2)}) collective-permute-start(bf16[256,2048]{1,0:T(8,128)(2,1)} %collective-permute-done.16), channel_id=1, source_target_pairs={{0,1},{1,2},{2,3},{3,0},{4,5},{5,6},{6,7},{7,4},{8,9},{9,10},{10,1... | collective-permute-start | bytes 3145736 | tf_op jit(solution)/shard_map/ppermute | solution.py:218
  498.0 23.0 %collective-permute-start.18 = (bf16[256,2048]{1,0:T(8,128)(2,1)S(1)}, bf16[256,2048]{1,0:T(8,128)(2,1)S(1)}, u32[]{:S(2)}, u32[]{:S(2)}) collective-permute-start(bf16[256,2048]{1,0:T(8,128)(2,1)S(1)} %convert_element_type.236), channel_id=1, source_target_pairs={{0,1},{1,2},{2,3},{3,0},{4,5},{5,6},{6,7},{7,4},{8,9},{9,10},{10,1... | collective-permute-start | bytes 3145736 | tf_op jit(solution)/shard_map/ppermute | solution.py:218
  521.4 22.5 %collective-permute-start.19 = (bf16[256,2048]{1,0:T(8,128)(2,1)S(1)}, bf16[256,2048]{1,0:T(8,128)(2,1)S(1)}, u32[]{:S(2)}, u32[]{:S(2)}) collective-permute-start(bf16[256,2048]{1,0:T(8,128)(2,1)S(1)} %add_convert_fusion.2), channel_id=1, source_target_pairs={{0,1},{1,2},{2,3},{3,0},{4,5},{5,6},{6,7},{7,4},{8,9},{9,10},{10,1... | collective-permute-start | bytes 3145736 | tf_op jit(solution)/shard_map/ppermute | solution.py:218
  547.8 27.9 %copy-start.44 = (bf16[256,2048]{1,0:T(8,128)(2,1)S(1)}, bf16[256,2048]{1,0:T(8,128)(2,1)}, u32[]{:S(2)}) copy-start(bf16[256,2048]{1,0:T(8,128)(2,1)} %copy-done.43) | copy-start | bytes 3145732
  547.8 27.9 %copy-start.71 = (f32[256]{0:T(256)S(1)}, f32[256]{0:T(256)}, u32[]{:S(2)}) copy-start(f32[256]{0:T(256)} %copy-done.70) | copy-start | bytes 3076
  547.8 27.9 %collective-permute-start.21 = (bf16[256,2048]{1,0:T(8,128)(2,1)S(1)}, bf16[256,2048]{1,0:T(8,128)(2,1)S(1)}, u32[]{:S(2)}, u32[]{:S(2)}) collective-permute-start(bf16[256,2048]{1,0:T(8,128)(2,1)S(1)} %get-tuple-element.118), channel_id=1, source_target_pairs={{0,1},{1,2},{2,3},{3,0},{4,5},{5,6},{6,7},{7,4},{8,9},{9,10},{10,1... | collective-permute-start | bytes 3145736 | tf_op jit(solution)/shard_map/ppermute | solution.py:218
  550.5 28.2 %copy-start.22 = (bf16[256,2048]{1,0:T(8,128)(2,1)S(1)}, bf16[256,2048]{1,0:T(8,128)(2,1)}, u32[]{:S(2)}) copy-start(bf16[256,2048]{1,0:T(8,128)(2,1)} %copy-done.21) | copy-start | bytes 3145732
  550.5 28.2 %copy-start.63 = (f32[256]{0:T(256)S(1)}, f32[256]{0:T(256)}, u32[]{:S(2)}) copy-start(f32[256]{0:T(256)} %copy-done.62) | copy-start | bytes 3076
  550.5 44.8 %collective-permute-start.20 = (bf16[256,2048]{1,0:T(8,128)(2,1)S(1)}, bf16[256,2048]{1,0:T(8,128)(2,1)S(1)}, u32[]{:S(2)}, u32[]{:S(2)}) collective-permute-start(bf16[256,2048]{1,0:T(8,128)(2,1)S(1)} %add_convert_fusion.1), channel_id=1, source_target_pairs={{0,1},{1,2},{2,3},{3,0},{4,5},{5,6},{6,7},{7,4},{8,9},{9,10},{10,1... | collective-permute-start | bytes 3145736 | tf_op jit(solution)/shard_map/ppermute | solution.py:218
  577.0 38.8 %collective-permute-start.22 = (bf16[256,2048]{1,0:T(8,128)(2,1)S(1)}, bf16[256,2048]{1,0:T(8,128)(2,1)S(1)}, u32[]{:S(2)}, u32[]{:S(2)}) collective-permute-start(bf16[256,2048]{1,0:T(8,128)(2,1)S(1)} %get-tuple-element.120), channel_id=1, source_target_pairs={{0,1},{1,2},{2,3},{3,0},{4,5},{5,6},{6,7},{7,4},{8,9},{9,10},{10,1... | collective-permute-start | bytes 3145736 | tf_op jit(solution)/shard_map/ppermute | solution.py:218
  616.1 16.6 %collective-permute-start.23 = (bf16[256,2048]{1,0:T(8,128)(2,1)S(1)}, bf16[256,2048]{1,0:T(8,128)(2,1)S(1)}, u32[]{:S(2)}, u32[]{:S(2)}) collective-permute-start(bf16[256,2048]{1,0:T(8,128)(2,1)S(1)} %convert_add_fusion.1), channel_id=1, source_target_pairs={{0,1},{1,2},{2,3},{3,0},{4,5},{5,6},{6,7},{7,4},{8,9},{9,10},{10,1... | collective-permute-start | bytes 3145736 | tf_op jit(solution)/shard_map/ppermute | solution.py:218
  640.9 220.1 %reduce-scatter.5.cloned.1.call-start = ((), (), s32[]{:S(2)}) async-start(), calls=%async_computation.5 | async-start | bytes 28311552 | tf_op jit(solution)/shard_map/reduce_scatter | solution.py:330
  702.1 10.2 %collective-permute-start.24 = (f32[256,2]{0,1:T(2,128)S(1)}, f32[256,2]{0,1:T(2,128)S(1)}, u32[]{:S(2)}, u32[]{:S(2)}) collective-permute-start(f32[256,2]{0,1:T(2,128)S(1)} %slice.189), channel_id=1, source_target_pairs={{0,1},{1,2},{2,3},{3,0},{4,5},{5,6},{6,7},{7,4},{8,9},{9,10},{10,1... | collective-permute-start | bytes 6152 | tf_op jit(solution)/shard_map/ppermute | solution.py:410
  703.6 8.7 collective-permute-start.25
  706.0 6.3 collective-permute-start.26
  (64 other events, 497.2 us)
Sparse Core Ops, SparseCore 0:
  10.4 34.8 all-gather.7
  47.3 28.0 all-gather.11
  77.3 55.8 all-gather.13
  135.5 89.7 all-gather.9
  641.0 60.3 reduce-scatter.2
  704.9 156.0 reduce-scatter.4

commit v4 on v3

--- a/solution.py
+++ b/solution.py
@@ -4,6 +4,7 @@
 import jax.numpy as jnp
 from jax import lax
 from jax.experimental import pallas as pl
+from jax.experimental.layout import Layout, with_layout_constraint
 from jax.experimental.pallas import tpu as pltpu
 from jax.sharding import PartitionSpec as P
 
@@ -109,18 +110,19 @@
 
 
 def mlp_kernel(reused, *refs):
-    x_ref, g_ref, w_gu_ref, w_down_ref = refs[:4]
-    hidden_ref, dgate_ref, dup_ref, x_all_ref, g_all_ref, back_ref, out_ref = refs[4 + reused :]
+    x_ref, g_ref, w_ref = refs[:3]
+    hidden_ref, dgu_ref, x_all_ref, g_all_ref, back_ref, out_ref = refs[3 + reused :]
     first = pl.program_id(0) == 0
     dims = (((1,), (1,)), ((), ()))
     x = x_ref[...]
     g = g_ref[...]
-    w_gate = w_gu_ref[0]
-    w_up = w_gu_ref[1]
-    w_down = w_down_ref[...]
+    w_gate = w_ref[0]
+    w_up = w_ref[1]
+    w_down = w_ref[2]
+    tile = w_down.shape[1]
     gate = jnp.dot(x, w_gate, preferred_element_type=jnp.float32)
     up = jnp.dot(x, w_up, preferred_element_type=jnp.float32)
-    grad_hidden = lax.dot_general(g, w_down, dims, preferred_element_type=jnp.float32)
+    grad_hidden = jnp.dot(g, w_down, preferred_element_type=jnp.float32)
     sigmoid_gate = 1.0 / (1.0 + jnp.exp(-gate))
     silu_gate = gate * sigmoid_gate
     hidden = (silu_gate * up).astype(jnp.bfloat16)
@@ -129,8 +131,8 @@
     )
     dup = (grad_hidden * silu_gate).astype(jnp.bfloat16)
     hidden_ref[...] = hidden
-    dgate_ref[...] = dgate
-    dup_ref[...] = dup
+    dgu_ref[:, :tile] = dgate
+    dgu_ref[:, tile:] = dup
 
     @pl.when(first)
     def _():
@@ -139,37 +141,42 @@
         out_ref[...] = jnp.zeros_like(out_ref)
         back_ref[...] = jnp.zeros_like(back_ref)
 
-    out_ref[...] += jnp.dot(hidden, w_down, preferred_element_type=jnp.float32)
+    out_ref[...] += lax.dot_general(hidden, w_down, dims, preferred_element_type=jnp.float32)
     back_ref[...] += lax.dot_general(
         dgate, w_gate, dims, preferred_element_type=jnp.float32
     ) + lax.dot_general(dup, w_up, dims, preferred_element_type=jnp.float32)
 
 
-def mlp_block(step, ring, x, g, w_gu, w_down, kept):
+def mlp_tile(hidden_width):
+    return min(512, hidden_width)
+
+
+def mlp_block(step, ring, x, g, w_mlp, kept):
     rows, width = x.shape
-    hidden_width = w_down.shape[0]
-    tile = min(512, hidden_width)
+    hidden_width = w_mlp.shape[2]
+    tile = mlp_tile(hidden_width)
     bf16, f32 = jnp.bfloat16, jnp.float32
     wide = jax.ShapeDtypeStruct((ring * rows, hidden_width), bf16)
+    pair = jax.ShapeDtypeStruct((ring * rows, 2 * hidden_width), bf16)
     whole = jax.ShapeDtypeStruct((ring * rows, width), bf16)
     part = jax.ShapeDtypeStruct((rows, width), f32)
     wide_spec = pl.BlockSpec((rows, tile), lambda t: (step, t))
+    pair_spec = pl.BlockSpec((rows, 2 * tile), lambda t: (step, t))
     whole_spec = pl.BlockSpec((rows, width), lambda t: (step, 0))
     block_spec = pl.BlockSpec((rows, width), lambda t: (0, 0))
     reused = len(kept)
     return pl.pallas_call(
         functools.partial(mlp_kernel, reused),
         grid=(hidden_width // tile,),
-        out_shape=(wide, wide, wide, whole, whole, part, part),
+        out_shape=(wide, pair, whole, whole, part, part),
         in_specs=[
             block_spec,
             block_spec,
-            pl.BlockSpec((2, width, tile), lambda t: (0, 0, t)),
-            pl.BlockSpec((tile, width), lambda t: (t, 0)),
+            pl.BlockSpec((3, width, tile), lambda t: (0, 0, t)),
         ]
         + [pl.BlockSpec(memory_space=pl.ANY)] * reused,
-        out_specs=(wide_spec, wide_spec, wide_spec, whole_spec, whole_spec, block_spec, block_spec),
-        input_output_aliases={4 + i: i for i in range(reused)},
+        out_specs=(wide_spec, pair_spec, whole_spec, whole_spec, block_spec, block_spec),
+        input_output_aliases={3 + i: i for i in range(reused)},
         cost_estimate=pl.CostEstimate(
             flops=12 * rows * width * hidden_width,
             bytes_accessed=6 * width * hidden_width + 12 * rows * width,
@@ -177,7 +184,7 @@
         ),
         compiler_params=pltpu.CompilerParams(vmem_limit_bytes=44 << 20),
         name="mlp_block",
-    )(x, g, w_gu, w_down, *kept)
+    )(x, g, w_mlp, *kept)
 
 
 def per_device(
@@ -205,6 +212,9 @@
     block_rows = min(512, row_count)
     score_scale = head_size ** (-0.5)
 
+    def row_major(array):
+        return with_layout_constraint(array, Layout(tuple(range(array.ndim))))
+
     def dot(a, b):
         return jnp.dot(a, b, preferred_element_type=f32)
 
@@ -229,33 +239,52 @@
             blocks.append(shift(blocks[-1]))
         return blocks
 
+    halves = 2
+    half_rows = local_rows // halves
+
+    def split(rows):
+        return [rows[half * half_rows : (half + 1) * half_rows] for half in range(halves)]
+
+    def spread_halves(rows):
+        pieces = lax.optimization_barrier(split(rows))
+        chains = [spread(piece) for piece in pieces]
+        return [[chain[step] for chain in chains] for step in range(ring)]
+
     def in_order(blocks):
-        whole = jnp.zeros((ring * local_rows,) + blocks[0].shape[1:], blocks[0].dtype)
-        for step, block in enumerate(blocks):
-            whole = lax.dynamic_update_slice_in_dim(whole, block, block_start_of(step), 0)
+        first = blocks[0][0]
+        whole = jnp.zeros((ring * local_rows,) + first.shape[1:], first.dtype)
+        for step, pieces in enumerate(blocks):
+            for half, piece in enumerate(pieces):
+                whole = lax.dynamic_update_slice_in_dim(
+                    whole, piece, block_start_of(step) + half * half_rows, 0
+                )
         return whole
 
-    def rows_of(whole, step):
-        return lax.dynamic_slice_in_dim(whole, block_start_of(step), local_rows, 0)
-
-    def collect(parts, last_gate=None):
+    def halves_of(whole, step):
+        return [
+            lax.dynamic_slice_in_dim(whole, block_start_of(step) + half * half_rows, half_rows, 0)
+            for half in range(halves)
+        ]
+
+    def collect(parts):
         total = parts[1 % ring].astype(f32)
         for step in range(2, ring + 1):
-            if step == ring and last_gate is not None:
-                total = after(total, last_gate)
             total = shift(total.astype(bf16)).astype(f32) + parts[step % ring]
         return total
 
-    w_qkv_local = jnp.concatenate(
-        [w_query[0], w_keyval[0].reshape(w_keyval.shape[1], -1)], axis=1
-    )
-    w_qkv = lax.all_gather(w_qkv_local, "fsdp", axis=0, tiled=True)
+    def collect_halves(parts):
+        return jnp.concatenate(
+            [collect([pieces[half] for pieces in parts]) for half in range(halves)],
+            axis=0,
+        )
+
+    w_qkv_local = jnp.concatenate([w_query[0], w_keyval[0].reshape(w_keyval.shape[1], -1)], axis=1)
+    w_qkv_local = row_major(w_qkv_local)
+    w_mlp_local = jnp.stack([w_gate_up[0, :, 0], w_gate_up[0, :, 1], jnp.swapaxes(w_down[0], 0, 1)])
+    w_qkv = row_major(lax.all_gather(w_qkv_local, "fsdp", axis=0, tiled=True))
     gains_all = lax.all_gather(norm_gains[0], "fsdp", axis=1, tiled=True)
     w_out_all = lax.all_gather(w_attn_out[0], "fsdp", axis=1, tiled=True)
-    w_gu_all = lax.all_gather(
-        jnp.swapaxes(w_gate_up[0], 0, 1), "fsdp", axis=1, tiled=True
-    )
-    w_down_all = lax.all_gather(w_down[0], "fsdp", axis=1, tiled=True)
+    w_mlp = lax.all_gather(w_mlp_local, "fsdp", axis=1, tiled=True)
 
     cosine, sine_table = rope_tables(doc_row, head_size)
     block_starts = list(range(0, row_count, block_rows))
@@ -267,12 +296,14 @@
         for index, start in enumerate(block_starts)
     ]
 
-    input_blocks = spread(block_input)
+    input_blocks = spread_halves(block_input)
     grad_blocks = spread(after(out_cotangent.astype(bf16), input_blocks[-1]))
-    normed_pairs = [norm_apply(block.astype(f32), gains_all[0]) for block in input_blocks]
+    normed_pairs = [
+        [norm_apply(piece.astype(f32), gains_all[0]) for piece in pieces] for pieces in input_blocks
+    ]
     residual = block_input.astype(f32)
-    inv_attn = normed_pairs[0][0]
-    normed_all = in_order([pair[1] for pair in normed_pairs])
+    inv_attn = norm_apply(residual, gains_all[0])[0]
+    normed_all = in_order([[pair[1] for pair in pairs] for pairs in normed_pairs])
     qkv = dot(normed_all, w_qkv)
     query_rows = rotate(
         qkv[:, :query_width].reshape(row_count, kv_local, group_size, head_size),
@@ -300,7 +331,9 @@
         out_list.append(out_block)
         total_list.append(log_total)
     attended = jnp.concatenate(out_list, axis=0).reshape(row_count, -1)
-    middle = residual + collect([dot(rows_of(attended, step), w_out_all) for step in range(ring)])
+    middle = residual + collect_halves(
+        [[dot(piece, w_out_all) for piece in halves_of(attended, step)] for step in range(ring)],
+    )
     inv_mlp, normed_mlp = norm_apply(middle, gains_all[1])
 
     normed_mlp_blocks = [normed_mlp]
@@ -315,27 +348,27 @@
         if step > 0:
             rows = after(rows, back_parts[step - 1])
         *kept, back_part, out_part = mlp_block(
-            step, ring, rows, grad_blocks[step], w_gu_all, w_down_all, tuple(kept)
+            step, ring, rows, grad_blocks[step], w_mlp, tuple(kept)
         )
         back_parts.append(back_part)
         out_parts.append(out_part)
-    hidden_all, dgate_all, dup_all, normed_mlp_all, grad_all = kept
+    hidden_all, dgu_all, normed_mlp_all, grad_all = kept
     grad_normed_mlp = collect(back_parts)
-    weight_grads = []
-    for left, right in (
-        (grad_all, hidden_all), (normed_mlp_all, dgate_all), (normed_mlp_all, dup_all)
-    ):
-        weight_grads.append(dot_tn(left, right).astype(bf16))
-    grad_mlp = jnp.stack(weight_grads)
-    grad_mlp = lax.psum_scatter(grad_mlp, "fsdp", scatter_dimension=1, tiled=True)
-    grad_mlp = grad_mlp.astype(f32)
-    grad_down = jnp.swapaxes(grad_mlp[0], 0, 1)
-    grad_wgu = jnp.swapaxes(grad_mlp[1:], 0, 1)
+    grad_down = dot_tn(grad_all, hidden_all).astype(bf16)
+    grad_wgu = dot_tn(normed_mlp_all, dgu_all).astype(bf16)
+    grad_down = lax.psum_scatter(grad_down, "fsdp", scatter_dimension=0, tiled=True)
+    grad_wgu = lax.psum_scatter(grad_wgu, "fsdp", scatter_dimension=0, tiled=True)
+    grad_down = jnp.swapaxes(grad_down.astype(f32), 0, 1)
+    tile = mlp_tile(w_mlp.shape[2])
+    grad_wgu = grad_wgu.astype(f32).reshape(grad_wgu.shape[0], -1, 2, tile)
+    grad_wgu = jnp.swapaxes(grad_wgu, 1, 2).reshape(grad_wgu.shape[0], 2, -1)
     norm_part, grad_gain_mlp = norm_back(middle, inv_mlp, gains_all[1], grad_normed_mlp)
     grad_middle = out_cotangent + norm_part
 
-    middle_blocks = spread(grad_middle.astype(bf16))
-    do_parts = [dot_nt(block, w_out_all).astype(bf16) for block in middle_blocks]
+    middle_blocks = spread_halves(grad_middle.astype(bf16))
+    do_parts = [
+        [dot_nt(piece, w_out_all).astype(bf16) for piece in pieces] for pieces in middle_blocks
+    ]
     grad_attended = in_order(do_parts).reshape(row_count, kv_local, group_size, head_size)
     middle_all = in_order(middle_blocks)
 
@@ -382,16 +415,16 @@
     )
     grad_qkv = jnp.concatenate([grad_query, grad_keyval], axis=1)
     grad_qkv = after(grad_qkv, out_totals[-2])
-    in_parts = [dot_nt(rows_of(grad_qkv, step), w_qkv) for step in range(ring)]
-    grad_normed = collect(in_parts, output_rows)
+    in_parts = [
+        [dot_nt(piece, w_qkv) for piece in halves_of(grad_qkv, step)] for step in range(ring)
+    ]
+    grad_normed = collect_halves(in_parts)
     norm_part, _ = norm_back(residual, inv_attn, gains_all[0], grad_normed)
     grad_rows = grad_middle + norm_part
 
-    grad_gain_attn = sum(
-        jnp.sum(part * block.astype(f32) * pair[0], axis=0)
-        for part, block, pair in zip(in_parts, input_blocks, normed_pairs)
-    )
-    grad_wqkv = dot_tn(normed_all, grad_qkv).astype(bf16)
+    grad_wqkv = dot_tn(normed_all, grad_qkv)
+    grad_gain_attn = jnp.sum(grad_wqkv * w_qkv.astype(f32), axis=1) / gains_all[0].astype(f32)
+    grad_wqkv = grad_wqkv.astype(bf16)
     gain_columns = jnp.stack([grad_gain_attn, grad_gain_mlp], axis=1).astype(bf16)
     gain_columns = jnp.pad(gain_columns, ((0, 0), (0, 126)))
     packed = lax.psum_scatter(

time: 883 us -> 765 us (0.87)
  waiting for transfers between devices: 523 us -> 350 us
  local copies, waits for them, and re-layouts: 47.5 us -> 72.4 us
  matrix products: 132 us -> 150 us
    reduce_scatter x1 -> x2, waiting for transfers between devices: 148 us -> 58.4 us  [the longest x1 58.4 us: per_device(): lax.psum_scatter(grad_wgu, 'fsdp', scatter_dimension=0, tiled=True)]
    ppermute x24 -> x36, waiting for transfers between devices: 368 us -> 291 us  [shift(): return lax.ppermute(rows, 'tensor', ring_pairs)]
    another operation x9, other arithmetic: 15.4 us -> 3.29 us  [the longest x1 2.08 us: per_device(): jnp.stack([w_gate_up[0, :, 0], w_gate_up[0, :, 1], jnp.swapaxes(w_down[0]...]
    dot_general x8 -> x16, matrix products: 16.1 us -> 27.7 us  [dot_nt(): lax.dot_general(a, b, (((1,), (1,)), ((), ())), preferred_element_type=f32)]
    ppermute x24 -> x36, starting transfers between devices: 4.55 us -> 14 us  [shift(): return lax.ppermute(rows, 'tensor', ring_pairs)]
    dot_general x5 -> x4, matrix products: 44.6 us -> 49.7 us  [dot_tn(): lax.dot_general(a, b, (((0,), (0,)), ((), ())), preferred_element_type=f32)]
    unnamed x160 -> x145, local copies, waits for them, and re-layouts: 27.5 us -> 26.7 us
  transfers between devices with their start and end apart: 33 -> 45, of which waited for: 23 -> 32; matrix products, arithmetic and copies ran while one was open for 21% -> 34% of each run, Pallas kernels for 9% -> 10%
where the time goes in v4:
time: 765 us; the launch traced here: 757 us
  waiting for transfers between devices  350 us (46%)
  matrix products  150 us (20%)
  Pallas kernels  74.7 us (10%)
  local copies, waits for them, and re-layouts  72.4 us (9%)
  other arithmetic  66 us (9%)
  starting transfers between devices  18.7 us (2%)
  between operations  16.2 us (2%)
  blocking collectives  8.94 us (1%)
    ppermute x36, waiting for transfers between devices, shift(): return lax.ppermute(rows, 'tensor', ring_pairs)  291 us
    pallas_call x4, Pallas kernels, mlp_block(): pl.pallas_call(functools.partial(mlp_kernel, reused), grid=(hidden_width...  74.7 us
    reduce_scatter x1, waiting for transfers between devices, per_device(): lax.psum_scatter(grad_wgu, 'fsdp', scatter_dimension=0, tiled=True)  58.4 us
    dot_general x4, matrix products, dot_tn(): lax.dot_general(a, b, (((0,), (0,)), ((), ())), preferred_element_type=f32)  49.7 us
    dot_general x16, matrix products, dot_nt(): lax.dot_general(a, b, (((1,), (1,)), ((), ())), preferred_element_type=f32)  27.7 us
    unnamed x145, local copies, waits for them, and re-layouts  26.7 us
  transfers between devices with their start and end apart: 45, of which 32 were waited for; matrix products, arithmetic and copies ran while one was open for 34% of the time, Pallas kernels for 10%

profile of v4, /device:TPU:0, one launch (start us, length us, event | category | flops | bytes accessed | tf_op | source)
XLA Modules:
  0.0 756.6 jit_solution(9852795600453256728)
XLA Ops:
  26.1 8.9 %all-gather = bf16[1,2,2048]{2,1,0:T(2,128)(2,1)S(1)} all-gather(bf16[1,2,256]{2,1,0:T(2,128)(2,1)S(1)} %copy-done.67), channel_id=2, replica_groups=mesh['fsdp'=8,'tensor'=4] {'fsdp'}, dimensions={2}, use_global_device_ids=true | all-gather | bytes 9216 | tf_op jit(solution)/shard_map/all_gather | solution.py:285
  56.0 7.6 collective-permute-done.2
  63.5 11.2 %collective-permute-done.3 = bf16[128,2048]{1,0:T(8,128)(2,1)S(1)} collective-permute-done((bf16[128,2048]{1,0:T(8,128)(2,1)}, bf16[128,2048]{1,0:T(8,128)(2,1)S(1)}, u32[]{:S(2)}, u32[]{:S(2)}) %collective-permute-start.3) | collective-permute-done | bytes 524320 | tf_op jit(solution)/shard_map/ppermute | solution.py:228
  76.1 9.9 %collective-permute-done.4 = bf16[128,2048]{1,0:T(8,128)(2,1)S(1)} collective-permute-done((bf16[128,2048]{1,0:T(8,128)(2,1)S(1)}, bf16[128,2048]{1,0:T(8,128)(2,1)S(1)}, u32[]{:S(2)}, u32[]{:S(2)}) %collective-permute-start.4) | collective-permute-done | bytes 524320 | tf_op jit(solution)/shard_map/ppermute | solution.py:228
  86.0 10.6 %collective-permute-done.5 = bf16[128,2048]{1,0:T(8,128)(2,1)S(1)} collective-permute-done((bf16[128,2048]{1,0:T(8,128)(2,1)S(1)}, bf16[128,2048]{1,0:T(8,128)(2,1)S(1)}, u32[]{:S(2)}, u32[]{:S(2)}) %collective-permute-start.5) | collective-permute-done | bytes 524320 | tf_op jit(solution)/shard_map/ppermute | solution.py:228
  97.9 24.9 %collective-permute-done.13.refs_1_ = bf16[256,2048]{1,0:T(8,128)(2,1)S(1)} collective-permute-done((bf16[256,2048]{1,0:T(8,128)(2,1)S(1)}, bf16[256,2048]{1,0:T(8,128)(2,1)S(1)}, u32[]{:S(2)}, u32[]{:S(2)}) %collective-permute-start.13) | collective-permute-done | bytes 1048608 | tf_op jit(solution)/shard_map/ppermute | solution.py:228
  125.8 22.6 %collective-permute-done.16.refs_1_ = bf16[256,2048]{1,0:T(8,128)(2,1)} collective-permute-done((bf16[256,2048]{1,0:T(8,128)(2,1)S(1)}, bf16[256,2048]{1,0:T(8,128)(2,1)}, u32[]{:S(2)}, u32[]{:S(2)}) %collective-permute-start.16) | collective-permute-done | bytes 1048608 | tf_op jit(solution)/shard_map/ppermute | solution.py:228
  148.6 6.6 fusion.219
  167.1 7.4 fusion.5
  174.4 9.3 %exponential_reduce_fusion = f32[2,4,512]{2,1,0:T(4,128)S(1)} fusion(f32[2,1024,512,4]{2,1,3,0:T(8,128)} %get-tuple-element.138, f32[2,4,512]{2,1,0:T(4,128)S(1)} %get-tuple-element.137, pred[512,1024]{0,1:T(8,128)(4,1)S(1)} %fusion.54), kind=kLoop, calls=%fused_computation.9 | loop fusion | flops 16773120 | bytes 17334272 | tf_op jit(solution)/shard_map/reduce_sum | solution.py:73
  183.8 10.1 %fusion.55 = bf16[2,64,4,512]{3,1,2,0:T(8,128)(2,1)S(1)} fusion(f32[2,1024,512,4]{2,1,3,0:T(8,128)} %get-tuple-element.138, f32[2,4,512]{2,1,0:T(4,128)S(1)} %bitcast.340, pred[512,1024]{0,1:T(8,128)(4,1)S(1)} %fusion.54, bf16[1024,2,64]{0,2,1:T(8,128)(2,1)} %slice.197), kind=kOutput, calls=%fused_computation.112 | convolution fusion | flops 553910272 | bytes 18104320 | tf_op jit(solution)/shard_map/kgqs,skd->qkgd/dot_general | solution.py:75
  200.2 8.2 %fusion.134 = f32[2,1024,512,4]{2,1,3,0:T(8,128)} fusion(bf16[512,2,4,64]{0,3,2,1:T(8,128)(2,1)S(1)} %pad_maximum_fusion.6, bf16[1024,2,32]{0,2,1:T(8,128)(2,1)S(1)} %get-tuple-element.119, bf16[1024,2,32]{0,2,1:T(8,128)(2,1)S(1)} %get-tuple-element.118), kind=kOutput, calls=%fused_computation.208 | convolution fusion | flops 537395200 | bytes 17563648 | tf_op jit(solution)/shard_map/qkgd,skd->kgqs/dot_general | solution.py:85
  209.3 5.4 collective-permute-done.6
  215.7 10.3 %collective-permute-done.9 = bf16[128,2048]{1,0:T(8,128)(2,1)S(1)} collective-permute-done((bf16[128,2048]{1,0:T(8,128)(2,1)S(1)}, bf16[128,2048]{1,0:T(8,128)(2,1)S(1)}, u32[]{:S(2)}, u32[]{:S(2)}) %collective-permute-start.9) | collective-permute-done | bytes 524320 | tf_op jit(solution)/shard_map/ppermute | solution.py:228
  227.0 10.2 %collective-permute-done.7 = bf16[128,2048]{1,0:T(8,128)(2,1)S(1)} collective-permute-done((bf16[128,2048]{1,0:T(8,128)(2,1)S(1)}, bf16[128,2048]{1,0:T(8,128)(2,1)S(1)}, u32[]{:S(2)}, u32[]{:S(2)}) %collective-permute-start.7) | collective-permute-done | bytes 524320 | tf_op jit(solution)/shard_map/ppermute | solution.py:228
  237.4 11.1 %collective-permute-done.10 = bf16[128,2048]{1,0:T(8,128)(2,1)S(1)} collective-permute-done((bf16[128,2048]{1,0:T(8,128)(2,1)S(1)}, bf16[128,2048]{1,0:T(8,128)(2,1)S(1)}, u32[]{:S(2)}, u32[]{:S(2)}) %collective-permute-start.10) | collective-permute-done | bytes 524320 | tf_op jit(solution)/shard_map/ppermute | solution.py:228
  249.1 10.5 %collective-permute-done.8 = bf16[128,2048]{1,0:T(8,128)(2,1)S(1)} collective-permute-done((bf16[128,2048]{1,0:T(8,128)(2,1)S(1)}, bf16[128,2048]{1,0:T(8,128)(2,1)S(1)}, u32[]{:S(2)}, u32[]{:S(2)}) %collective-permute-start.8) | collective-permute-done | bytes 524320 | tf_op jit(solution)/shard_map/ppermute | solution.py:228
  259.8 7.9 %collective-permute-done.11 = bf16[128,2048]{1,0:T(8,128)(2,1)S(1)} collective-permute-done((bf16[128,2048]{1,0:T(8,128)(2,1)S(1)}, bf16[128,2048]{1,0:T(8,128)(2,1)S(1)}, u32[]{:S(2)}, u32[]{:S(2)}) %collective-permute-start.11) | collective-permute-done | bytes 524320 | tf_op jit(solution)/shard_map/ppermute | solution.py:228
  270.7 18.7 %mlp_block.4 = (bf16[1024,2048]{1,0:T(8,128)(2,1)}, bf16[1024,4096]{1,0:T(8,128)(2,1)}, bf16[1024,2048]{1,0:T(8,128)(2,1)}, bf16[1024,2048]{1,0:T(8,128)(2,1)}, ...) custom-call(bf16[256,2048]{1,0:T(8,128)(2,1)} %multiply_convert_fusion.refs_0_, ...), custom_call_target="tpu_custom_call" | custom-call | flops 12884901888 | bytes 31457280 | tf_op jit(solution)/shard_map/mlp_block/pallas_call | solution.py:168
  290.7 4.0 collective-permute-done.12.refs_0_
  296.0 18.7 %mlp_block.5 = (bf16[1024,2048]{1,0:T(8,128)(2,1)}, bf16[1024,4096]{1,0:T(8,128)(2,1)}, bf16[1024,2048]{1,0:T(8,128)(2,1)}, bf16[1024,2048]{1,0:T(8,128)(2,1)}, ...) custom-call(bf16[256,2048]{1,0:T(8,128)(2,1)} %collective-permute-do, ...), custom_call_target="tpu_custom_call", output_to_operand_aliasing={{0}: (3, {}), {1}: (4, {}), {2}: (5, {}), {3}: (6, {})} | custom-call | flops 12884901888 | bytes 31457280 | tf_op jit(solution)/shard_map/mlp_block/pallas_call | solution.py:168
  319.2 18.7 %mlp_block.6 = (bf16[1024,2048]{1,0:T(8,128)(2,1)}, bf16[1024,4096]{1,0:T(8,128)(2,1)}, bf16[1024,2048]{1,0:T(8,128)(2,1)}, bf16[1024,2048]{1,0:T(8,128)(2,1)}, ...) custom-call(bf16[256,2048]{1,0:T(8,128)(2,1)S(1)} %collective-permut, ...), custom_call_target="tpu_custom_call", output_to_operand_aliasing={{0}: (3, {}), {1}: (4, {}), {2}: (5, {}), {3}: (6, {})} | custom-call | flops 12884901888 | bytes 31457280 | tf_op jit(solution)/shard_map/mlp_block/pallas_call | solution.py:168
  337.9 6.2 collective-permute-done.14
  344.4 22.1 %collective-permute-done.18.refs_0_ = bf16[256,2048]{1,0:T(8,128)(2,1)S(1)} collective-permute-done((bf16[256,2048]{1,0:T(8,128)(2,1)S(1)}, bf16[256,2048]{1,0:T(8,128)(2,1)S(1)}, u32[]{:S(2)}, u32[]{:S(2)}) %collective-permute-start.18) | collective-permute-done | bytes 1048608 | tf_op jit(solution)/shard_map/ppermute | solution.py:228
  366.6 18.7 %mlp_block.7 = (bf16[1024,2048]{1,0:T(8,128)(2,1)}, bf16[1024,4096]{1,0:T(8,128)(2,1)}, bf16[1024,2048]{1,0:T(8,128)(2,1)}, bf16[1024,2048]{1,0:T(8,128)(2,1)}, ...) custom-call(bf16[256,2048]{1,0:T(8,128)(2,1)S(1)} %collective-permut, ...), custom_call_target="tpu_custom_call", output_to_operand_aliasing={{0}: (3, {}), {1}: (4, {}), {2}: (5, {}), {3}: (6, {})} | custom-call | flops 12884901888 | bytes 31457280 | tf_op jit(solution)/shard_map/mlp_block/pallas_call | solution.py:168
  389.1 13.5 %convolution_convert_fusion.1 = bf16[2048,2048]{1,0:T(8,128)(2,1)} fusion(bf16[1024,2048]{1,0:T(8,128)(2,1)} %get-tuple-element.84, bf16[1024,2048]{1,0:T(8,128)(2,1)S(1)} %copy-done.17), kind=kOutput, calls=%fused_computation.24 | convolution fusion | flops 8594128896 | bytes 16777216 | tf_op jit(solution)/shard_map/dot_general | solution.py:225
  403.2 6.8 collective-permute-done.20
  423.8 6.4 collective-permute-done.21
  432.2 3.6 collective-permute-done.24
  443.0 9.8 %collective-permute-done.22 = bf16[128,2048]{1,0:T(8,128)(2,1)S(1)} collective-permute-done((bf16[128,2048]{1,0:T(8,128)(2,1)}, bf16[128,2048]{1,0:T(8,128)(2,1)S(1)}, u32[]{:S(2)}, u32[]{:S(2)}) %collective-permute-start.22) | collective-permute-done | bytes 524320 | tf_op jit(solution)/shard_map/ppermute | solution.py:228
  466.2 9.4 %collective-permute-done.23 = bf16[128,2048]{1,0:T(8,128)(2,1)S(1)} collective-permute-done((bf16[128,2048]{1,0:T(8,128)(2,1)}, bf16[128,2048]{1,0:T(8,128)(2,1)S(1)}, u32[]{:S(2)}, u32[]{:S(2)}) %collective-permute-start.23) | collective-permute-done | bytes 524320 | tf_op jit(solution)/shard_map/ppermute | solution.py:228
  490.5 3.7 convolution_convert_fusion.2
  502.0 7.2 collective-permute-done.27
  510.0 9.3 %fusion.2 = bf16[2,4,512,1024]{2,3,1,0:T(8,128)(2,1)S(1)} fusion(f32[2,1024,512,4]{2,1,3,0:T(8,128)} %fusion.134, f32[2,4,512]{2,1,0:T(4,128)S(1)} %fusion.117, f32[2,4,512]{2,1,0:T(4,128)S(1)} %bitcast.341, pred[512,1024]{0,1:T(8,128)(4,1)S(1)} %copy-done.28, bf16[512,2,4,64]{0,3,2,1:T(8,128)(2,1)S(1)} %bitcast.310, bf16[1024,2,128]{0,2,1:T(8,128)(2,1)S(1)} %copy-done.51), kind=kOutput, calls=%fused_computation.3 | convolution fusion | flops 566231040 | bytes 26509312 | tf_op jit(solution)/shard_map/qkgd,skd->kgqs/dot_general | solution.py:91
  522.1 8.0 %fusion.63 = bf16[1024,2,64]{0,2,1:T(8,128)(2,1)S(1)} fusion(bf16[512,2,4,64]{0,3,2,1:T(8,128)(2,1)S(1)} %bitcast.311, f32[2,1024,512,4]{2,1,3,0:T(8,128)} %fusion.134, f32[2,4,512]{2,1,0:T(4,128)S(1)} %bitcast.342, pred[512,1024]{0,1:T(8,128)(4,1)S(1)} %copy-done.28, f32[512,2,64]{0,2,1:T(8,128)S(1)} %convolution_bitcast_fusion.3), kind=kOutput, calls=%fused_computation.118 | convolution fusion | flops 553910272 | bytes 18366464 | tf_op jit(solution)/shard_map/kgqs,qkgd->skd/dot_general | solution.py:103
  535.5 7.9 %fusion.218 = (bf16[2048,768]{0,1:T(8,128)(2,1)}, f32[2048,768]{0,1:T(8,128)}) fusion(bf16[1024,768]{0,1:T(8,128)(2,1)S(1)} %pad_maximum_fusion.2, bf16[1024,2048]{1,0:T(8,128)(2,1)} %fusion.121), kind=kOutput, calls=%fused_computation.315 | convolution fusion | flops 3222798336 | bytes 15204352 | tf_op jit(solution)/shard_map/dot_general | solution.py:225
  543.4 6.8 copy.73
  550.2 3.5 multiply_reduce_fusion
  553.8 6.1 pad_maximum_fusion
  560.2 24.6 %convolution_convert_fusion = bf16[2048,4096]{1,0:T(8,128)(2,1)} fusion(bf16[1024,2048]{1,0:T(8,128)(2,1)} %get-tuple-element.82, bf16[1024,4096]{1,0:T(8,128)(2,1)} %get-tuple-element.83), kind=kOutput, calls=%fused_computation.10 | convolution fusion | flops 17188257792 | bytes 29360128 | tf_op jit(solution)/shard_map/dot_general | solution.py:225
  589.0 4.3 collective-permute-start.29
  593.3 10.4 %collective-permute-done.30 = bf16[128,2048]{1,0:T(8,128)(2,1)S(1)} collective-permute-done((bf16[128,2048]{1,0:T(8,128)(2,1)S(1)}, bf16[128,2048]{1,0:T(8,128)(2,1)S(1)}, u32[]{:S(2)}, u32[]{:S(2)}) %collective-permute-start.30) | collective-permute-done | bytes 524320 | tf_op jit(solution)/shard_map/ppermute | solution.py:228
  605.0 10.0 %collective-permute-done.33 = bf16[128,2048]{1,0:T(8,128)(2,1)S(1)} collective-permute-done((bf16[128,2048]{1,0:T(8,128)(2,1)S(1)}, bf16[128,2048]{1,0:T(8,128)(2,1)S(1)}, u32[]{:S(2)}, u32[]{:S(2)}) %collective-permute-start.33) | collective-permute-done | bytes 524320 | tf_op jit(solution)/shard_map/ppermute | solution.py:228
  616.5 32.2 %collective-permute-done.31 = bf16[128,2048]{1,0:T(8,128)(2,1)S(1)} collective-permute-done((bf16[128,2048]{1,0:T(8,128)(2,1)S(1)}, bf16[128,2048]{1,0:T(8,128)(2,1)S(1)}, u32[]{:S(2)}, u32[]{:S(2)}) %collective-permute-start.31) | collective-permute-done | bytes 524320 | tf_op jit(solution)/shard_map/ppermute | solution.py:228
  650.0 5.2 collective-permute-done.34
  662.1 5.3 collective-permute-done.35
  684.4 58.4 %reduce-scatter.6.cloned.1.call-done = bf16[256,4096]{1,0:T(8,128)(2,1)} async-done(((bf16[2048,4096]{1,0:T(8,128)(2,1)}), bf16[256,4096]{1,0:T(8,128)(2,1)}) %reduce-scatter.6.cloned.1.call-update) | async-done | bytes 2097168 | tf_op jit(solution)/shard_map/reduce_scatter | solution.py:360
  742.8 6.6 reshape.474
  (371 shorter events, 181.8 us)
Async XLA Ops:
  7.2 141.4 %all-gather.6.cloned.1.call-start = ((), (), s32[]{:S(2)}) async-start(), calls=%async_computation.3 | async-start | bytes 3538944 | tf_op jit(solution)/shard_map/all_gather | solution.py:284
  10.0 185.8 %all-gather.10.cloned.1.call-start = ((), (), s32[]{:S(2)}) async-start(), calls=%async_computation.8 | async-start | bytes 2359296 | tf_op jit(solution)/shard_map/all_gather | solution.py:286
  10.8 259.9 %all-gather.8.cloned.1.call-start = ((), (), s32[]{:S(2)}) async-start(), calls=%async_computation.4 | async-start | bytes 28311552 | tf_op jit(solution)/shard_map/all_gather | solution.py:287
  18.7 652.5 %reduce-scatter.8.cloned.1.call-start = ((), (), s32[]{:S(2)}) async-start(), calls=%async_computation.7 | async-start | bytes 9437184 | tf_op jit(solution)/shard_map/reduce_scatter | solution.py:359
  20.8 25.9 %collective-permute-start = (bf16[128,2048]{1,0:T(8,128)(2,1)}, bf16[128,2048]{1,0:T(8,128)(2,1)}, u32[]{:S(2)}, u32[]{:S(2)}) collective-permute-start(bf16[128,2048]{1,0:T(8,128)(2,1)} %get-tuple-element.47), channel_id=1, source_target_pairs={{0,1},{1,2},{2,3},{3,0},{4,5},{5,6},{6,7},{7,4},{8,9},{9,10},{10,1... | collective-permute-start | bytes 1572872 | tf_op jit(solution)/shard_map/ppermute | solution.py:228
  23.9 25.5 %collective-permute-start.1 = (bf16[128,2048]{1,0:T(8,128)(2,1)S(1)}, bf16[128,2048]{1,0:T(8,128)(2,1)}, u32[]{:S(2)}, u32[]{:S(2)}) collective-permute-start(bf16[128,2048]{1,0:T(8,128)(2,1)S(1)} %get-tuple-element.48), channel_id=1, source_target_pairs={{0,1},{1,2},{2,3},{3,0},{4,5},{5,6},{6,7},{7,4},{8,9},{9,10},{10,1... | collective-permute-start | bytes 1572872 | tf_op jit(solution)/shard_map/ppermute | solution.py:228
  38.8 119.0 %copy-start.41 = (f32[1024,32]{0,1:T(8,128)}, f32[1024,32]{0,1:T(8,128)S(1)}, u32[]{:S(2)}) copy-start(f32[1024,32]{0,1:T(8,128)S(1)} %get-tuple-element.132) | copy-start | bytes 393220
  39.3 144.5 %copy-start.27 = (pred[512,1024]{0,1:T(8,128)(4,1)}, pred[512,1024]{0,1:T(8,128)(4,1)S(1)}, u32[]{:S(2)}) copy-start(pred[512,1024]{0,1:T(8,128)(4,1)S(1)} %fusion.54) | copy-start | bytes 1572868
  39.3 85.5 %copy-start.57 = (f32[1,1,2048]{2,1,0:T(1,128)}, f32[1,1,2048]{2,1,0:T(1,128)S(1)}, u32[]{:S(2)}) copy-start(f32[1,1,2048]{2,1,0:T(1,128)S(1)} %get-tuple-element.129) | copy-start | bytes 24580
  46.7 16.8 %collective-permute-start.2 = (bf16[128,2048]{1,0:T(8,128)(2,1)}, bf16[128,2048]{1,0:T(8,128)(2,1)S(1)}, u32[]{:S(2)}, u32[]{:S(2)}) collective-permute-start(bf16[128,2048]{1,0:T(8,128)(2,1)} %collective-permute-done), channel_id=1, source_target_pairs={{0,1},{1,2},{2,3},{3,0},{4,5},{5,6},{6,7},{7,4},{8,9},{9,10},{10,1... | collective-permute-start | bytes 1572872 | tf_op jit(solution)/shard_map/ppermute | solution.py:228
  49.4 25.3 %collective-permute-start.3 = (bf16[128,2048]{1,0:T(8,128)(2,1)}, bf16[128,2048]{1,0:T(8,128)(2,1)S(1)}, u32[]{:S(2)}, u32[]{:S(2)}) collective-permute-start(bf16[128,2048]{1,0:T(8,128)(2,1)} %collective-permute-done.1), channel_id=1, source_target_pairs={{0,1},{1,2},{2,3},{3,0},{4,5},{5,6},{6,7},{7,4},{8,9},{9,10},{10,1... | collective-permute-start | bytes 1572872 | tf_op jit(solution)/shard_map/ppermute | solution.py:228
  63.5 22.5 %collective-permute-start.4 = (bf16[128,2048]{1,0:T(8,128)(2,1)S(1)}, bf16[128,2048]{1,0:T(8,128)(2,1)S(1)}, u32[]{:S(2)}, u32[]{:S(2)}) collective-permute-start(bf16[128,2048]{1,0:T(8,128)(2,1)S(1)} %collective-permute-done.2), channel_id=1, source_target_pairs={{0,1},{1,2},{2,3},{3,0},{4,5},{5,6},{6,7},{7,4},{8,9},{9,10},{10,1... | collective-permute-start | bytes 1572872 | tf_op jit(solution)/shard_map/ppermute | solution.py:228
  74.8 21.8 %collective-permute-start.5 = (bf16[128,2048]{1,0:T(8,128)(2,1)S(1)}, bf16[128,2048]{1,0:T(8,128)(2,1)S(1)}, u32[]{:S(2)}, u32[]{:S(2)}) collective-permute-start(bf16[128,2048]{1,0:T(8,128)(2,1)S(1)} %collective-permute-done.3), channel_id=1, source_target_pairs={{0,1},{1,2},{2,3},{3,0},{4,5},{5,6},{6,7},{7,4},{8,9},{9,10},{10,1... | collective-permute-start | bytes 1572872 | tf_op jit(solution)/shard_map/ppermute | solution.py:228
  96.6 26.3 %collective-permute-start.13 = (bf16[256,2048]{1,0:T(8,128)(2,1)S(1)}, bf16[256,2048]{1,0:T(8,128)(2,1)S(1)}, u32[]{:S(2)}, u32[]{:S(2)}) collective-permute-start(bf16[256,2048]{1,0:T(8,128)(2,1)S(1)} %convert_element_type.329.refs_1_), channel_id=1, source_target_pairs={{0,1},{1,2},{2,3},{3,0},{4,5},{5,6},{6,7},{7,4},{8,9},{9,10},{10,1... | collective-permute-start | bytes 3145736 | tf_op jit(solution)/shard_map/ppermute | solution.py:228
  122.9 25.6 %collective-permute-start.16 = (bf16[256,2048]{1,0:T(8,128)(2,1)S(1)}, bf16[256,2048]{1,0:T(8,128)(2,1)}, u32[]{:S(2)}, u32[]{:S(2)}) collective-permute-start(bf16[256,2048]{1,0:T(8,128)(2,1)S(1)} %collective-permute-done.13.refs_1_), channel_id=1, source_target_pairs={{0,1},{1,2},{2,3},{3,0},{4,5},{5,6},{6,7},{7,4},{8,9},{9,10},{10,1... | collective-permute-start | bytes 3145736 | tf_op jit(solution)/shard_map/ppermute | solution.py:228
  148.4 218.2 %collective-permute-start.19 = (bf16[256,2048]{1,0:T(8,128)(2,1)}, bf16[256,2048]{1,0:T(8,128)(2,1)}, u32[]{:S(2)}, u32[]{:S(2)}) collective-permute-start(bf16[256,2048]{1,0:T(8,128)(2,1)} %collective-permute-done.16.refs_1_), channel_id=1, source_target_pairs={{0,1},{1,2},{2,3},{3,0},{4,5},{5,6},{6,7},{7,4},{8,9},{9,10},{10,1... | collective-permute-start | bytes 3145736 | tf_op jit(solution)/shard_map/ppermute | solution.py:228
  198.1 16.6 %collective-permute-start.6 = (bf16[128,2048]{1,0:T(8,128)(2,1)S(1)}, bf16[128,2048]{1,0:T(8,128)(2,1)S(1)}, u32[]{:S(2)}, u32[]{:S(2)}) collective-permute-start(bf16[128,2048]{1,0:T(8,128)(2,1)S(1)} %convolution_convert_fusion.6), channel_id=1, source_target_pairs={{0,1},{1,2},{2,3},{3,0},{4,5},{5,6},{6,7},{7,4},{8,9},{9,10},{10,1... | collective-permute-start | bytes 1572872 | tf_op jit(solution)/shard_map/ppermute | solution.py:228
  199.6 26.4 %collective-permute-start.9 = (bf16[128,2048]{1,0:T(8,128)(2,1)S(1)}, bf16[128,2048]{1,0:T(8,128)(2,1)S(1)}, u32[]{:S(2)}, u32[]{:S(2)}) collective-permute-start(bf16[128,2048]{1,0:T(8,128)(2,1)S(1)} %convolution_convert_fusion.5), channel_id=1, source_target_pairs={{0,1},{1,2},{2,3},{3,0},{4,5},{5,6},{6,7},{7,4},{8,9},{9,10},{10,1... | collective-permute-start | bytes 1572872 | tf_op jit(solution)/shard_map/ppermute | solution.py:228
  215.2 22.0 %collective-permute-start.7 = (bf16[128,2048]{1,0:T(8,128)(2,1)S(1)}, bf16[128,2048]{1,0:T(8,128)(2,1)S(1)}, u32[]{:S(2)}, u32[]{:S(2)}) collective-permute-start(bf16[128,2048]{1,0:T(8,128)(2,1)S(1)} %add_convert_fusion.12), channel_id=1, source_target_pairs={{0,1},{1,2},{2,3},{3,0},{4,5},{5,6},{6,7},{7,4},{8,9},{9,10},{10,1... | collective-permute-start | bytes 1572872 | tf_op jit(solution)/shard_map/ppermute | solution.py:228
  226.5 22.0 %collective-permute-start.10 = (bf16[128,2048]{1,0:T(8,128)(2,1)S(1)}, bf16[128,2048]{1,0:T(8,128)(2,1)S(1)}, u32[]{:S(2)}, u32[]{:S(2)}) collective-permute-start(bf16[128,2048]{1,0:T(8,128)(2,1)S(1)} %add_convert_fusion.10), channel_id=1, source_target_pairs={{0,1},{1,2},{2,3},{3,0},{4,5},{5,6},{6,7},{7,4},{8,9},{9,10},{10,1... | collective-permute-start | bytes 1572872 | tf_op jit(solution)/shard_map/ppermute | solution.py:228
  237.3 22.4 %collective-permute-start.8 = (bf16[128,2048]{1,0:T(8,128)(2,1)S(1)}, bf16[128,2048]{1,0:T(8,128)(2,1)S(1)}, u32[]{:S(2)}, u32[]{:S(2)}) collective-permute-start(bf16[128,2048]{1,0:T(8,128)(2,1)S(1)} %add_convert_fusion.11), channel_id=1, source_target_pairs={{0,1},{1,2},{2,3},{3,0},{4,5},{5,6},{6,7},{7,4},{8,9},{9,10},{10,1... | collective-permute-start | bytes 1572872 | tf_op jit(solution)/shard_map/ppermute | solution.py:228
  248.6 19.1 %collective-permute-start.11 = (bf16[128,2048]{1,0:T(8,128)(2,1)S(1)}, bf16[128,2048]{1,0:T(8,128)(2,1)S(1)}, u32[]{:S(2)}, u32[]{:S(2)}) collective-permute-start(bf16[128,2048]{1,0:T(8,128)(2,1)S(1)} %add_convert_fusion.9), channel_id=1, source_target_pairs={{0,1},{1,2},{2,3},{3,0},{4,5},{5,6},{6,7},{7,4},{8,9},{9,10},{10,1... | collective-permute-start | bytes 1572872 | tf_op jit(solution)/shard_map/ppermute | solution.py:228
  270.7 24.0 %collective-permute-start.12 = (bf16[256,2048]{1,0:T(8,128)(2,1)}, bf16[256,2048]{1,0:T(8,128)(2,1)}, u32[]{:S(2)}, u32[]{:S(2)}) collective-permute-start(bf16[256,2048]{1,0:T(8,128)(2,1)} %multiply_convert_fusion.refs_0_), channel_id=1, source_target_pairs={{0,1},{1,2},{2,3},{3,0},{4,5},{5,6},{6,7},{7,4},{8,9},{9,10},{10,1... | collective-permute-start | bytes 3145736 | tf_op jit(solution)/shard_map/ppermute | solution.py:228
  294.8 24.2 %collective-permute-start.15 = (bf16[256,2048]{1,0:T(8,128)(2,1)}, bf16[256,2048]{1,0:T(8,128)(2,1)S(1)}, u32[]{:S(2)}, u32[]{:S(2)}) collective-permute-start(bf16[256,2048]{1,0:T(8,128)(2,1)} %collective-permute-done.12.refs_0_), channel_id=1, source_target_pairs={{0,1},{1,2},{2,3},{3,0},{4,5},{5,6},{6,7},{7,4},{8,9},{9,10},{10,1... | collective-permute-start | bytes 3145736 | tf_op jit(solution)/shard_map/ppermute | solution.py:228
  316.2 27.9 %collective-permute-start.14 = (bf16[256,2048]{1,0:T(8,128)(2,1)S(1)}, bf16[256,2048]{1,0:T(8,128)(2,1)S(1)}, u32[]{:S(2)}, u32[]{:S(2)}) collective-permute-start(bf16[256,2048]{1,0:T(8,128)(2,1)S(1)} %convert_element_type.330), channel_id=1, source_target_pairs={{0,1},{1,2},{2,3},{3,0},{4,5},{5,6},{6,7},{7,4},{8,9},{9,10},{10,1... | collective-permute-start | bytes 3145736 | tf_op jit(solution)/shard_map/ppermute | solution.py:228
  319.0 47.6 %collective-permute-start.18 = (bf16[256,2048]{1,0:T(8,128)(2,1)S(1)}, bf16[256,2048]{1,0:T(8,128)(2,1)S(1)}, u32[]{:S(2)}, u32[]{:S(2)}) collective-permute-start(bf16[256,2048]{1,0:T(8,128)(2,1)S(1)} %collective-permute-done.15.refs_0_), channel_id=1, source_target_pairs={{0,1},{1,2},{2,3},{3,0},{4,5},{5,6},{6,7},{7,4},{8,9},{9,10},{10,1... | collective-permute-start | bytes 3145736 | tf_op jit(solution)/shard_map/ppermute | solution.py:228
  344.4 42.2 %collective-permute-start.17 = (bf16[256,2048]{1,0:T(8,128)(2,1)S(1)}, bf16[256,2048]{1,0:T(8,128)(2,1)S(1)}, u32[]{:S(2)}, u32[]{:S(2)}) collective-permute-start(bf16[256,2048]{1,0:T(8,128)(2,1)S(1)} %add_convert_fusion.3), channel_id=1, source_target_pairs={{0,1},{1,2},{2,3},{3,0},{4,5},{5,6},{6,7},{7,4},{8,9},{9,10},{10,1... | collective-permute-start | bytes 3145736 | tf_op jit(solution)/shard_map/ppermute | solution.py:228
  387.9 22.1 %collective-permute-start.20 = (bf16[256,2048]{1,0:T(8,128)(2,1)}, bf16[256,2048]{1,0:T(8,128)(2,1)S(1)}, u32[]{:S(2)}, u32[]{:S(2)}) collective-permute-start(bf16[256,2048]{1,0:T(8,128)(2,1)} %add_convert_fusion.2), channel_id=1, source_target_pairs={{0,1},{1,2},{2,3},{3,0},{4,5},{5,6},{6,7},{7,4},{8,9},{9,10},{10,1... | collective-permute-start | bytes 3145736 | tf_op jit(solution)/shard_map/ppermute | solution.py:228
  402.7 271.8 %reduce-scatter.4.cloned.1.call-start = ((), (), s32[]{:S(2)}) async-start(), calls=%async_computation.5 | async-start | bytes 6488064 | tf_op jit(solution)/shard_map/reduce_scatter | solution.py:430
  415.1 15.1 %collective-permute-start.21 = (bf16[128,2048]{1,0:T(8,128)(2,1)S(1)}, bf16[128,2048]{1,0:T(8,128)(2,1)}, u32[]{:S(2)}, u32[]{:S(2)}) collective-permute-start(bf16[128,2048]{1,0:T(8,128)(2,1)S(1)} %get-tuple-element.73), channel_id=1, source_target_pairs={{0,1},{1,2},{2,3},{3,0},{4,5},{5,6},{6,7},{7,4},{8,9},{9,10},{10,1... | collective-permute-start | bytes 1572872 | tf_op jit(solution)/shard_map/ppermute | solution.py:228
  415.2 20.6 %collective-permute-start.24 = (bf16[128,2048]{1,0:T(8,128)(2,1)S(1)}, bf16[128,2048]{1,0:T(8,128)(2,1)}, u32[]{:S(2)}, u32[]{:S(2)}) collective-permute-start(bf16[128,2048]{1,0:T(8,128)(2,1)S(1)} %get-tuple-element.74), channel_id=1, source_target_pairs={{0,1},{1,2},{2,3},{3,0},{4,5},{5,6},{6,7},{7,4},{8,9},{9,10},{10,1... | collective-permute-start | bytes 1572872 | tf_op jit(solution)/shard_map/ppermute | solution.py:228
  438.5 14.3 %collective-permute-start.22 = (bf16[128,2048]{1,0:T(8,128)(2,1)}, bf16[128,2048]{1,0:T(8,128)(2,1)S(1)}, u32[]{:S(2)}, u32[]{:S(2)}) collective-permute-start(bf16[128,2048]{1,0:T(8,128)(2,1)} %collective-permute-done.21), channel_id=1, source_target_pairs={{0,1},{1,2},{2,3},{3,0},{4,5},{5,6},{6,7},{7,4},{8,9},{9,10},{10,1... | collective-permute-start | bytes 1572872 | tf_op jit(solution)/shard_map/ppermute | solution.py:228
  439.2 19.4 %collective-permute-start.25 = (bf16[128,2048]{1,0:T(8,128)(2,1)}, bf16[128,2048]{1,0:T(8,128)(2,1)}, u32[]{:S(2)}, u32[]{:S(2)}) collective-permute-start(bf16[128,2048]{1,0:T(8,128)(2,1)} %collective-permute-done.24), channel_id=1, source_target_pairs={{0,1},{1,2},{2,3},{3,0},{4,5},{5,6},{6,7},{7,4},{8,9},{9,10},{10,1... | collective-permute-start | bytes 1572872 | tf_op jit(solution)/shard_map/ppermute | solution.py:228
  462.3 13.3 %collective-permute-start.23 = (bf16[128,2048]{1,0:T(8,128)(2,1)}, bf16[128,2048]{1,0:T(8,128)(2,1)S(1)}, u32[]{:S(2)}, u32[]{:S(2)}) collective-permute-start(bf16[128,2048]{1,0:T(8,128)(2,1)} %copy-done.49), channel_id=1, source_target_pairs={{0,1},{1,2},{2,3},{3,0},{4,5},{5,6},{6,7},{7,4},{8,9},{9,10},{10,1... | collective-permute-start | bytes 1572872 | tf_op jit(solution)/shard_map/ppermute | solution.py:228
  462.4 18.9 %collective-permute-start.26 = (bf16[128,2048]{1,0:T(8,128)(2,1)}, bf16[128,2048]{1,0:T(8,128)(2,1)}, u32[]{:S(2)}, u32[]{:S(2)}) collective-permute-start(bf16[128,2048]{1,0:T(8,128)(2,1)} %collective-permute-done.25), channel_id=1, source_target_pairs={{0,1},{1,2},{2,3},{3,0},{4,5},{5,6},{6,7},{7,4},{8,9},{9,10},{10,1... | collective-permute-start | bytes 1572872 | tf_op jit(solution)/shard_map/ppermute | solution.py:228
  486.4 22.8 %collective-permute-start.27 = (bf16[256,2048]{1,0:T(8,128)(2,1)S(1)}, bf16[256,2048]{1,0:T(8,128)(2,1)S(1)}, u32[]{:S(2)}, u32[]{:S(2)}) collective-permute-start(bf16[256,2048]{1,0:T(8,128)(2,1)S(1)} %convert_element_type.337), channel_id=1, source_target_pairs={{0,1},{1,2},{2,3},{3,0},{4,5},{5,6},{6,7},{7,4},{8,9},{9,10},{10,1... | collective-permute-start | bytes 3145736 | tf_op jit(solution)/shard_map/ppermute | solution.py:228
  509.6 22.7 %collective-permute-start.28 = (bf16[256,2048]{1,0:T(8,128)(2,1)S(1)}, bf16[256,2048]{1,0:T(8,128)(2,1)S(1)}, u32[]{:S(2)}, u32[]{:S(2)}) collective-permute-start(bf16[256,2048]{1,0:T(8,128)(2,1)S(1)} %add_convert_fusion.1), channel_id=1, source_target_pairs={{0,1},{1,2},{2,3},{3,0},{4,5},{5,6},{6,7},{7,4},{8,9},{9,10},{10,1... | collective-permute-start | bytes 3145736 | tf_op jit(solution)/shard_map/ppermute | solution.py:228
  559.9 182.8 %reduce-scatter.6.cloned.1.call-start = ((), (), s32[]{:S(2)}) async-start(), calls=%async_computation.6 | async-start | bytes 18874368 | tf_op jit(solution)/shard_map/reduce_scatter | solution.py:360
  587.1 16.6 %collective-permute-start.30 = (bf16[128,2048]{1,0:T(8,128)(2,1)S(1)}, bf16[128,2048]{1,0:T(8,128)(2,1)S(1)}, u32[]{:S(2)}, u32[]{:S(2)}) collective-permute-start(bf16[128,2048]{1,0:T(8,128)(2,1)S(1)} %convolution_convert_fusion.4), channel_id=1, source_target_pairs={{0,1},{1,2},{2,3},{3,0},{4,5},{5,6},{6,7},{7,4},{8,9},{9,10},{10,1... | collective-permute-start | bytes 1572872 | tf_op jit(solution)/shard_map/ppermute | solution.py:228
  588.4 26.6 %collective-permute-start.33 = (bf16[128,2048]{1,0:T(8,128)(2,1)S(1)}, bf16[128,2048]{1,0:T(8,128)(2,1)S(1)}, u32[]{:S(2)}, u32[]{:S(2)}) collective-permute-start(bf16[128,2048]{1,0:T(8,128)(2,1)S(1)} %convolution_convert_fusion.3), channel_id=1, source_target_pairs={{0,1},{1,2},{2,3},{3,0},{4,5},{5,6},{6,7},{7,4},{8,9},{9,10},{10,1... | collective-permute-start | bytes 1572872 | tf_op jit(solution)/shard_map/ppermute | solution.py:228
  589.0 67.3 %collective-permute-start.29 = (bf16[256,2048]{1,0:T(8,128)(2,1)S(1)}, bf16[256,2048]{1,0:T(8,128)(2,1)S(1)}, u32[]{:S(2)}, u32[]{:S(2)}) collective-permute-start(bf16[256,2048]{1,0:T(8,128)(2,1)S(1)} %copy-done.56), channel_id=1, source_target_pairs={{0,1},{1,2},{2,3},{3,0},{4,5},{5,6},{6,7},{7,4},{8,9},{9,10},{10,1... | collective-permute-start | bytes 3145736 | tf_op jit(solution)/shard_map/ppermute | solution.py:228
  604.9 43.8 %collective-permute-start.31 = (bf16[128,2048]{1,0:T(8,128)(2,1)S(1)}, bf16[128,2048]{1,0:T(8,128)(2,1)S(1)}, u32[]{:S(2)}, u32[]{:S(2)}) collective-permute-start(bf16[128,2048]{1,0:T(8,128)(2,1)S(1)} %add_convert_fusion.7), channel_id=1, source_target_pairs={{0,1},{1,2},{2,3},{3,0},{4,5},{5,6},{6,7},{7,4},{8,9},{9,10},{10,1... | collective-permute-start | bytes 1572872 | tf_op jit(solution)/shard_map/ppermute | solution.py:228
  616.2 39.0 %collective-permute-start.34 = (bf16[128,2048]{1,0:T(8,128)(2,1)S(1)}, bf16[128,2048]{1,0:T(8,128)(2,1)S(1)}, u32[]{:S(2)}, u32[]{:S(2)}) collective-permute-start(bf16[128,2048]{1,0:T(8,128)(2,1)S(1)} %add_convert_fusion.5), channel_id=1, source_target_pairs={{0,1},{1,2},{2,3},{3,0},{4,5},{5,6},{6,7},{7,4},{8,9},{9,10},{10,1... | collective-permute-start | bytes 1572872 | tf_op jit(solution)/shard_map/ppermute | solution.py:228
  649.9 11.0 %collective-permute-start.32 = (bf16[128,2048]{1,0:T(8,128)(2,1)S(1)}, bf16[128,2048]{1,0:T(8,128)(2,1)S(1)}, u32[]{:S(2)}, u32[]{:S(2)}) collective-permute-start(bf16[128,2048]{1,0:T(8,128)(2,1)S(1)} %add_convert_fusion.6), channel_id=1, source_target_pairs={{0,1},{1,2},{2,3},{3,0},{4,5},{5,6},{6,7},{7,4},{8,9},{9,10},{10,1... | collective-permute-start | bytes 1572872 | tf_op jit(solution)/shard_map/ppermute | solution.py:228
  656.3 11.1 %collective-permute-start.35 = (bf16[128,2048]{1,0:T(8,128)(2,1)S(1)}, bf16[128,2048]{1,0:T(8,128)(2,1)S(1)}, u32[]{:S(2)}, u32[]{:S(2)}) collective-permute-start(bf16[128,2048]{1,0:T(8,128)(2,1)S(1)} %add_convert_fusion.4), channel_id=1, source_target_pairs={{0,1},{1,2},{2,3},{3,0},{4,5},{5,6},{6,7},{7,4},{8,9},{9,10},{10,1... | collective-permute-start | bytes 1572872 | tf_op jit(solution)/shard_map/ppermute | solution.py:228
  675.1 8.7 %collective-permute-start.36 = (f32[256,2]{0,1:T(2,128)S(1)}, f32[256,2]{0,1:T(2,128)S(1)}, u32[]{:S(2)}, u32[]{:S(2)}) collective-permute-start(f32[256,2]{0,1:T(2,128)S(1)} %slice.210), channel_id=1, source_target_pairs={{0,1},{1,2},{2,3},{3,0},{4,5},{5,6},{6,7},{7,4},{8,9},{9,10},{10,1... | collective-permute-start | bytes 6152 | tf_op jit(solution)/shard_map/ppermute | solution.py:443
  675.1 8.7 %collective-permute-start.37 = (f32[256,2]{0,1:T(2,128)S(1)}, f32[256,2]{0,1:T(2,128)S(1)}, u32[]{:S(2)}, u32[]{:S(2)}) collective-permute-start(f32[256,2]{0,1:T(2,128)S(1)} %slice.210), channel_id=1, source_target_pairs={{0,2},{1,3},{2,0},{3,1},{4,6},{5,7},{6,4},{7,5},{8,10},{9,11},{10,... | collective-permute-start | bytes 6152 | tf_op jit(solution)/shard_map/ppermute | solution.py:443
  676.5 7.3 collective-permute-start.38
  (68 other events, 387.5 us)
Sparse Core Ops, SparseCore 0:
  10.4 34.8 all-gather.5
  47.3 28.0 all-gather.9
  77.3 125.1 all-gather.7
  402.8 71.3 reduce-scatter.7
  560.0 62.9 reduce-scatter.3
  626.5 116.2 reduce-scatter.5

commit v5 on v4

--- a/solution.py
+++ b/solution.py
@@ -298,9 +298,9 @@
 
     input_blocks = spread_halves(block_input)
     grad_blocks = spread(after(out_cotangent.astype(bf16), input_blocks[-1]))
-    normed_pairs = [
-        [norm_apply(piece.astype(f32), gains_all[0]) for piece in pieces] for pieces in input_blocks
-    ]
+    normed_pairs = []
+    for pieces in input_blocks:
+        normed_pairs.append([norm_apply(piece.astype(f32), gains_all[0]) for piece in pieces])
     residual = block_input.astype(f32)
     inv_attn = norm_apply(residual, gains_all[0])[0]
     normed_all = in_order([[pair[1] for pair in pairs] for pairs in normed_pairs])
@@ -362,10 +362,11 @@
     tile = mlp_tile(w_mlp.shape[2])
     grad_wgu = grad_wgu.astype(f32).reshape(grad_wgu.shape[0], -1, 2, tile)
     grad_wgu = jnp.swapaxes(grad_wgu, 1, 2).reshape(grad_wgu.shape[0], 2, -1)
-    norm_part, grad_gain_mlp = norm_back(middle, inv_mlp, gains_all[1], grad_normed_mlp)
+    gain_mlp_part = jnp.sum(grad_wgu * w_gate_up[0].astype(f32), axis=(1, 2))
+    norm_part, _ = norm_back(middle, inv_mlp, gains_all[1], grad_normed_mlp)
     grad_middle = out_cotangent + norm_part
 
-    middle_blocks = spread_halves(grad_middle.astype(bf16))
+    middle_blocks = [[block] for block in spread(grad_middle.astype(bf16))]
     do_parts = [
         [dot_nt(piece, w_out_all).astype(bf16) for piece in pieces] for pieces in middle_blocks
     ]
@@ -376,7 +377,10 @@
 
     out_totals = [after(out_parts[1 % ring], middle_blocks[-1]).astype(bf16)]
     for step in range(2, ring + 1):
-        out_totals.append((shift(out_totals[-1]).astype(f32) + out_parts[step % ring]))
+        source = out_totals[-1]
+        if step == ring:
+            source = after(source, (grad_wgu, grad_down, gain_mlp_part))
+        out_totals.append((shift(source).astype(f32) + out_parts[step % ring]))
         if step < ring:
             out_totals[-1] = out_totals[-1].astype(bf16)
     output_rows = middle + out_totals[-1]
@@ -423,21 +427,18 @@
     grad_rows = grad_middle + norm_part
 
     grad_wqkv = dot_tn(normed_all, grad_qkv)
-    grad_gain_attn = jnp.sum(grad_wqkv * w_qkv.astype(f32), axis=1) / gains_all[0].astype(f32)
     grad_wqkv = grad_wqkv.astype(bf16)
-    gain_columns = jnp.stack([grad_gain_attn, grad_gain_mlp], axis=1).astype(bf16)
-    gain_columns = jnp.pad(gain_columns, ((0, 0), (0, 126)))
     packed = lax.psum_scatter(
-        jnp.concatenate([grad_wqkv, grad_wo, gain_columns], axis=1),
+        jnp.concatenate([grad_wqkv, grad_wo], axis=1),
         "fsdp", scatter_dimension=0, tiled=True,
     )
     packed = packed.astype(f32)
     qkv_width = grad_wqkv.shape[1]
-    gain_start = qkv_width + grad_wo.shape[1]
     grad_wq = packed[:, :query_width]
     grad_wkv = packed[:, query_width:qkv_width].reshape(-1, kv_local, 2 * head_size)
-    grad_wo = jnp.swapaxes(packed[:, qkv_width:gain_start], 0, 1)
-    gain_part = packed[:, gain_start : gain_start + 2]
+    grad_wo = jnp.swapaxes(packed[:, qkv_width:], 0, 1)
+    gain_attn_part = jnp.sum(packed[:, :qkv_width] * w_qkv_local.astype(f32), axis=1)
+    gain_part = jnp.stack([gain_attn_part, gain_mlp_part]) / norm_gains[0].astype(f32)
     gain_total = gain_part
     for distance in range(1, ring):
         gain_total = gain_total + lax.ppermute(
@@ -451,7 +452,7 @@
         grad_wo[None],
         grad_wgu[None],
         grad_down[None],
-        gain_total.T[None],
+        gain_total[None],
     )
 
 

time: 765 us -> 702 us (0.918)
  waiting for transfers between devices: 350 us -> 301 us
  matrix products: 150 us -> 139 us
    reduce_scatter x1, waiting for transfers between devices: 58.4 us -> 0.01 us  [per_device(): lax.psum_scatter(grad_wgu, 'fsdp', scatter_dimension=0, tiled=True)]
    ppermute x36 -> x33, waiting for transfers between devices: 291 us -> 298 us  [shift(): return lax.ppermute(rows, 'tensor', ring_pairs)]
    dot_general x16 -> x12, matrix products: 27.7 us -> 20.3 us  [dot_nt(): lax.dot_general(a, b, (((1,), (1,)), ((), ())), preferred_element_type=f32)]
    unnamed x145 -> x166, local copies, waits for them, and re-layouts: 26.7 us -> 31.1 us
  transfers between devices with their start and end apart: 45 -> 42, of which waited for: 32 -> 30; matrix products, arithmetic and copies ran while one was open for 34% -> 31% of each run, Pallas kernels for 10% -> 8%
where the time goes in v5:
time: 702 us; the launch traced here: 695 us
  waiting for transfers between devices  301 us (43%)
  matrix products  139 us (20%)
  Pallas kernels  74.9 us (11%)
  other arithmetic  69.4 us (10%)
  local copies, waits for them, and re-layouts  65.5 us (9%)
  starting transfers between devices  19.2 us (3%)
  between operations  16.2 us (2%)
  blocking collectives  8.94 us (1%)
    ppermute x33, waiting for transfers between devices, shift(): return lax.ppermute(rows, 'tensor', ring_pairs)  298 us
    pallas_call x4, Pallas kernels, mlp_block(): pl.pallas_call(functools.partial(mlp_kernel, reused), grid=(hidden_width...  74.9 us
    dot_general x4, matrix products, dot_tn(): lax.dot_general(a, b, (((0,), (0,)), ((), ())), preferred_element_type=f32)  46.9 us
    unnamed x166, local copies, waits for them, and re-layouts  31.1 us
    dot_general x12, matrix products, dot_nt(): lax.dot_general(a, b, (((1,), (1,)), ((), ())), preferred_element_type=f32)  20.3 us
    ppermute x33, starting transfers between devices, shift(): return lax.ppermute(rows, 'tensor', ring_pairs)  14.5 us
  transfers between devices with their start and end apart: 42, of which 30 were waited for; matrix products, arithmetic and copies ran while one was open for 31% of the time, Pallas kernels for 8%

profile of v5, /device:TPU:0, one launch (start us, length us, event | category | flops | bytes accessed | tf_op | source)
XLA Modules:
  0.0 694.5 jit_solution(10173891634735625683)
XLA Ops:
  26.7 8.9 %all-gather = bf16[1,2,2048]{2,1,0:T(2,128)(2,1)S(1)} all-gather(bf16[1,2,256]{2,1,0:T(2,128)(2,1)S(1)} %copy-done.74), channel_id=2, replica_groups=mesh['fsdp'=8,'tensor'=4] {'fsdp'}, dimensions={2}, use_global_device_ids=true | all-gather | bytes 9216 | tf_op jit(solution)/shard_map/all_gather | solution.py:285
  56.6 7.6 %collective-permute-done.2 = bf16[128,2048]{1,0:T(8,128)(2,1)S(1)} collective-permute-done((bf16[128,2048]{1,0:T(8,128)(2,1)}, bf16[128,2048]{1,0:T(8,128)(2,1)S(1)}, u32[]{:S(2)}, u32[]{:S(2)}) %collective-permute-start.2) | collective-permute-done | bytes 524320 | tf_op jit(solution)/shard_map/ppermute | solution.py:228
  64.2 11.2 %collective-permute-done.3 = bf16[128,2048]{1,0:T(8,128)(2,1)S(1)} collective-permute-done((bf16[128,2048]{1,0:T(8,128)(2,1)}, bf16[128,2048]{1,0:T(8,128)(2,1)S(1)}, u32[]{:S(2)}, u32[]{:S(2)}) %collective-permute-start.3) | collective-permute-done | bytes 524320 | tf_op jit(solution)/shard_map/ppermute | solution.py:228
  76.8 9.9 %collective-permute-done.4 = bf16[128,2048]{1,0:T(8,128)(2,1)S(1)} collective-permute-done((bf16[128,2048]{1,0:T(8,128)(2,1)S(1)}, bf16[128,2048]{1,0:T(8,128)(2,1)S(1)}, u32[]{:S(2)}, u32[]{:S(2)}) %collective-permute-start.4) | collective-permute-done | bytes 524320 | tf_op jit(solution)/shard_map/ppermute | solution.py:228
  86.6 10.6 %collective-permute-done.5 = bf16[128,2048]{1,0:T(8,128)(2,1)S(1)} collective-permute-done((bf16[128,2048]{1,0:T(8,128)(2,1)S(1)}, bf16[128,2048]{1,0:T(8,128)(2,1)S(1)}, u32[]{:S(2)}, u32[]{:S(2)}) %collective-permute-start.5) | collective-permute-done | bytes 524320 | tf_op jit(solution)/shard_map/ppermute | solution.py:228
  98.6 25.0 %collective-permute-done.13.refs_1_ = bf16[256,2048]{1,0:T(8,128)(2,1)S(1)} collective-permute-done((bf16[256,2048]{1,0:T(8,128)(2,1)S(1)}, bf16[256,2048]{1,0:T(8,128)(2,1)S(1)}, u32[]{:S(2)}, u32[]{:S(2)}) %collective-permute-start.13) | collective-permute-done | bytes 1048608 | tf_op jit(solution)/shard_map/ppermute | solution.py:228
  126.5 22.6 %collective-permute-done.16.refs_1_ = bf16[256,2048]{1,0:T(8,128)(2,1)} collective-permute-done((bf16[256,2048]{1,0:T(8,128)(2,1)S(1)}, bf16[256,2048]{1,0:T(8,128)(2,1)}, u32[]{:S(2)}, u32[]{:S(2)}) %collective-permute-start.16) | collective-permute-done | bytes 1048608 | tf_op jit(solution)/shard_map/ppermute | solution.py:228
  149.4 6.6 fusion.194
  164.7 3.1 convolution_convert_fusion.8
  167.8 7.6 %fusion.5 = (f32[2,4,512]{2,1,0:T(4,128)S(1)}, f32[2,1024,512,4]{2,1,3,0:T(8,128)}) fusion(pred[512,1024]{0,1:T(8,128)(4,1)S(1)} %fusion.47, bf16[512,2,4,64]{0,3,2,1:T(8,128)(2,1)S(1)} %pad_maximum_fusion.6, bf16[1024,2,64]{0,2,1:T(8,128)(2,1)S(1)} %pad_maximum_fusion.9), kind=kOutput, calls=%fused_computation.11 | convolution fusion | flops 549449728 | bytes 18104320 | tf_op jit(solution)/shard_map/qkgd,skd->kgqs/dot_general | solution.py:68
  175.5 9.3 %exponential_reduce_fusion = f32[2,4,512]{2,1,0:T(4,128)S(1)} fusion(f32[2,1024,512,4]{2,1,3,0:T(8,128)} %get-tuple-element.133, f32[2,4,512]{2,1,0:T(4,128)S(1)} %get-tuple-element.132, pred[512,1024]{0,1:T(8,128)(4,1)S(1)} %fusion.47), kind=kLoop, calls=%fused_computation.9 | loop fusion | flops 16773120 | bytes 17334272 | tf_op jit(solution)/shard_map/reduce_sum | solution.py:73
  184.8 8.1 %fusion.48 = bf16[2,64,4,512]{3,1,2,0:T(8,128)(2,1)S(1)} fusion(f32[2,1024,512,4]{2,1,3,0:T(8,128)} %get-tuple-element.133, f32[2,4,512]{2,1,0:T(4,128)S(1)} %bitcast.323, pred[512,1024]{0,1:T(8,128)(4,1)S(1)} %fusion.47, bf16[1024,2,64]{0,2,1:T(8,128)(2,1)S(1)} %slice-done.3), kind=kOutput, calls=%fused_computation.105 | convolution fusion | flops 553910272 | bytes 18104320 | tf_op jit(solution)/shard_map/kgqs,skd->qkgd/dot_general | solution.py:75
  198.6 14.4 %collective-permute-done.6 = bf16[128,2048]{1,0:T(8,128)(2,1)S(1)} collective-permute-done((bf16[128,2048]{1,0:T(8,128)(2,1)S(1)}, bf16[128,2048]{1,0:T(8,128)(2,1)S(1)}, u32[]{:S(2)}, u32[]{:S(2)}) %collective-permute-start.6) | collective-permute-done | bytes 524320 | tf_op jit(solution)/shard_map/ppermute | solution.py:228
  213.6 10.7 %collective-permute-done.9 = bf16[128,2048]{1,0:T(8,128)(2,1)S(1)} collective-permute-done((bf16[128,2048]{1,0:T(8,128)(2,1)S(1)}, bf16[128,2048]{1,0:T(8,128)(2,1)S(1)}, u32[]{:S(2)}, u32[]{:S(2)}) %collective-permute-start.9) | collective-permute-done | bytes 524320 | tf_op jit(solution)/shard_map/ppermute | solution.py:228
  225.3 10.2 %collective-permute-done.7 = bf16[128,2048]{1,0:T(8,128)(2,1)S(1)} collective-permute-done((bf16[128,2048]{1,0:T(8,128)(2,1)S(1)}, bf16[128,2048]{1,0:T(8,128)(2,1)S(1)}, u32[]{:S(2)}, u32[]{:S(2)}) %collective-permute-start.7) | collective-permute-done | bytes 524320 | tf_op jit(solution)/shard_map/ppermute | solution.py:228
  235.7 11.1 %collective-permute-done.10 = bf16[128,2048]{1,0:T(8,128)(2,1)S(1)} collective-permute-done((bf16[128,2048]{1,0:T(8,128)(2,1)S(1)}, bf16[128,2048]{1,0:T(8,128)(2,1)S(1)}, u32[]{:S(2)}, u32[]{:S(2)}) %collective-permute-start.10) | collective-permute-done | bytes 524320 | tf_op jit(solution)/shard_map/ppermute | solution.py:228
  247.4 10.5 %collective-permute-done.8 = bf16[128,2048]{1,0:T(8,128)(2,1)S(1)} collective-permute-done((bf16[128,2048]{1,0:T(8,128)(2,1)S(1)}, bf16[128,2048]{1,0:T(8,128)(2,1)S(1)}, u32[]{:S(2)}, u32[]{:S(2)}) %collective-permute-start.8) | collective-permute-done | bytes 524320 | tf_op jit(solution)/shard_map/ppermute | solution.py:228
  258.1 7.9 %collective-permute-done.11 = bf16[128,2048]{1,0:T(8,128)(2,1)S(1)} collective-permute-done((bf16[128,2048]{1,0:T(8,128)(2,1)S(1)}, bf16[128,2048]{1,0:T(8,128)(2,1)S(1)}, u32[]{:S(2)}, u32[]{:S(2)}) %collective-permute-start.11) | collective-permute-done | bytes 524320 | tf_op jit(solution)/shard_map/ppermute | solution.py:228
  268.0 18.9 %mlp_block.4 = (bf16[1024,2048]{1,0:T(8,128)(2,1)}, bf16[1024,4096]{1,0:T(8,128)(2,1)}, bf16[1024,2048]{1,0:T(8,128)(2,1)}, bf16[1024,2048]{1,0:T(8,128)(2,1)}, ...) custom-call(bf16[256,2048]{1,0:T(8,128)(2,1)} %multiply_convert_fusion.refs_0_, ...), custom_call_target="tpu_custom_call" | custom-call | flops 12884901888 | bytes 31457280 | tf_op jit(solution)/shard_map/mlp_block/pallas_call | solution.py:168
  288.2 3.9 collective-permute-done.12.refs_0_
  293.3 18.7 %mlp_block.5 = (bf16[1024,2048]{1,0:T(8,128)(2,1)}, bf16[1024,4096]{1,0:T(8,128)(2,1)}, bf16[1024,2048]{1,0:T(8,128)(2,1)}, bf16[1024,2048]{1,0:T(8,128)(2,1)}, ...) custom-call(bf16[256,2048]{1,0:T(8,128)(2,1)} %collective-permute-do, ...), custom_call_target="tpu_custom_call", output_to_operand_aliasing={{0}: (3, {}), {1}: (4, {}), {2}: (5, {}), {3}: (6, {})} | custom-call | flops 12884901888 | bytes 31457280 | tf_op jit(solution)/shard_map/mlp_block/pallas_call | solution.py:168
  315.4 18.7 %mlp_block.6 = (bf16[1024,2048]{1,0:T(8,128)(2,1)}, bf16[1024,4096]{1,0:T(8,128)(2,1)}, bf16[1024,2048]{1,0:T(8,128)(2,1)}, bf16[1024,2048]{1,0:T(8,128)(2,1)}, ...) custom-call(bf16[256,2048]{1,0:T(8,128)(2,1)S(1)} %collective-permut, ...), custom_call_target="tpu_custom_call", output_to_operand_aliasing={{0}: (3, {}), {1}: (4, {}), {2}: (5, {}), {3}: (6, {})} | custom-call | flops 12884901888 | bytes 31457280 | tf_op jit(solution)/shard_map/mlp_block/pallas_call | solution.py:168
  337.7 18.7 %mlp_block.7 = (bf16[1024,2048]{1,0:T(8,128)(2,1)}, bf16[1024,4096]{1,0:T(8,128)(2,1)}, bf16[1024,2048]{1,0:T(8,128)(2,1)}, bf16[1024,2048]{1,0:T(8,128)(2,1)}, ...) custom-call(bf16[256,2048]{1,0:T(8,128)(2,1)S(1)} %collective-permut, ...), custom_call_target="tpu_custom_call", output_to_operand_aliasing={{0}: (3, {}), {1}: (4, {}), {2}: (5, {}), {3}: (6, {})} | custom-call | flops 12884901888 | bytes 31457280 | tf_op jit(solution)/shard_map/mlp_block/pallas_call | solution.py:168
  359.1 24.9 %convolution_convert_fusion = bf16[2048,4096]{1,0:T(8,128)(2,1)} fusion(bf16[1024,2048]{1,0:T(8,128)(2,1)} %get-tuple-element.77, bf16[1024,4096]{1,0:T(8,128)(2,1)} %get-tuple-element.78), kind=kOutput, calls=%fused_computation.10 | convolution fusion | flops 17188257792 | bytes 29360128 | tf_op jit(solution)/shard_map/dot_general | solution.py:225
  386.0 22.9 %collective-permute-done.14 = bf16[256,2048]{1,0:T(8,128)(2,1)S(1)} collective-permute-done((bf16[256,2048]{1,0:T(8,128)(2,1)S(1)}, bf16[256,2048]{1,0:T(8,128)(2,1)S(1)}, u32[]{:S(2)}, u32[]{:S(2)}) %collective-permute-start.14) | collective-permute-done | bytes 1048608 | tf_op jit(solution)/shard_map/ppermute | solution.py:228
  410.1 22.2 %collective-permute-done.17 = bf16[256,2048]{1,0:T(8,128)(2,1)S(1)} collective-permute-done((bf16[256,2048]{1,0:T(8,128)(2,1)S(1)}, bf16[256,2048]{1,0:T(8,128)(2,1)S(1)}, u32[]{:S(2)}, u32[]{:S(2)}) %collective-permute-start.17) | collective-permute-done | bytes 1048608 | tf_op jit(solution)/shard_map/ppermute | solution.py:228
  433.4 19.0 %collective-permute-done.20 = bf16[256,2048]{1,0:T(8,128)(2,1)S(1)} collective-permute-done((bf16[256,2048]{1,0:T(8,128)(2,1)S(1)}, bf16[256,2048]{1,0:T(8,128)(2,1)S(1)}, u32[]{:S(2)}, u32[]{:S(2)}) %collective-permute-start.20) | collective-permute-done | bytes 1048608 | tf_op jit(solution)/shard_map/ppermute | solution.py:228
  458.0 9.8 %fusion.113 = f32[2,1024,512,4]{2,1,3,0:T(8,128)} fusion(bf16[512,2,4,64]{0,3,2,1:T(8,128)(2,1)S(1)} %copy-done.37, bf16[1024,2,32]{0,2,1:T(8,128)(2,1)S(1)} %get-tuple-element.114, bf16[1024,2,32]{0,2,1:T(8,128)(2,1)S(1)} %get-tuple-element.113), kind=kOutput, calls=%fused_computation.195 | convolution fusion | flops 537395200 | bytes 17563648 | tf_op jit(solution)/shard_map/qkgd,skd->kgqs/dot_general | solution.py:85
  467.8 13.2 %collective-permute-done.21 = bf16[256,2048]{1,0:T(8,128)(2,1)} collective-permute-done((bf16[256,2048]{1,0:T(8,128)(2,1)S(1)}, bf16[256,2048]{1,0:T(8,128)(2,1)}, u32[]{:S(2)}, u32[]{:S(2)}) %collective-permute-start.21) | collective-permute-done | bytes 1048608 | tf_op jit(solution)/shard_map/ppermute | solution.py:228
  481.0 11.5 %convolution_convert_fusion.1 = bf16[2048,2048]{1,0:T(8,128)(2,1)} fusion(bf16[1024,2048]{1,0:T(8,128)(2,1)S(1)} %copy-done.24, bf16[1024,2048]{1,0:T(8,128)(2,1)S(1)} %copy-done.23), kind=kOutput, calls=%fused_computation.24 | convolution fusion | flops 8594128896 | bytes 16777216 | tf_op jit(solution)/shard_map/dot_general | solution.py:225
  507.2 3.6 fusion.62
  516.5 9.8 %collective-permute-done.23 = bf16[256,2048]{1,0:T(8,128)(2,1)} collective-permute-done((bf16[256,2048]{1,0:T(8,128)(2,1)}, bf16[256,2048]{1,0:T(8,128)(2,1)}, u32[]{:S(2)}, u32[]{:S(2)}) %collective-permute-start.23) | collective-permute-done | bytes 1048608 | tf_op jit(solution)/shard_map/ppermute | solution.py:228
  532.8 4.7 convolution_convert_fusion.3
  537.6 3.2 fusion.9
  545.3 4.0 collective-permute-done.24
  551.4 9.5 %fusion.2 = bf16[2,4,512,1024]{2,3,1,0:T(8,128)(2,1)S(1)} fusion(f32[2,1024,512,4]{2,1,3,0:T(8,128)} %fusion.113, f32[2,4,512]{2,1,0:T(4,128)S(1)} %fusion.96, f32[2,4,512]{2,1,0:T(4,128)S(1)} %bitcast.324, pred[512,1024]{0,1:T(8,128)(4,1)S(1)} %copy-done.40, bf16[512,2,4,64]{0,3,2,1:T(8,128)(2,1)S(1)} %bitcast.293, bf16[1024,2,128]{0,2,1:T(8,128)(2,1)S(1)} %copy-done.57), kind=kOutput, calls=%fused_computation.3 | convolution fusion | flops 566231040 | bytes 26509312 | tf_op jit(solution)/shard_map/qkgd,skd->kgqs/dot_general | solution.py:91
  563.7 8.3 %fusion.68 = bf16[1024,2,64]{0,2,1:T(8,128)(2,1)S(1)} fusion(bf16[512,2,4,64]{0,3,2,1:T(8,128)(2,1)S(1)} %bitcast.294, f32[2,1024,512,4]{2,1,3,0:T(8,128)} %fusion.113, f32[2,4,512]{2,1,0:T(4,128)S(1)} %bitcast.325, pred[512,1024]{0,1:T(8,128)(4,1)S(1)} %copy-done.40, f32[512,2,64]{0,2,1:T(8,128)S(1)} %convolution_bitcast_fusion.3), kind=kOutput, calls=%fused_computation.115 | convolution fusion | flops 553910272 | bytes 18366464 | tf_op jit(solution)/shard_map/kgqs,qkgd->skd/dot_general | solution.py:103
  577.4 5.8 convolution_convert_fusion.2
  593.5 13.2 %collective-permute-done.27 = bf16[128,2048]{1,0:T(8,128)(2,1)S(1)} collective-permute-done((bf16[128,2048]{1,0:T(8,128)(2,1)S(1)}, bf16[128,2048]{1,0:T(8,128)(2,1)S(1)}, u32[]{:S(2)}, u32[]{:S(2)}) %collective-permute-start.27) | collective-permute-done | bytes 524320 | tf_op jit(solution)/shard_map/ppermute | solution.py:228
  608.2 9.7 %collective-permute-done.30 = bf16[128,2048]{1,0:T(8,128)(2,1)S(1)} collective-permute-done((bf16[128,2048]{1,0:T(8,128)(2,1)S(1)}, bf16[128,2048]{1,0:T(8,128)(2,1)S(1)}, u32[]{:S(2)}, u32[]{:S(2)}) %collective-permute-start.30) | collective-permute-done | bytes 524320 | tf_op jit(solution)/shard_map/ppermute | solution.py:228
  619.5 9.7 %collective-permute-done.28 = bf16[128,2048]{1,0:T(8,128)(2,1)S(1)} collective-permute-done((bf16[128,2048]{1,0:T(8,128)(2,1)S(1)}, bf16[128,2048]{1,0:T(8,128)(2,1)S(1)}, u32[]{:S(2)}, u32[]{:S(2)}) %collective-permute-start.28) | collective-permute-done | bytes 524320 | tf_op jit(solution)/shard_map/ppermute | solution.py:228
  630.7 5.1 collective-permute-done.31
  637.9 3.5 collective-permute-done.29
  642.6 5.7 collective-permute-done.32
  651.1 6.7 reshape.457
  657.8 5.3 fusion.17
  668.7 4.4 collective-permute-start.34
  680.7 6.5 fusion.23
  (366 shorter events, 162.2 us)
Async XLA Ops:
  7.2 142.2 %all-gather.6.cloned.1.call-start = ((), (), s32[]{:S(2)}) async-start(), calls=%async_computation.3 | async-start | bytes 3538944 | tf_op jit(solution)/shard_map/all_gather | solution.py:284
  10.7 183.2 %all-gather.10.cloned.1.call-start = ((), (), s32[]{:S(2)}) async-start(), calls=%async_computation.8 | async-start | bytes 2359296 | tf_op jit(solution)/shard_map/all_gather | solution.py:286
  11.4 256.5 %all-gather.8.cloned.1.call-start = ((), (), s32[]{:S(2)}) async-start(), calls=%async_computation.4 | async-start | bytes 28311552 | tf_op jit(solution)/shard_map/all_gather | solution.py:287
  19.4 631.7 %reduce-scatter.6.cloned.1.call-start = ((), (), s32[]{:S(2)}) async-start(), calls=%async_computation.6 | async-start | bytes 18874368 | tf_op jit(solution)/shard_map/reduce_scatter | solution.py:360
  21.5 25.8 %collective-permute-start = (bf16[128,2048]{1,0:T(8,128)(2,1)}, bf16[128,2048]{1,0:T(8,128)(2,1)}, u32[]{:S(2)}, u32[]{:S(2)}) collective-permute-start(bf16[128,2048]{1,0:T(8,128)(2,1)} %get-tuple-element.46), channel_id=1, source_target_pairs={{0,1},{1,2},{2,3},{3,0},{4,5},{5,6},{6,7},{7,4},{8,9},{9,10},{10,1... | collective-permute-start | bytes 1572872 | tf_op jit(solution)/shard_map/ppermute | solution.py:228
  24.6 25.5 %collective-permute-start.1 = (bf16[128,2048]{1,0:T(8,128)(2,1)S(1)}, bf16[128,2048]{1,0:T(8,128)(2,1)}, u32[]{:S(2)}, u32[]{:S(2)}) collective-permute-start(bf16[128,2048]{1,0:T(8,128)(2,1)S(1)} %get-tuple-element.47), channel_id=1, source_target_pairs={{0,1},{1,2},{2,3},{3,0},{4,5},{5,6},{6,7},{7,4},{8,9},{9,10},{10,1... | collective-permute-start | bytes 1572872 | tf_op jit(solution)/shard_map/ppermute | solution.py:228
  39.5 118.4 %copy-start.50 = (f32[1024,32]{0,1:T(8,128)}, f32[1024,32]{0,1:T(8,128)S(1)}, u32[]{:S(2)}) copy-start(f32[1024,32]{0,1:T(8,128)S(1)} %get-tuple-element.127) | copy-start | bytes 393220
  40.0 144.8 %copy-start.39 = (pred[512,1024]{0,1:T(8,128)(4,1)}, pred[512,1024]{0,1:T(8,128)(4,1)S(1)}, u32[]{:S(2)}) copy-start(pred[512,1024]{0,1:T(8,128)(4,1)S(1)} %fusion.47) | copy-start | bytes 1572868
  40.0 85.6 %copy-start.67 = (f32[1,1,2048]{2,1,0:T(1,128)}, f32[1,1,2048]{2,1,0:T(1,128)S(1)}, u32[]{:S(2)}) copy-start(f32[1,1,2048]{2,1,0:T(1,128)S(1)} %get-tuple-element.123) | copy-start | bytes 24580
  47.4 16.8 %collective-permute-start.2 = (bf16[128,2048]{1,0:T(8,128)(2,1)}, bf16[128,2048]{1,0:T(8,128)(2,1)S(1)}, u32[]{:S(2)}, u32[]{:S(2)}) collective-permute-start(bf16[128,2048]{1,0:T(8,128)(2,1)} %collective-permute-done), channel_id=1, source_target_pairs={{0,1},{1,2},{2,3},{3,0},{4,5},{5,6},{6,7},{7,4},{8,9},{9,10},{10,1... | collective-permute-start | bytes 1572872 | tf_op jit(solution)/shard_map/ppermute | solution.py:228
  50.1 25.3 %collective-permute-start.3 = (bf16[128,2048]{1,0:T(8,128)(2,1)}, bf16[128,2048]{1,0:T(8,128)(2,1)S(1)}, u32[]{:S(2)}, u32[]{:S(2)}) collective-permute-start(bf16[128,2048]{1,0:T(8,128)(2,1)} %collective-permute-done.1), channel_id=1, source_target_pairs={{0,1},{1,2},{2,3},{3,0},{4,5},{5,6},{6,7},{7,4},{8,9},{9,10},{10,1... | collective-permute-start | bytes 1572872 | tf_op jit(solution)/shard_map/ppermute | solution.py:228
  64.2 22.5 %collective-permute-start.4 = (bf16[128,2048]{1,0:T(8,128)(2,1)S(1)}, bf16[128,2048]{1,0:T(8,128)(2,1)S(1)}, u32[]{:S(2)}, u32[]{:S(2)}) collective-permute-start(bf16[128,2048]{1,0:T(8,128)(2,1)S(1)} %collective-permute-done.2), channel_id=1, source_target_pairs={{0,1},{1,2},{2,3},{3,0},{4,5},{5,6},{6,7},{7,4},{8,9},{9,10},{10,1... | collective-permute-start | bytes 1572872 | tf_op jit(solution)/shard_map/ppermute | solution.py:228
  75.4 21.8 %collective-permute-start.5 = (bf16[128,2048]{1,0:T(8,128)(2,1)S(1)}, bf16[128,2048]{1,0:T(8,128)(2,1)S(1)}, u32[]{:S(2)}, u32[]{:S(2)}) collective-permute-start(bf16[128,2048]{1,0:T(8,128)(2,1)S(1)} %collective-permute-done.3), channel_id=1, source_target_pairs={{0,1},{1,2},{2,3},{3,0},{4,5},{5,6},{6,7},{7,4},{8,9},{9,10},{10,1... | collective-permute-start | bytes 1572872 | tf_op jit(solution)/shard_map/ppermute | solution.py:228
  97.3 26.3 %collective-permute-start.13 = (bf16[256,2048]{1,0:T(8,128)(2,1)S(1)}, bf16[256,2048]{1,0:T(8,128)(2,1)S(1)}, u32[]{:S(2)}, u32[]{:S(2)}) collective-permute-start(bf16[256,2048]{1,0:T(8,128)(2,1)S(1)} %convert_element_type.311.refs_1_), channel_id=1, source_target_pairs={{0,1},{1,2},{2,3},{3,0},{4,5},{5,6},{6,7},{7,4},{8,9},{9,10},{10,1... | collective-permute-start | bytes 3145736 | tf_op jit(solution)/shard_map/ppermute | solution.py:228
  123.6 25.6 %collective-permute-start.16 = (bf16[256,2048]{1,0:T(8,128)(2,1)S(1)}, bf16[256,2048]{1,0:T(8,128)(2,1)}, u32[]{:S(2)}, u32[]{:S(2)}) collective-permute-start(bf16[256,2048]{1,0:T(8,128)(2,1)S(1)} %collective-permute-done.13.refs_1_), channel_id=1, source_target_pairs={{0,1},{1,2},{2,3},{3,0},{4,5},{5,6},{6,7},{7,4},{8,9},{9,10},{10,1... | collective-permute-start | bytes 3145736 | tf_op jit(solution)/shard_map/ppermute | solution.py:228
  149.2 188.5 %collective-permute-start.19 = (bf16[256,2048]{1,0:T(8,128)(2,1)}, bf16[256,2048]{1,0:T(8,128)(2,1)}, u32[]{:S(2)}, u32[]{:S(2)}) collective-permute-start(bf16[256,2048]{1,0:T(8,128)(2,1)} %collective-permute-done.16.refs_1_), channel_id=1, source_target_pairs={{0,1},{1,2},{2,3},{3,0},{4,5},{5,6},{6,7},{7,4},{8,9},{9,10},{10,1... | collective-permute-start | bytes 3145736 | tf_op jit(solution)/shard_map/ppermute | solution.py:228
  193.8 53.1 %copy-start.47 = (bf16[1024,2,4,64]{0,3,2,1:T(8,128)(2,1)}, bf16[1024,2,4,64]{0,3,2,1:T(8,128)(2,1)S(1)}, u32[]{:S(2)}) copy-start(bf16[1024,2,4,64]{0,3,2,1:T(8,128)(2,1)S(1)} %pad_maximum_fusion.4) | copy-start | bytes 3145732
  196.4 16.6 %collective-permute-start.6 = (bf16[128,2048]{1,0:T(8,128)(2,1)S(1)}, bf16[128,2048]{1,0:T(8,128)(2,1)S(1)}, u32[]{:S(2)}, u32[]{:S(2)}) collective-permute-start(bf16[128,2048]{1,0:T(8,128)(2,1)S(1)} %convolution_convert_fusion.7), channel_id=1, source_target_pairs={{0,1},{1,2},{2,3},{3,0},{4,5},{5,6},{6,7},{7,4},{8,9},{9,10},{10,1... | collective-permute-start | bytes 1572872 | tf_op jit(solution)/shard_map/ppermute | solution.py:228
  197.0 27.3 %collective-permute-start.9 = (bf16[128,2048]{1,0:T(8,128)(2,1)S(1)}, bf16[128,2048]{1,0:T(8,128)(2,1)S(1)}, u32[]{:S(2)}, u32[]{:S(2)}) collective-permute-start(bf16[128,2048]{1,0:T(8,128)(2,1)S(1)} %convolution_convert_fusion.6), channel_id=1, source_target_pairs={{0,1},{1,2},{2,3},{3,0},{4,5},{5,6},{6,7},{7,4},{8,9},{9,10},{10,1... | collective-permute-start | bytes 1572872 | tf_op jit(solution)/shard_map/ppermute | solution.py:228
  213.5 22.0 %collective-permute-start.7 = (bf16[128,2048]{1,0:T(8,128)(2,1)S(1)}, bf16[128,2048]{1,0:T(8,128)(2,1)S(1)}, u32[]{:S(2)}, u32[]{:S(2)}) collective-permute-start(bf16[128,2048]{1,0:T(8,128)(2,1)S(1)} %add_convert_fusion.12), channel_id=1, source_target_pairs={{0,1},{1,2},{2,3},{3,0},{4,5},{5,6},{6,7},{7,4},{8,9},{9,10},{10,1... | collective-permute-start | bytes 1572872 | tf_op jit(solution)/shard_map/ppermute | solution.py:228
  224.7 22.0 %collective-permute-start.10 = (bf16[128,2048]{1,0:T(8,128)(2,1)S(1)}, bf16[128,2048]{1,0:T(8,128)(2,1)S(1)}, u32[]{:S(2)}, u32[]{:S(2)}) collective-permute-start(bf16[128,2048]{1,0:T(8,128)(2,1)S(1)} %add_convert_fusion.10), channel_id=1, source_target_pairs={{0,1},{1,2},{2,3},{3,0},{4,5},{5,6},{6,7},{7,4},{8,9},{9,10},{10,1... | collective-permute-start | bytes 1572872 | tf_op jit(solution)/shard_map/ppermute | solution.py:228
  235.6 22.4 %collective-permute-start.8 = (bf16[128,2048]{1,0:T(8,128)(2,1)S(1)}, bf16[128,2048]{1,0:T(8,128)(2,1)S(1)}, u32[]{:S(2)}, u32[]{:S(2)}) collective-permute-start(bf16[128,2048]{1,0:T(8,128)(2,1)S(1)} %add_convert_fusion.11), channel_id=1, source_target_pairs={{0,1},{1,2},{2,3},{3,0},{4,5},{5,6},{6,7},{7,4},{8,9},{9,10},{10,1... | collective-permute-start | bytes 1572872 | tf_op jit(solution)/shard_map/ppermute | solution.py:228
  246.8 19.2 %collective-permute-start.11 = (bf16[128,2048]{1,0:T(8,128)(2,1)S(1)}, bf16[128,2048]{1,0:T(8,128)(2,1)S(1)}, u32[]{:S(2)}, u32[]{:S(2)}) collective-permute-start(bf16[128,2048]{1,0:T(8,128)(2,1)S(1)} %add_convert_fusion.9), channel_id=1, source_target_pairs={{0,1},{1,2},{2,3},{3,0},{4,5},{5,6},{6,7},{7,4},{8,9},{9,10},{10,1... | collective-permute-start | bytes 1572872 | tf_op jit(solution)/shard_map/ppermute | solution.py:228
  268.0 24.1 %collective-permute-start.12 = (bf16[256,2048]{1,0:T(8,128)(2,1)}, bf16[256,2048]{1,0:T(8,128)(2,1)}, u32[]{:S(2)}, u32[]{:S(2)}) collective-permute-start(bf16[256,2048]{1,0:T(8,128)(2,1)} %multiply_convert_fusion.refs_0_), channel_id=1, source_target_pairs={{0,1},{1,2},{2,3},{3,0},{4,5},{5,6},{6,7},{7,4},{8,9},{9,10},{10,1... | collective-permute-start | bytes 3145736 | tf_op jit(solution)/shard_map/ppermute | solution.py:228
  292.1 23.3 %collective-permute-start.15 = (bf16[256,2048]{1,0:T(8,128)(2,1)}, bf16[256,2048]{1,0:T(8,128)(2,1)S(1)}, u32[]{:S(2)}, u32[]{:S(2)}) collective-permute-start(bf16[256,2048]{1,0:T(8,128)(2,1)} %collective-permute-done.12.refs_0_), channel_id=1, source_target_pairs={{0,1},{1,2},{2,3},{3,0},{4,5},{5,6},{6,7},{7,4},{8,9},{9,10},{10,1... | collective-permute-start | bytes 3145736 | tf_op jit(solution)/shard_map/ppermute | solution.py:228
  315.4 22.4 %collective-permute-start.18 = (bf16[256,2048]{1,0:T(8,128)(2,1)S(1)}, bf16[256,2048]{1,0:T(8,128)(2,1)S(1)}, u32[]{:S(2)}, u32[]{:S(2)}) collective-permute-start(bf16[256,2048]{1,0:T(8,128)(2,1)S(1)} %collective-permute-done.15.refs_0_), channel_id=1, source_target_pairs={{0,1},{1,2},{2,3},{3,0},{4,5},{5,6},{6,7},{7,4},{8,9},{9,10},{10,1... | collective-permute-start | bytes 3145736 | tf_op jit(solution)/shard_map/ppermute | solution.py:228
  384.0 279.1 %reduce-scatter.4.cloned.1.call-start = ((), (), s32[]{:S(2)}) async-start(), calls=%async_computation.5 | async-start | bytes 9437184 | tf_op jit(solution)/shard_map/reduce_scatter | solution.py:359
  384.1 48.2 %copy-start.12 = (f32[256,2048]{1,0:T(8,128)S(1)}, f32[256,2048]{1,0:T(8,128)}, u32[]{:S(2)}) copy-start(f32[256,2048]{1,0:T(8,128)} %copy-done.11) | copy-start | bytes 6291460
  386.0 23.0 %collective-permute-start.14 = (bf16[256,2048]{1,0:T(8,128)(2,1)S(1)}, bf16[256,2048]{1,0:T(8,128)(2,1)S(1)}, u32[]{:S(2)}, u32[]{:S(2)}) collective-permute-start(bf16[256,2048]{1,0:T(8,128)(2,1)S(1)} %convert_element_type.312), channel_id=1, source_target_pairs={{0,1},{1,2},{2,3},{3,0},{4,5},{5,6},{6,7},{7,4},{8,9},{9,10},{10,1... | collective-permute-start | bytes 3145736 | tf_op jit(solution)/shard_map/ppermute | solution.py:228
  409.3 43.2 %copy-start.20 = (bf16[256,2048]{1,0:T(8,128)(2,1)S(1)}, bf16[256,2048]{1,0:T(8,128)(2,1)}, u32[]{:S(2)}) copy-start(bf16[256,2048]{1,0:T(8,128)(2,1)} %param.10) | copy-start | bytes 3145732
  409.3 23.0 %collective-permute-start.17 = (bf16[256,2048]{1,0:T(8,128)(2,1)S(1)}, bf16[256,2048]{1,0:T(8,128)(2,1)S(1)}, u32[]{:S(2)}, u32[]{:S(2)}) collective-permute-start(bf16[256,2048]{1,0:T(8,128)(2,1)S(1)} %add_convert_fusion.3), channel_id=1, source_target_pairs={{0,1},{1,2},{2,3},{3,0},{4,5},{5,6},{6,7},{7,4},{8,9},{9,10},{10,1... | collective-permute-start | bytes 3145736 | tf_op jit(solution)/shard_map/ppermute | solution.py:228
  432.6 19.9 %collective-permute-start.20 = (bf16[256,2048]{1,0:T(8,128)(2,1)S(1)}, bf16[256,2048]{1,0:T(8,128)(2,1)S(1)}, u32[]{:S(2)}, u32[]{:S(2)}) collective-permute-start(bf16[256,2048]{1,0:T(8,128)(2,1)S(1)} %add_convert_fusion.2), channel_id=1, source_target_pairs={{0,1},{1,2},{2,3},{3,0},{4,5},{5,6},{6,7},{7,4},{8,9},{9,10},{10,1... | collective-permute-start | bytes 3145736 | tf_op jit(solution)/shard_map/ppermute | solution.py:228
  457.4 23.6 %collective-permute-start.21 = (bf16[256,2048]{1,0:T(8,128)(2,1)S(1)}, bf16[256,2048]{1,0:T(8,128)(2,1)}, u32[]{:S(2)}, u32[]{:S(2)}) collective-permute-start(bf16[256,2048]{1,0:T(8,128)(2,1)S(1)} %get-tuple-element.103), channel_id=1, source_target_pairs={{0,1},{1,2},{2,3},{3,0},{4,5},{5,6},{6,7},{7,4},{8,9},{9,10},{10,1... | collective-permute-start | bytes 3145736 | tf_op jit(solution)/shard_map/ppermute | solution.py:228
  481.0 23.3 %collective-permute-start.22 = (bf16[256,2048]{1,0:T(8,128)(2,1)}, bf16[256,2048]{1,0:T(8,128)(2,1)}, u32[]{:S(2)}, u32[]{:S(2)}) collective-permute-start(bf16[256,2048]{1,0:T(8,128)(2,1)} %collective-permute-done.21), channel_id=1, source_target_pairs={{0,1},{1,2},{2,3},{3,0},{4,5},{5,6},{6,7},{7,4},{8,9},{9,10},{10,1... | collective-permute-start | bytes 3145736 | tf_op jit(solution)/shard_map/ppermute | solution.py:228
  492.5 173.9 %reduce-scatter.8.cloned.1.call-start = ((), (), s32[]{:S(2)}) async-start(), calls=%async_computation.7 | async-start | bytes 5898240 | tf_op jit(solution)/shard_map/reduce_scatter | solution.py:431
  504.3 22.1 %collective-permute-start.23 = (bf16[256,2048]{1,0:T(8,128)(2,1)}, bf16[256,2048]{1,0:T(8,128)(2,1)}, u32[]{:S(2)}, u32[]{:S(2)}) collective-permute-start(bf16[256,2048]{1,0:T(8,128)(2,1)} %collective-permute-done.22), channel_id=1, source_target_pairs={{0,1},{1,2},{2,3},{3,0},{4,5},{5,6},{6,7},{7,4},{8,9},{9,10},{10,1... | collective-permute-start | bytes 3145736 | tf_op jit(solution)/shard_map/ppermute | solution.py:228
  527.4 21.9 %collective-permute-start.24 = (bf16[256,2048]{1,0:T(8,128)(2,1)}, bf16[256,2048]{1,0:T(8,128)(2,1)}, u32[]{:S(2)}, u32[]{:S(2)}) collective-permute-start(bf16[256,2048]{1,0:T(8,128)(2,1)} %convert_element_type.319), channel_id=1, source_target_pairs={{0,1},{1,2},{2,3},{3,0},{4,5},{5,6},{6,7},{7,4},{8,9},{9,10},{10,1... | collective-permute-start | bytes 3145736 | tf_op jit(solution)/shard_map/ppermute | solution.py:228
  550.9 23.3 %collective-permute-start.25 = (bf16[256,2048]{1,0:T(8,128)(2,1)S(1)}, bf16[256,2048]{1,0:T(8,128)(2,1)S(1)}, u32[]{:S(2)}, u32[]{:S(2)}) collective-permute-start(bf16[256,2048]{1,0:T(8,128)(2,1)S(1)} %add_convert_fusion.1), channel_id=1, source_target_pairs={{0,1},{1,2},{2,3},{3,0},{4,5},{5,6},{6,7},{7,4},{8,9},{9,10},{10,1... | collective-permute-start | bytes 3145736 | tf_op jit(solution)/shard_map/ppermute | solution.py:228
  590.0 16.7 %collective-permute-start.27 = (bf16[128,2048]{1,0:T(8,128)(2,1)S(1)}, bf16[128,2048]{1,0:T(8,128)(2,1)S(1)}, u32[]{:S(2)}, u32[]{:S(2)}) collective-permute-start(bf16[128,2048]{1,0:T(8,128)(2,1)S(1)} %convolution_convert_fusion.5), channel_id=1, source_target_pairs={{0,1},{1,2},{2,3},{3,0},{4,5},{5,6},{6,7},{7,4},{8,9},{9,10},{10,1... | collective-permute-start | bytes 1572872 | tf_op jit(solution)/shard_map/ppermute | solution.py:228
  593.4 24.5 %collective-permute-start.30 = (bf16[128,2048]{1,0:T(8,128)(2,1)S(1)}, bf16[128,2048]{1,0:T(8,128)(2,1)S(1)}, u32[]{:S(2)}, u32[]{:S(2)}) collective-permute-start(bf16[128,2048]{1,0:T(8,128)(2,1)S(1)} %convolution_convert_fusion.4), channel_id=1, source_target_pairs={{0,1},{1,2},{2,3},{3,0},{4,5},{5,6},{6,7},{7,4},{8,9},{9,10},{10,1... | collective-permute-start | bytes 1572872 | tf_op jit(solution)/shard_map/ppermute | solution.py:228
  607.8 21.3 %collective-permute-start.28 = (bf16[128,2048]{1,0:T(8,128)(2,1)S(1)}, bf16[128,2048]{1,0:T(8,128)(2,1)S(1)}, u32[]{:S(2)}, u32[]{:S(2)}) collective-permute-start(bf16[128,2048]{1,0:T(8,128)(2,1)S(1)} %add_convert_fusion.7), channel_id=1, source_target_pairs={{0,1},{1,2},{2,3},{3,0},{4,5},{5,6},{6,7},{7,4},{8,9},{9,10},{10,1... | collective-permute-start | bytes 1572872 | tf_op jit(solution)/shard_map/ppermute | solution.py:228
  619.1 16.7 %collective-permute-start.31 = (bf16[128,2048]{1,0:T(8,128)(2,1)S(1)}, bf16[128,2048]{1,0:T(8,128)(2,1)S(1)}, u32[]{:S(2)}, u32[]{:S(2)}) collective-permute-start(bf16[128,2048]{1,0:T(8,128)(2,1)S(1)} %add_convert_fusion.5), channel_id=1, source_target_pairs={{0,1},{1,2},{2,3},{3,0},{4,5},{5,6},{6,7},{7,4},{8,9},{9,10},{10,1... | collective-permute-start | bytes 1572872 | tf_op jit(solution)/shard_map/ppermute | solution.py:228
  630.3 11.1 %collective-permute-start.29 = (bf16[128,2048]{1,0:T(8,128)(2,1)S(1)}, bf16[128,2048]{1,0:T(8,128)(2,1)S(1)}, u32[]{:S(2)}, u32[]{:S(2)}) collective-permute-start(bf16[128,2048]{1,0:T(8,128)(2,1)S(1)} %add_convert_fusion.6), channel_id=1, source_target_pairs={{0,1},{1,2},{2,3},{3,0},{4,5},{5,6},{6,7},{7,4},{8,9},{9,10},{10,1... | collective-permute-start | bytes 1572872 | tf_op jit(solution)/shard_map/ppermute | solution.py:228
  637.0 11.3 %collective-permute-start.32 = (bf16[128,2048]{1,0:T(8,128)(2,1)S(1)}, bf16[128,2048]{1,0:T(8,128)(2,1)S(1)}, u32[]{:S(2)}, u32[]{:S(2)}) collective-permute-start(bf16[128,2048]{1,0:T(8,128)(2,1)S(1)} %add_convert_fusion.4), channel_id=1, source_target_pairs={{0,1},{1,2},{2,3},{3,0},{4,5},{5,6},{6,7},{7,4},{8,9},{9,10},{10,1... | collective-permute-start | bytes 1572872 | tf_op jit(solution)/shard_map/ppermute | solution.py:228
  663.1 17.6 %collective-permute-start.26 = (bf16[256,2048]{1,0:T(8,128)(2,1)}, bf16[256,2048]{1,0:T(8,128)(2,1)}, u32[]{:S(2)}, u32[]{:S(2)}) collective-permute-start(bf16[256,2048]{1,0:T(8,128)(2,1)} %add_convert_fusion), channel_id=1, source_target_pairs={{0,1},{1,2},{2,3},{3,0},{4,5},{5,6},{6,7},{7,4},{8,9},{9,10},{10,1... | collective-permute-start | bytes 3145736 | tf_op jit(solution)/shard_map/ppermute | solution.py:228
  668.6 11.4 %collective-permute-start.33 = (f32[2,256]{1,0:T(2,128)S(1)}, f32[2,256]{1,0:T(2,128)S(1)}, u32[]{:S(2)}, u32[]{:S(2)}) collective-permute-start(f32[2,256]{1,0:T(2,128)S(1)} %maximum_divide_fusion), channel_id=1, source_target_pairs={{0,1},{1,2},{2,3},{3,0},{4,5},{5,6},{6,7},{7,4},{8,9},{9,10},{10,1... | collective-permute-start | bytes 6152 | tf_op jit(solution)/shard_map/ppermute | solution.py:444
  668.7 11.4 %collective-permute-start.34 = (f32[2,256]{1,0:T(2,128)S(1)}, f32[2,256]{1,0:T(2,128)S(1)}, u32[]{:S(2)}, u32[]{:S(2)}) collective-permute-start(f32[2,256]{1,0:T(2,128)S(1)} %maximum_divide_fusion), channel_id=1, source_target_pairs={{0,2},{1,3},{2,0},{3,1},{4,6},{5,7},{6,4},{7,5},{8,10},{9,11},{10,... | collective-permute-start | bytes 6152 | tf_op jit(solution)/shard_map/ppermute | solution.py:444
  673.1 7.0 %collective-permute-start.35 = (f32[2,256]{1,0:T(2,128)S(1)}, f32[2,256]{1,0:T(2,128)S(1)}, u32[]{:S(2)}, u32[]{:S(2)}) collective-permute-start(f32[2,256]{1,0:T(2,128)S(1)} %maximum_divide_fusion), channel_id=1, source_target_pairs={{0,3},{1,0},{2,1},{3,2},{4,7},{5,4},{6,5},{7,6},{8,11},{9,8},{10,9... | collective-permute-start | bytes 6152 | tf_op jit(solution)/shard_map/ppermute | solution.py:444
  (77 other events, 519.9 us)
Sparse Core Ops, SparseCore 0:
  10.8 34.8 all-gather.5
  47.6 28.0 all-gather.9
  77.7 125.2 all-gather.7
  384.1 116.2 reduce-scatter.5
  503.8 71.4 reduce-scatter.3
  586.1 57.4 reduce-scatter.7

commit v6 on v5

--- a/solution.py
+++ b/solution.py
@@ -111,7 +111,7 @@
 
 def mlp_kernel(reused, *refs):
     x_ref, g_ref, w_ref = refs[:3]
-    hidden_ref, dgu_ref, x_all_ref, g_all_ref, back_ref, out_ref = refs[3 + reused :]
+    right_ref, left_ref, back_ref, out_ref = refs[3 + reused :]
     first = pl.program_id(0) == 0
     dims = (((1,), (1,)), ((), ()))
     x = x_ref[...]
@@ -119,7 +119,6 @@
     w_gate = w_ref[0]
     w_up = w_ref[1]
     w_down = w_ref[2]
-    tile = w_down.shape[1]
     gate = jnp.dot(x, w_gate, preferred_element_type=jnp.float32)
     up = jnp.dot(x, w_up, preferred_element_type=jnp.float32)
     grad_hidden = jnp.dot(g, w_down, preferred_element_type=jnp.float32)
@@ -130,14 +129,15 @@
         jnp.bfloat16
     )
     dup = (grad_hidden * silu_gate).astype(jnp.bfloat16)
-    hidden_ref[...] = hidden
-    dgu_ref[:, :tile] = dgate
-    dgu_ref[:, tile:] = dup
+    right_ref[0] = hidden
+    right_ref[1] = dgate
+    right_ref[2] = dup
 
     @pl.when(first)
     def _():
-        x_all_ref[...] = x
-        g_all_ref[...] = g
+        left_ref[0] = g
+        left_ref[1] = x
+        left_ref[2] = x
         out_ref[...] = jnp.zeros_like(out_ref)
         back_ref[...] = jnp.zeros_like(back_ref)
 
@@ -147,35 +147,29 @@
     ) + lax.dot_general(dup, w_up, dims, preferred_element_type=jnp.float32)
 
 
-def mlp_tile(hidden_width):
-    return min(512, hidden_width)
-
-
 def mlp_block(step, ring, x, g, w_mlp, kept):
     rows, width = x.shape
     hidden_width = w_mlp.shape[2]
-    tile = mlp_tile(hidden_width)
+    tile = min(512, hidden_width)
     bf16, f32 = jnp.bfloat16, jnp.float32
-    wide = jax.ShapeDtypeStruct((ring * rows, hidden_width), bf16)
-    pair = jax.ShapeDtypeStruct((ring * rows, 2 * hidden_width), bf16)
-    whole = jax.ShapeDtypeStruct((ring * rows, width), bf16)
+    right = jax.ShapeDtypeStruct((3, ring * rows, hidden_width), bf16)
+    left = jax.ShapeDtypeStruct((3, ring * rows, width), bf16)
     part = jax.ShapeDtypeStruct((rows, width), f32)
-    wide_spec = pl.BlockSpec((rows, tile), lambda t: (step, t))
-    pair_spec = pl.BlockSpec((rows, 2 * tile), lambda t: (step, t))
-    whole_spec = pl.BlockSpec((rows, width), lambda t: (step, 0))
+    right_spec = pl.BlockSpec((3, rows, tile), lambda t: (0, step, t))
+    left_spec = pl.BlockSpec((3, rows, width), lambda t: (0, step, 0))
     block_spec = pl.BlockSpec((rows, width), lambda t: (0, 0))
     reused = len(kept)
     return pl.pallas_call(
         functools.partial(mlp_kernel, reused),
         grid=(hidden_width // tile,),
-        out_shape=(wide, pair, whole, whole, part, part),
+        out_shape=(right, left, part, part),
         in_specs=[
             block_spec,
             block_spec,
             pl.BlockSpec((3, width, tile), lambda t: (0, 0, t)),
         ]
         + [pl.BlockSpec(memory_space=pl.ANY)] * reused,
-        out_specs=(wide_spec, pair_spec, whole_spec, whole_spec, block_spec, block_spec),
+        out_specs=(right_spec, left_spec, block_spec, block_spec),
         input_output_aliases={3 + i: i for i in range(reused)},
         cost_estimate=pl.CostEstimate(
             flops=12 * rows * width * hidden_width,
@@ -352,16 +346,15 @@
         )
         back_parts.append(back_part)
         out_parts.append(out_part)
-    hidden_all, dgu_all, normed_mlp_all, grad_all = kept
+    right_rows, left_rows = kept
     grad_normed_mlp = collect(back_parts)
-    grad_down = dot_tn(grad_all, hidden_all).astype(bf16)
-    grad_wgu = dot_tn(normed_mlp_all, dgu_all).astype(bf16)
-    grad_down = lax.psum_scatter(grad_down, "fsdp", scatter_dimension=0, tiled=True)
-    grad_wgu = lax.psum_scatter(grad_wgu, "fsdp", scatter_dimension=0, tiled=True)
-    grad_down = jnp.swapaxes(grad_down.astype(f32), 0, 1)
-    tile = mlp_tile(w_mlp.shape[2])
-    grad_wgu = grad_wgu.astype(f32).reshape(grad_wgu.shape[0], -1, 2, tile)
-    grad_wgu = jnp.swapaxes(grad_wgu, 1, 2).reshape(grad_wgu.shape[0], 2, -1)
+    grad_mlp = lax.dot_general(
+        left_rows, right_rows, (((1,), (1,)), ((0,), (0,))), preferred_element_type=f32
+    ).astype(bf16)
+    grad_mlp = lax.psum_scatter(grad_mlp, "fsdp", scatter_dimension=1, tiled=True)
+    grad_mlp = grad_mlp.astype(f32)
+    grad_down = jnp.swapaxes(grad_mlp[0], 0, 1)
+    grad_wgu = jnp.swapaxes(grad_mlp[1:], 0, 1)
     gain_mlp_part = jnp.sum(grad_wgu * w_gate_up[0].astype(f32), axis=(1, 2))
     norm_part, _ = norm_back(middle, inv_mlp, gains_all[1], grad_normed_mlp)
     grad_middle = out_cotangent + norm_part
@@ -432,7 +425,7 @@
         jnp.concatenate([grad_wqkv, grad_wo], axis=1),
         "fsdp", scatter_dimension=0, tiled=True,
     )
-    packed = packed.astype(f32)
+    packed = after(packed, (grad_rows, output_rows)).astype(f32)
     qkv_width = grad_wqkv.shape[1]
     grad_wq = packed[:, :query_width]
     grad_wkv = packed[:, query_width:qkv_width].reshape(-1, kv_local, 2 * head_size)

time: 702 us -> 722 us (1.028)
  waiting for transfers between devices: 301 us -> 322 us
  Pallas kernels: 74.9 us -> 82.7 us
    dot_general x4 -> x2, matrix products: 46.9 us -> 10.5 us  [dot_tn(): lax.dot_general(a, b, (((0,), (0,)), ((), ())), preferred_element_type=f32)]
    dot_general x0 -> x1, matrix products: none -> 35.8 us  [per_device(): lax.dot_general(left_rows, right_rows, (((1,), (1,)), ((0,), (0,))), pref...]
    ppermute x33, waiting for transfers between devices: 298 us -> 321 us  [shift(): return lax.ppermute(rows, 'tensor', ring_pairs)]
    pallas_call x4, Pallas kernels: 74.9 us -> 82.7 us  [mlp_block(): pl.pallas_call(functools.partial(mlp_kernel, reused), grid=(hidden_width...]
    unnamed x166 -> x158, local copies, waits for them, and re-layouts: 31.1 us -> 37 us
  transfers between devices with their start and end apart: 42 -> 41, of which waited for: 30 -> 28; matrix products, arithmetic and copies ran while one was open for 31% -> 28% of each run, Pallas kernels for 8% -> 9%
where the time goes in v6:
time: 722 us; the launch traced here: 715 us
  waiting for transfers between devices  322 us (45%)
  matrix products  136 us (19%)
  Pallas kernels  82.7 us (11%)
  other arithmetic  65 us (9%)
  local copies, waits for them, and re-layouts  61.1 us (8%)
  starting transfers between devices  23.8 us (3%)
  between operations  15.4 us (2%)
  blocking collectives  8.95 us (1%)
    ppermute x33, waiting for transfers between devices, shift(): return lax.ppermute(rows, 'tensor', ring_pairs)  321 us
    pallas_call x4, Pallas kernels, mlp_block(): pl.pallas_call(functools.partial(mlp_kernel, reused), grid=(hidden_width...  82.7 us
    unnamed x158, local copies, waits for them, and re-layouts  37 us
    dot_general x1, matrix products, per_device(): lax.dot_general(left_rows, right_rows, (((1,), (1,)), ((0,), (0,))), pref...  35.8 us
    ppermute x33, starting transfers between devices, shift(): return lax.ppermute(rows, 'tensor', ring_pairs)  19.8 us
    dot_general x12, matrix products, dot_nt(): lax.dot_general(a, b, (((1,), (1,)), ((), ())), preferred_element_type=f32)  19.7 us
  transfers between devices with their start and end apart: 41, of which 28 were waited for; matrix products, arithmetic and copies ran while one was open for 28% of the time, Pallas kernels for 9%

profile of v6, /device:TPU:0, one launch (start us, length us, event | category | flops | bytes accessed | tf_op | source)
XLA Modules:
  0.0 715.3 jit_solution(15452294159294322786)
XLA Ops:
  19.5 3.1 collective-permute-start
  24.8 8.9 %all-gather = bf16[1,2,2048]{2,1,0:T(2,128)(2,1)S(1)} all-gather(bf16[1,2,256]{2,1,0:T(2,128)(2,1)S(1)} %copy-done.72), channel_id=2, replica_groups=mesh['fsdp'=8,'tensor'=4] {'fsdp'}, dimensions={2}, use_global_device_ids=true | all-gather | bytes 9216 | tf_op jit(solution)/shard_map/all_gather | solution.py:279
  54.6 7.6 %collective-permute-done.2 = bf16[128,2048]{1,0:T(8,128)(2,1)S(1)} collective-permute-done((bf16[128,2048]{1,0:T(8,128)(2,1)}, bf16[128,2048]{1,0:T(8,128)(2,1)S(1)}, u32[]{:S(2)}, u32[]{:S(2)}) %collective-permute-start.2) | collective-permute-done | bytes 524320 | tf_op jit(solution)/shard_map/ppermute | solution.py:222
  62.2 11.2 %collective-permute-done.3 = bf16[128,2048]{1,0:T(8,128)(2,1)S(1)} collective-permute-done((bf16[128,2048]{1,0:T(8,128)(2,1)}, bf16[128,2048]{1,0:T(8,128)(2,1)S(1)}, u32[]{:S(2)}, u32[]{:S(2)}) %collective-permute-start.3) | collective-permute-done | bytes 524320 | tf_op jit(solution)/shard_map/ppermute | solution.py:222
  74.8 9.9 %collective-permute-done.4 = bf16[128,2048]{1,0:T(8,128)(2,1)S(1)} collective-permute-done((bf16[128,2048]{1,0:T(8,128)(2,1)S(1)}, bf16[128,2048]{1,0:T(8,128)(2,1)S(1)}, u32[]{:S(2)}, u32[]{:S(2)}) %collective-permute-start.4) | collective-permute-done | bytes 524320 | tf_op jit(solution)/shard_map/ppermute | solution.py:222
  84.7 10.6 %collective-permute-done.5 = bf16[128,2048]{1,0:T(8,128)(2,1)S(1)} collective-permute-done((bf16[128,2048]{1,0:T(8,128)(2,1)S(1)}, bf16[128,2048]{1,0:T(8,128)(2,1)S(1)}, u32[]{:S(2)}, u32[]{:S(2)}) %collective-permute-start.5) | collective-permute-done | bytes 524320 | tf_op jit(solution)/shard_map/ppermute | solution.py:222
  96.7 25.0 %collective-permute-done.13.refs_1_ = bf16[256,2048]{1,0:T(8,128)(2,1)S(1)} collective-permute-done((bf16[256,2048]{1,0:T(8,128)(2,1)S(1)}, bf16[256,2048]{1,0:T(8,128)(2,1)S(1)}, u32[]{:S(2)}, u32[]{:S(2)}) %collective-permute-start.13) | collective-permute-done | bytes 1048608 | tf_op jit(solution)/shard_map/ppermute | solution.py:222
  124.6 22.6 %collective-permute-done.16.refs_1_ = bf16[256,2048]{1,0:T(8,128)(2,1)} collective-permute-done((bf16[256,2048]{1,0:T(8,128)(2,1)S(1)}, bf16[256,2048]{1,0:T(8,128)(2,1)}, u32[]{:S(2)}, u32[]{:S(2)}) %collective-permute-start.16) | collective-permute-done | bytes 1048608 | tf_op jit(solution)/shard_map/ppermute | solution.py:222
  147.7 6.2 fusion.193
  162.6 3.1 convolution_convert_fusion.7
  165.7 7.4 %fusion.5 = (f32[2,4,512]{2,1,0:T(4,128)S(1)}, f32[2,1024,512,4]{2,1,3,0:T(8,128)}) fusion(pred[512,1024]{0,1:T(8,128)(4,1)S(1)} %fusion.47, bf16[512,2,4,64]{0,3,2,1:T(8,128)(2,1)S(1)} %pad_maximum_fusion.6, bf16[1024,2,64]{0,2,1:T(8,128)(2,1)S(1)} %pad_maximum_fusion.9), kind=kOutput, calls=%fused_computation.11 | convolution fusion | flops 549449728 | bytes 18104320 | tf_op jit(solution)/shard_map/qkgd,skd->kgqs/dot_general | solution.py:68
  173.1 9.4 %exponential_reduce_fusion = f32[2,4,512]{2,1,0:T(4,128)S(1)} fusion(f32[2,1024,512,4]{2,1,3,0:T(8,128)} %get-tuple-element.119, f32[2,4,512]{2,1,0:T(4,128)S(1)} %get-tuple-element.118, pred[512,1024]{0,1:T(8,128)(4,1)S(1)} %fusion.47), kind=kLoop, calls=%fused_computation.9 | loop fusion | flops 16773120 | bytes 17334272 | tf_op jit(solution)/shard_map/reduce_sum | solution.py:73
  182.6 8.5 %fusion.48 = bf16[2,64,4,512]{3,1,2,0:T(8,128)(2,1)S(1)} fusion(f32[2,1024,512,4]{2,1,3,0:T(8,128)} %get-tuple-element.119, f32[2,4,512]{2,1,0:T(4,128)S(1)} %bitcast.325, pred[512,1024]{0,1:T(8,128)(4,1)S(1)} %fusion.47, bf16[1024,2,64]{0,2,1:T(8,128)(2,1)S(1)} %slice-done.3), kind=kOutput, calls=%fused_computation.106 | convolution fusion | flops 553910272 | bytes 18104320 | tf_op jit(solution)/shard_map/kgqs,skd->qkgd/dot_general | solution.py:75
  196.9 14.3 %collective-permute-done.6 = bf16[128,2048]{1,0:T(8,128)(2,1)S(1)} collective-permute-done((bf16[128,2048]{1,0:T(8,128)(2,1)S(1)}, bf16[128,2048]{1,0:T(8,128)(2,1)S(1)}, u32[]{:S(2)}, u32[]{:S(2)}) %collective-permute-start.6) | collective-permute-done | bytes 524320 | tf_op jit(solution)/shard_map/ppermute | solution.py:222
  211.7 10.7 %collective-permute-done.9 = bf16[128,2048]{1,0:T(8,128)(2,1)S(1)} collective-permute-done((bf16[128,2048]{1,0:T(8,128)(2,1)S(1)}, bf16[128,2048]{1,0:T(8,128)(2,1)S(1)}, u32[]{:S(2)}, u32[]{:S(2)}) %collective-permute-start.9) | collective-permute-done | bytes 524320 | tf_op jit(solution)/shard_map/ppermute | solution.py:222
  223.5 10.2 %collective-permute-done.7 = bf16[128,2048]{1,0:T(8,128)(2,1)S(1)} collective-permute-done((bf16[128,2048]{1,0:T(8,128)(2,1)S(1)}, bf16[128,2048]{1,0:T(8,128)(2,1)S(1)}, u32[]{:S(2)}, u32[]{:S(2)}) %collective-permute-start.7) | collective-permute-done | bytes 524320 | tf_op jit(solution)/shard_map/ppermute | solution.py:222
  233.8 11.1 %collective-permute-done.10 = bf16[128,2048]{1,0:T(8,128)(2,1)S(1)} collective-permute-done((bf16[128,2048]{1,0:T(8,128)(2,1)S(1)}, bf16[128,2048]{1,0:T(8,128)(2,1)S(1)}, u32[]{:S(2)}, u32[]{:S(2)}) %collective-permute-start.10) | collective-permute-done | bytes 524320 | tf_op jit(solution)/shard_map/ppermute | solution.py:222
  245.6 10.5 %collective-permute-done.8 = bf16[128,2048]{1,0:T(8,128)(2,1)S(1)} collective-permute-done((bf16[128,2048]{1,0:T(8,128)(2,1)S(1)}, bf16[128,2048]{1,0:T(8,128)(2,1)S(1)}, u32[]{:S(2)}, u32[]{:S(2)}) %collective-permute-start.8) | collective-permute-done | bytes 524320 | tf_op jit(solution)/shard_map/ppermute | solution.py:222
  256.3 8.1 %collective-permute-done.11 = bf16[128,2048]{1,0:T(8,128)(2,1)S(1)} collective-permute-done((bf16[128,2048]{1,0:T(8,128)(2,1)S(1)}, bf16[128,2048]{1,0:T(8,128)(2,1)S(1)}, u32[]{:S(2)}, u32[]{:S(2)}) %collective-permute-start.11) | collective-permute-done | bytes 524320 | tf_op jit(solution)/shard_map/ppermute | solution.py:222
  266.3 20.8 %mlp_block.4 = (bf16[3,1024,2048]{2,1,0:T(8,128)(2,1)}, bf16[3,1024,2048]{2,1,0:T(8,128)(2,1)}, f32[256,2048]{1,0:T(8,128)S(1)}, f32[256,2048]{1,0:T(8,128)S(1)}) custom-call(bf16[256,2048]{1,0:T(8,128)(2,1)} %multiply_convert_fusion.refs_0_, bf16[256,2048]{1,0:T(8,128)(2,1)S(1)} %convert_element_type.308.refs_1_, ...), custom_call_target="tpu_custom_call" | custom-call | flops 12884901888 | bytes 31457280 | tf_op jit(solution)/shard_map/mlp_block/pallas_call | solution.py:162
  291.7 20.6 %mlp_block.5 = (bf16[3,1024,2048]{2,1,0:T(8,128)(2,1)}, bf16[3,1024,2048]{2,1,0:T(8,128)(2,1)}, f32[256,2048]{1,0:T(8,128)S(1)}, f32[256,2048]{1,0:T(8,128)S(1)}) custom-call(bf16[256,2048]{1,0:T(8,128)(2,1)} %collective-permute-done.12.refs_0_, bf16[256,2048]{1,0:T(8,128)(2,1)S(1)} %copy-done.14, ...), custom_call_target="tpu_custom_call", output_to_operand_aliasing={{0}: (3, {}), {1}: (4, {})} | custom-call | flops 12884901888 | bytes 31457280 | tf_op jit(solution)/shard_map/mlp_block/pallas_call | solution.py:162
  315.5 20.6 %mlp_block.6 = (bf16[3,1024,2048]{2,1,0:T(8,128)(2,1)}, bf16[3,1024,2048]{2,1,0:T(8,128)(2,1)}, f32[256,2048]{1,0:T(8,128)S(1)}, f32[256,2048]{1,0:T(8,128)S(1)}) custom-call(bf16[256,2048]{1,0:T(8,128)(2,1)S(1)} %collective-permute-done.15.refs_0_, bf16[256,2048]{1,0:T(8,128)(2,1)} %collective-permute-done.16.refs_1_, ...), custom_call_target="tpu_custom_call", output_to_operand_aliasing={{0}: (3, {}), {1}: (4, {})} | custom-call | flops 12884901888 | bytes 31457280 | tf_op jit(solution)/shard_map/mlp_block/pallas_call | solution.py:162
  338.9 20.7 %mlp_block.7 = (bf16[3,1024,2048]{2,1,0:T(8,128)(2,1)}, bf16[3,1024,2048]{2,1,0:T(8,128)(2,1)}, f32[256,2048]{1,0:T(8,128)S(1)}, f32[256,2048]{1,0:T(8,128)S(1)}) custom-call(bf16[256,2048]{1,0:T(8,128)(2,1)S(1)} %collective-permute-done.18.refs_0_, bf16[256,2048]{1,0:T(8,128)(2,1)} %collective-permute-done.19.refs_1_, ...), custom_call_target="tpu_custom_call", output_to_operand_aliasing={{0}: (3, {}), {1}: (4, {})} | custom-call | flops 12884901888 | bytes 31457280 | tf_op jit(solution)/shard_map/mlp_block/pallas_call | solution.py:162
  362.2 35.8 %convolution_convert_fusion = bf16[3,2048,2048]{2,1,0:T(8,128)(2,1)} fusion(bf16[3,1024,2048]{2,1,0:T(8,128)(2,1)} %get-tuple-element.62, bf16[3,1024,2048]{2,1,0:T(8,128)(2,1)} %get-tuple-element.63), kind=kOutput, calls=%fused_computation.10 | convolution fusion | flops 25782386688 | bytes 50331648 | tf_op jit(solution)/shard_map/dot_general | solution.py:351
  402.3 20.7 %collective-permute-done.14 = bf16[256,2048]{1,0:T(8,128)(2,1)S(1)} collective-permute-done((bf16[256,2048]{1,0:T(8,128)(2,1)S(1)}, bf16[256,2048]{1,0:T(8,128)(2,1)S(1)}, u32[]{:S(2)}, u32[]{:S(2)}) %collective-permute-start.14) | collective-permute-done | bytes 1048608 | tf_op jit(solution)/shard_map/ppermute | solution.py:222
  425.6 20.7 %collective-permute-done.17 = bf16[256,2048]{1,0:T(8,128)(2,1)S(1)} collective-permute-done((bf16[256,2048]{1,0:T(8,128)(2,1)S(1)}, bf16[256,2048]{1,0:T(8,128)(2,1)S(1)}, u32[]{:S(2)}, u32[]{:S(2)}) %collective-permute-start.17) | collective-permute-done | bytes 1048608 | tf_op jit(solution)/shard_map/ppermute | solution.py:222
  448.9 18.8 %collective-permute-done.20 = bf16[256,2048]{1,0:T(8,128)(2,1)S(1)} collective-permute-done((bf16[256,2048]{1,0:T(8,128)(2,1)S(1)}, bf16[256,2048]{1,0:T(8,128)(2,1)S(1)}, u32[]{:S(2)}, u32[]{:S(2)}) %collective-permute-start.20) | collective-permute-done | bytes 1048608 | tf_op jit(solution)/shard_map/ppermute | solution.py:222
  473.4 22.2 %collective-permute-done.21 = bf16[256,2048]{1,0:T(8,128)(2,1)} collective-permute-done((bf16[256,2048]{1,0:T(8,128)(2,1)S(1)}, bf16[256,2048]{1,0:T(8,128)(2,1)}, u32[]{:S(2)}, u32[]{:S(2)}) %collective-permute-start.21) | collective-permute-done | bytes 1048608 | tf_op jit(solution)/shard_map/ppermute | solution.py:222
  496.0 8.2 %fusion.113 = f32[2,1024,512,4]{2,1,3,0:T(8,128)} fusion(bf16[512,2,4,64]{0,3,2,1:T(8,128)(2,1)S(1)} %copy-done.34, bf16[1024,2,32]{0,2,1:T(8,128)(2,1)S(1)} %copy-done.50, bf16[1024,2,32]{0,2,1:T(8,128)(2,1)S(1)} %copy-done.48), kind=kOutput, calls=%fused_computation.196 | convolution fusion | flops 537395200 | bytes 17563648 | tf_op jit(solution)/shard_map/qkgd,skd->kgqs/dot_general | solution.py:85
  510.9 8.2 %collective-permute-done.22 = bf16[256,2048]{1,0:T(8,128)(2,1)} collective-permute-done((bf16[256,2048]{1,0:T(8,128)(2,1)}, bf16[256,2048]{1,0:T(8,128)(2,1)}, u32[]{:S(2)}, u32[]{:S(2)}) %collective-permute-start.22) | collective-permute-done | bytes 1048608 | tf_op jit(solution)/shard_map/ppermute | solution.py:222
  521.7 3.5 fusion.62
  530.5 10.8 %collective-permute-done.23 = bf16[256,2048]{1,0:T(8,128)(2,1)} collective-permute-done((bf16[256,2048]{1,0:T(8,128)(2,1)}, bf16[256,2048]{1,0:T(8,128)(2,1)}, u32[]{:S(2)}, u32[]{:S(2)}) %collective-permute-start.23) | collective-permute-done | bytes 1048608 | tf_op jit(solution)/shard_map/ppermute | solution.py:222
  547.8 4.7 convolution_convert_fusion.2
  552.7 3.2 fusion.9
  560.4 3.7 collective-permute-done.24
  566.4 9.4 %fusion.2 = bf16[2,4,512,1024]{2,3,1,0:T(8,128)(2,1)S(1)} fusion(f32[2,1024,512,4]{2,1,3,0:T(8,128)} %fusion.113, f32[2,4,512]{2,1,0:T(4,128)S(1)} %fusion.96, f32[2,4,512]{2,1,0:T(4,128)S(1)} %bitcast.326, pred[512,1024]{0,1:T(8,128)(4,1)S(1)} %copy-done.37, bf16[512,2,4,64]{0,3,2,1:T(8,128)(2,1)S(1)} %bitcast.295, bf16[1024,2,128]{0,2,1:T(8,128)(2,1)S(1)} %copy-done.58), kind=kOutput, calls=%fused_computation.3 | convolution fusion | flops 566231040 | bytes 26509312 | tf_op jit(solution)/shard_map/qkgd,skd->kgqs/dot_general | solution.py:91
  578.6 8.4 %fusion.68 = bf16[1024,2,64]{0,2,1:T(8,128)(2,1)S(1)} fusion(bf16[512,2,4,64]{0,3,2,1:T(8,128)(2,1)S(1)} %bitcast.296, f32[2,1024,512,4]{2,1,3,0:T(8,128)} %fusion.113, f32[2,4,512]{2,1,0:T(4,128)S(1)} %bitcast.327, pred[512,1024]{0,1:T(8,128)(4,1)S(1)} %copy-done.37, f32[512,2,64]{0,2,1:T(8,128)S(1)} %convolution_bitcast_fusion.3), kind=kOutput, calls=%fused_computation.116 | convolution fusion | flops 553910272 | bytes 18366464 | tf_op jit(solution)/shard_map/kgqs,qkgd->skd/dot_general | solution.py:103
  592.4 5.8 convolution_convert_fusion.1
  608.2 13.5 %collective-permute-done.27 = bf16[128,2048]{1,0:T(8,128)(2,1)S(1)} collective-permute-done((bf16[128,2048]{1,0:T(8,128)(2,1)S(1)}, bf16[128,2048]{1,0:T(8,128)(2,1)S(1)}, u32[]{:S(2)}, u32[]{:S(2)}) %collective-permute-start.27) | collective-permute-done | bytes 524320 | tf_op jit(solution)/shard_map/ppermute | solution.py:222
  622.9 10.0 %collective-permute-done.30 = bf16[128,2048]{1,0:T(8,128)(2,1)S(1)} collective-permute-done((bf16[128,2048]{1,0:T(8,128)(2,1)S(1)}, bf16[128,2048]{1,0:T(8,128)(2,1)S(1)}, u32[]{:S(2)}, u32[]{:S(2)}) %collective-permute-start.30) | collective-permute-done | bytes 524320 | tf_op jit(solution)/shard_map/ppermute | solution.py:222
  634.2 10.0 %collective-permute-done.28 = bf16[128,2048]{1,0:T(8,128)(2,1)S(1)} collective-permute-done((bf16[128,2048]{1,0:T(8,128)(2,1)S(1)}, bf16[128,2048]{1,0:T(8,128)(2,1)S(1)}, u32[]{:S(2)}, u32[]{:S(2)}) %collective-permute-start.28) | collective-permute-done | bytes 524320 | tf_op jit(solution)/shard_map/ppermute | solution.py:222
  645.4 6.1 collective-permute-done.31
  653.0 4.2 collective-permute-done.29
  658.4 10.4 %collective-permute-done.32 = bf16[128,2048]{1,0:T(8,128)(2,1)S(1)} collective-permute-done((bf16[128,2048]{1,0:T(8,128)(2,1)S(1)}, bf16[128,2048]{1,0:T(8,128)(2,1)S(1)}, u32[]{:S(2)}, u32[]{:S(2)}) %collective-permute-start.32) | collective-permute-done | bytes 524320 | tf_op jit(solution)/shard_map/ppermute | solution.py:222
  675.9 5.3 copy.66
  685.7 6.7 collective-permute-done.26
  692.4 6.6 fusion.23
  700.5 3.7 collective-permute-start.35
  (354 shorter events, 158.1 us)
Async XLA Ops:
  7.2 140.5 %all-gather.6.cloned.1.call-start = ((), (), s32[]{:S(2)}) async-start(), calls=%async_computation.2 | async-start | bytes 3538944 | tf_op jit(solution)/shard_map/all_gather | solution.py:278
  10.5 181.5 %all-gather.10.cloned.1.call-start = ((), (), s32[]{:S(2)}) async-start(), calls=%async_computation.6 | async-start | bytes 2359296 | tf_op jit(solution)/shard_map/all_gather | solution.py:280
  11.3 255.0 %all-gather.8.cloned.1.call-start = ((), (), s32[]{:S(2)}) async-start(), calls=%async_computation.3 | async-start | bytes 28311552 | tf_op jit(solution)/shard_map/all_gather | solution.py:281
  17.5 654.1 %reduce-scatter.3.cloned.1.call-start = ((), (), s32[]{:S(2)}) async-start(), calls=%async_computation.4 | async-start | bytes 28311552 | tf_op jit(solution)/shard_map/reduce_scatter | solution.py:354
  19.5 25.9 %collective-permute-start = (bf16[128,2048]{1,0:T(8,128)(2,1)}, bf16[128,2048]{1,0:T(8,128)(2,1)}, u32[]{:S(2)}, u32[]{:S(2)}) collective-permute-start(bf16[128,2048]{1,0:T(8,128)(2,1)} %get-tuple-element.39), channel_id=1, source_target_pairs={{0,1},{1,2},{2,3},{3,0},{4,5},{5,6},{6,7},{7,4},{8,9},{9,10},{10,1... | collective-permute-start | bytes 1572872 | tf_op jit(solution)/shard_map/ppermute | solution.py:222
  22.6 25.5 %collective-permute-start.1 = (bf16[128,2048]{1,0:T(8,128)(2,1)S(1)}, bf16[128,2048]{1,0:T(8,128)(2,1)}, u32[]{:S(2)}, u32[]{:S(2)}) collective-permute-start(bf16[128,2048]{1,0:T(8,128)(2,1)S(1)} %get-tuple-element.40), channel_id=1, source_target_pairs={{0,1},{1,2},{2,3},{3,0},{4,5},{5,6},{6,7},{7,4},{8,9},{9,10},{10,1... | collective-permute-start | bytes 1572872 | tf_op jit(solution)/shard_map/ppermute | solution.py:222
  37.5 118.3 %copy-start.51 = (f32[1024,32]{0,1:T(8,128)}, f32[1024,32]{0,1:T(8,128)S(1)}, u32[]{:S(2)}) copy-start(f32[1024,32]{0,1:T(8,128)S(1)} %get-tuple-element.113) | copy-start | bytes 393220
  38.0 144.6 %copy-start.36 = (pred[512,1024]{0,1:T(8,128)(4,1)}, pred[512,1024]{0,1:T(8,128)(4,1)S(1)}, u32[]{:S(2)}) copy-start(pred[512,1024]{0,1:T(8,128)(4,1)S(1)} %fusion.47) | copy-start | bytes 1572868
  38.0 85.6 %copy-start.65 = (f32[1,1,2048]{2,1,0:T(1,128)}, f32[1,1,2048]{2,1,0:T(1,128)S(1)}, u32[]{:S(2)}) copy-start(f32[1,1,2048]{2,1,0:T(1,128)S(1)} %get-tuple-element.109) | copy-start | bytes 24580
  45.4 16.8 %collective-permute-start.2 = (bf16[128,2048]{1,0:T(8,128)(2,1)}, bf16[128,2048]{1,0:T(8,128)(2,1)S(1)}, u32[]{:S(2)}, u32[]{:S(2)}) collective-permute-start(bf16[128,2048]{1,0:T(8,128)(2,1)} %collective-permute-done), channel_id=1, source_target_pairs={{0,1},{1,2},{2,3},{3,0},{4,5},{5,6},{6,7},{7,4},{8,9},{9,10},{10,1... | collective-permute-start | bytes 1572872 | tf_op jit(solution)/shard_map/ppermute | solution.py:222
  48.1 25.4 %collective-permute-start.3 = (bf16[128,2048]{1,0:T(8,128)(2,1)}, bf16[128,2048]{1,0:T(8,128)(2,1)S(1)}, u32[]{:S(2)}, u32[]{:S(2)}) collective-permute-start(bf16[128,2048]{1,0:T(8,128)(2,1)} %collective-permute-done.1), channel_id=1, source_target_pairs={{0,1},{1,2},{2,3},{3,0},{4,5},{5,6},{6,7},{7,4},{8,9},{9,10},{10,1... | collective-permute-start | bytes 1572872 | tf_op jit(solution)/shard_map/ppermute | solution.py:222
  62.2 22.5 %collective-permute-start.4 = (bf16[128,2048]{1,0:T(8,128)(2,1)S(1)}, bf16[128,2048]{1,0:T(8,128)(2,1)S(1)}, u32[]{:S(2)}, u32[]{:S(2)}) collective-permute-start(bf16[128,2048]{1,0:T(8,128)(2,1)S(1)} %collective-permute-done.2), channel_id=1, source_target_pairs={{0,1},{1,2},{2,3},{3,0},{4,5},{5,6},{6,7},{7,4},{8,9},{9,10},{10,1... | collective-permute-start | bytes 1572872 | tf_op jit(solution)/shard_map/ppermute | solution.py:222
  73.4 21.8 %collective-permute-start.5 = (bf16[128,2048]{1,0:T(8,128)(2,1)S(1)}, bf16[128,2048]{1,0:T(8,128)(2,1)S(1)}, u32[]{:S(2)}, u32[]{:S(2)}) collective-permute-start(bf16[128,2048]{1,0:T(8,128)(2,1)S(1)} %collective-permute-done.3), channel_id=1, source_target_pairs={{0,1},{1,2},{2,3},{3,0},{4,5},{5,6},{6,7},{7,4},{8,9},{9,10},{10,1... | collective-permute-start | bytes 1572872 | tf_op jit(solution)/shard_map/ppermute | solution.py:222
  95.3 26.3 %collective-permute-start.13 = (bf16[256,2048]{1,0:T(8,128)(2,1)S(1)}, bf16[256,2048]{1,0:T(8,128)(2,1)S(1)}, u32[]{:S(2)}, u32[]{:S(2)}) collective-permute-start(bf16[256,2048]{1,0:T(8,128)(2,1)S(1)} %convert_element_type.308.refs_1_), channel_id=1, source_target_pairs={{0,1},{1,2},{2,3},{3,0},{4,5},{5,6},{6,7},{7,4},{8,9},{9,10},{10,1... | collective-permute-start | bytes 3145736 | tf_op jit(solution)/shard_map/ppermute | solution.py:222
  121.6 25.6 %collective-permute-start.16 = (bf16[256,2048]{1,0:T(8,128)(2,1)S(1)}, bf16[256,2048]{1,0:T(8,128)(2,1)}, u32[]{:S(2)}, u32[]{:S(2)}) collective-permute-start(bf16[256,2048]{1,0:T(8,128)(2,1)S(1)} %collective-permute-done.13.refs_1_), channel_id=1, source_target_pairs={{0,1},{1,2},{2,3},{3,0},{4,5},{5,6},{6,7},{7,4},{8,9},{9,10},{10,1... | collective-permute-start | bytes 3145736 | tf_op jit(solution)/shard_map/ppermute | solution.py:222
  147.2 191.7 %collective-permute-start.19 = (bf16[256,2048]{1,0:T(8,128)(2,1)}, bf16[256,2048]{1,0:T(8,128)(2,1)}, u32[]{:S(2)}, u32[]{:S(2)}) collective-permute-start(bf16[256,2048]{1,0:T(8,128)(2,1)} %collective-permute-done.16.refs_1_), channel_id=1, source_target_pairs={{0,1},{1,2},{2,3},{3,0},{4,5},{5,6},{6,7},{7,4},{8,9},{9,10},{10,1... | collective-permute-start | bytes 3145736 | tf_op jit(solution)/shard_map/ppermute | solution.py:222
  192.0 53.1 %copy-start.44 = (bf16[1024,2,4,64]{0,3,2,1:T(8,128)(2,1)}, bf16[1024,2,4,64]{0,3,2,1:T(8,128)(2,1)S(1)}, u32[]{:S(2)}) copy-start(bf16[1024,2,4,64]{0,3,2,1:T(8,128)(2,1)S(1)} %pad_maximum_fusion.4) | copy-start | bytes 3145732
  194.5 16.6 %collective-permute-start.6 = (bf16[128,2048]{1,0:T(8,128)(2,1)S(1)}, bf16[128,2048]{1,0:T(8,128)(2,1)S(1)}, u32[]{:S(2)}, u32[]{:S(2)}) collective-permute-start(bf16[128,2048]{1,0:T(8,128)(2,1)S(1)} %convolution_convert_fusion.6), channel_id=1, source_target_pairs={{0,1},{1,2},{2,3},{3,0},{4,5},{5,6},{6,7},{7,4},{8,9},{9,10},{10,1... | collective-permute-start | bytes 1572872 | tf_op jit(solution)/shard_map/ppermute | solution.py:222
  195.1 27.3 %collective-permute-start.9 = (bf16[128,2048]{1,0:T(8,128)(2,1)S(1)}, bf16[128,2048]{1,0:T(8,128)(2,1)S(1)}, u32[]{:S(2)}, u32[]{:S(2)}) collective-permute-start(bf16[128,2048]{1,0:T(8,128)(2,1)S(1)} %convolution_convert_fusion.5), channel_id=1, source_target_pairs={{0,1},{1,2},{2,3},{3,0},{4,5},{5,6},{6,7},{7,4},{8,9},{9,10},{10,1... | collective-permute-start | bytes 1572872 | tf_op jit(solution)/shard_map/ppermute | solution.py:222
  211.7 22.0 %collective-permute-start.7 = (bf16[128,2048]{1,0:T(8,128)(2,1)S(1)}, bf16[128,2048]{1,0:T(8,128)(2,1)S(1)}, u32[]{:S(2)}, u32[]{:S(2)}) collective-permute-start(bf16[128,2048]{1,0:T(8,128)(2,1)S(1)} %add_convert_fusion.12), channel_id=1, source_target_pairs={{0,1},{1,2},{2,3},{3,0},{4,5},{5,6},{6,7},{7,4},{8,9},{9,10},{10,1... | collective-permute-start | bytes 1572872 | tf_op jit(solution)/shard_map/ppermute | solution.py:222
  222.9 22.0 %collective-permute-start.10 = (bf16[128,2048]{1,0:T(8,128)(2,1)S(1)}, bf16[128,2048]{1,0:T(8,128)(2,1)S(1)}, u32[]{:S(2)}, u32[]{:S(2)}) collective-permute-start(bf16[128,2048]{1,0:T(8,128)(2,1)S(1)} %add_convert_fusion.10), channel_id=1, source_target_pairs={{0,1},{1,2},{2,3},{3,0},{4,5},{5,6},{6,7},{7,4},{8,9},{9,10},{10,1... | collective-permute-start | bytes 1572872 | tf_op jit(solution)/shard_map/ppermute | solution.py:222
  233.8 22.4 %collective-permute-start.8 = (bf16[128,2048]{1,0:T(8,128)(2,1)S(1)}, bf16[128,2048]{1,0:T(8,128)(2,1)S(1)}, u32[]{:S(2)}, u32[]{:S(2)}) collective-permute-start(bf16[128,2048]{1,0:T(8,128)(2,1)S(1)} %add_convert_fusion.11), channel_id=1, source_target_pairs={{0,1},{1,2},{2,3},{3,0},{4,5},{5,6},{6,7},{7,4},{8,9},{9,10},{10,1... | collective-permute-start | bytes 1572872 | tf_op jit(solution)/shard_map/ppermute | solution.py:222
  245.0 19.3 %collective-permute-start.11 = (bf16[128,2048]{1,0:T(8,128)(2,1)S(1)}, bf16[128,2048]{1,0:T(8,128)(2,1)S(1)}, u32[]{:S(2)}, u32[]{:S(2)}) collective-permute-start(bf16[128,2048]{1,0:T(8,128)(2,1)S(1)} %add_convert_fusion.9), channel_id=1, source_target_pairs={{0,1},{1,2},{2,3},{3,0},{4,5},{5,6},{6,7},{7,4},{8,9},{9,10},{10,1... | collective-permute-start | bytes 1572872 | tf_op jit(solution)/shard_map/ppermute | solution.py:222
  266.2 24.2 %collective-permute-start.12 = (bf16[256,2048]{1,0:T(8,128)(2,1)}, bf16[256,2048]{1,0:T(8,128)(2,1)}, u32[]{:S(2)}, u32[]{:S(2)}) collective-permute-start(bf16[256,2048]{1,0:T(8,128)(2,1)} %multiply_convert_fusion.refs_0_), channel_id=1, source_target_pairs={{0,1},{1,2},{2,3},{3,0},{4,5},{5,6},{6,7},{7,4},{8,9},{9,10},{10,1... | collective-permute-start | bytes 3145736 | tf_op jit(solution)/shard_map/ppermute | solution.py:222
  290.5 24.5 %collective-permute-start.15 = (bf16[256,2048]{1,0:T(8,128)(2,1)}, bf16[256,2048]{1,0:T(8,128)(2,1)S(1)}, u32[]{:S(2)}, u32[]{:S(2)}) collective-permute-start(bf16[256,2048]{1,0:T(8,128)(2,1)} %collective-permute-done.12.refs_0_), channel_id=1, source_target_pairs={{0,1},{1,2},{2,3},{3,0},{4,5},{5,6},{6,7},{7,4},{8,9},{9,10},{10,1... | collective-permute-start | bytes 3145736 | tf_op jit(solution)/shard_map/ppermute | solution.py:222
  314.9 23.9 %collective-permute-start.18 = (bf16[256,2048]{1,0:T(8,128)(2,1)S(1)}, bf16[256,2048]{1,0:T(8,128)(2,1)S(1)}, u32[]{:S(2)}, u32[]{:S(2)}) collective-permute-start(bf16[256,2048]{1,0:T(8,128)(2,1)S(1)} %collective-permute-done.15.refs_0_), channel_id=1, source_target_pairs={{0,1},{1,2},{2,3},{3,0},{4,5},{5,6},{6,7},{7,4},{8,9},{9,10},{10,1... | collective-permute-start | bytes 3145736 | tf_op jit(solution)/shard_map/ppermute | solution.py:222
  398.0 301.0 %reduce-scatter.5.cloned.1.call-start = ((), (), s32[]{:S(2)}) async-start(), calls=%async_computation.5 | async-start | bytes 5898240 | tf_op jit(solution)/shard_map/reduce_scatter | solution.py:424
  398.1 48.3 %copy-start.12 = (f32[256,2048]{1,0:T(8,128)S(1)}, f32[256,2048]{1,0:T(8,128)}, u32[]{:S(2)}) copy-start(f32[256,2048]{1,0:T(8,128)} %copy-done.11) | copy-start | bytes 6291460
  400.0 23.0 %collective-permute-start.14 = (bf16[256,2048]{1,0:T(8,128)(2,1)S(1)}, bf16[256,2048]{1,0:T(8,128)(2,1)S(1)}, u32[]{:S(2)}, u32[]{:S(2)}) collective-permute-start(bf16[256,2048]{1,0:T(8,128)(2,1)S(1)} %convert_element_type.309), channel_id=1, source_target_pairs={{0,1},{1,2},{2,3},{3,0},{4,5},{5,6},{6,7},{7,4},{8,9},{9,10},{10,1... | collective-permute-start | bytes 3145736 | tf_op jit(solution)/shard_map/ppermute | solution.py:222
  423.3 44.4 %copy-start.20 = (bf16[256,2048]{1,0:T(8,128)(2,1)S(1)}, bf16[256,2048]{1,0:T(8,128)(2,1)}, u32[]{:S(2)}) copy-start(bf16[256,2048]{1,0:T(8,128)(2,1)} %param.10) | copy-start | bytes 3145732
  423.3 44.4 %copy-start.24 = (f32[128,2048]{1,0:T(8,128)S(1)}, f32[128,2048]{1,0:T(8,128)}, u32[]{:S(2)}) copy-start(f32[128,2048]{1,0:T(8,128)} %copy-done.23) | copy-start | bytes 3145732
  423.3 23.0 %collective-permute-start.17 = (bf16[256,2048]{1,0:T(8,128)(2,1)S(1)}, bf16[256,2048]{1,0:T(8,128)(2,1)S(1)}, u32[]{:S(2)}, u32[]{:S(2)}) collective-permute-start(bf16[256,2048]{1,0:T(8,128)(2,1)S(1)} %add_convert_fusion.3), channel_id=1, source_target_pairs={{0,1},{1,2},{2,3},{3,0},{4,5},{5,6},{6,7},{7,4},{8,9},{9,10},{10,1... | collective-permute-start | bytes 3145736 | tf_op jit(solution)/shard_map/ppermute | solution.py:222
  446.6 21.1 %collective-permute-start.20 = (bf16[256,2048]{1,0:T(8,128)(2,1)S(1)}, bf16[256,2048]{1,0:T(8,128)(2,1)S(1)}, u32[]{:S(2)}, u32[]{:S(2)}) collective-permute-start(bf16[256,2048]{1,0:T(8,128)(2,1)S(1)} %add_convert_fusion.2), channel_id=1, source_target_pairs={{0,1},{1,2},{2,3},{3,0},{4,5},{5,6},{6,7},{7,4},{8,9},{9,10},{10,1... | collective-permute-start | bytes 3145736 | tf_op jit(solution)/shard_map/ppermute | solution.py:222
  472.7 23.0 %collective-permute-start.21 = (bf16[256,2048]{1,0:T(8,128)(2,1)S(1)}, bf16[256,2048]{1,0:T(8,128)(2,1)}, u32[]{:S(2)}, u32[]{:S(2)}) collective-permute-start(bf16[256,2048]{1,0:T(8,128)(2,1)S(1)} %get-tuple-element.89), channel_id=1, source_target_pairs={{0,1},{1,2},{2,3},{3,0},{4,5},{5,6},{6,7},{7,4},{8,9},{9,10},{10,1... | collective-permute-start | bytes 3145736 | tf_op jit(solution)/shard_map/ppermute | solution.py:222
  495.6 23.5 %collective-permute-start.22 = (bf16[256,2048]{1,0:T(8,128)(2,1)}, bf16[256,2048]{1,0:T(8,128)(2,1)}, u32[]{:S(2)}, u32[]{:S(2)}) collective-permute-start(bf16[256,2048]{1,0:T(8,128)(2,1)} %collective-permute-done.21), channel_id=1, source_target_pairs={{0,1},{1,2},{2,3},{3,0},{4,5},{5,6},{6,7},{7,4},{8,9},{9,10},{10,1... | collective-permute-start | bytes 3145736 | tf_op jit(solution)/shard_map/ppermute | solution.py:222
  519.1 22.2 %collective-permute-start.23 = (bf16[256,2048]{1,0:T(8,128)(2,1)}, bf16[256,2048]{1,0:T(8,128)(2,1)}, u32[]{:S(2)}, u32[]{:S(2)}) collective-permute-start(bf16[256,2048]{1,0:T(8,128)(2,1)} %collective-permute-done.22), channel_id=1, source_target_pairs={{0,1},{1,2},{2,3},{3,0},{4,5},{5,6},{6,7},{7,4},{8,9},{9,10},{10,1... | collective-permute-start | bytes 3145736 | tf_op jit(solution)/shard_map/ppermute | solution.py:222
  542.4 21.7 %collective-permute-start.24 = (bf16[256,2048]{1,0:T(8,128)(2,1)}, bf16[256,2048]{1,0:T(8,128)(2,1)}, u32[]{:S(2)}, u32[]{:S(2)}) collective-permute-start(bf16[256,2048]{1,0:T(8,128)(2,1)} %convert_element_type.316), channel_id=1, source_target_pairs={{0,1},{1,2},{2,3},{3,0},{4,5},{5,6},{6,7},{7,4},{8,9},{9,10},{10,1... | collective-permute-start | bytes 3145736 | tf_op jit(solution)/shard_map/ppermute | solution.py:222
  565.7 23.5 %collective-permute-start.25 = (bf16[256,2048]{1,0:T(8,128)(2,1)S(1)}, bf16[256,2048]{1,0:T(8,128)(2,1)S(1)}, u32[]{:S(2)}, u32[]{:S(2)}) collective-permute-start(bf16[256,2048]{1,0:T(8,128)(2,1)S(1)} %add_convert_fusion.1), channel_id=1, source_target_pairs={{0,1},{1,2},{2,3},{3,0},{4,5},{5,6},{6,7},{7,4},{8,9},{9,10},{10,1... | collective-permute-start | bytes 3145736 | tf_op jit(solution)/shard_map/ppermute | solution.py:222
  605.0 16.6 %collective-permute-start.27 = (bf16[128,2048]{1,0:T(8,128)(2,1)S(1)}, bf16[128,2048]{1,0:T(8,128)(2,1)S(1)}, u32[]{:S(2)}, u32[]{:S(2)}) collective-permute-start(bf16[128,2048]{1,0:T(8,128)(2,1)S(1)} %convolution_convert_fusion.4), channel_id=1, source_target_pairs={{0,1},{1,2},{2,3},{3,0},{4,5},{5,6},{6,7},{7,4},{8,9},{9,10},{10,1... | collective-permute-start | bytes 1572872 | tf_op jit(solution)/shard_map/ppermute | solution.py:222
  608.1 24.8 %collective-permute-start.30 = (bf16[128,2048]{1,0:T(8,128)(2,1)S(1)}, bf16[128,2048]{1,0:T(8,128)(2,1)S(1)}, u32[]{:S(2)}, u32[]{:S(2)}) collective-permute-start(bf16[128,2048]{1,0:T(8,128)(2,1)S(1)} %convolution_convert_fusion.3), channel_id=1, source_target_pairs={{0,1},{1,2},{2,3},{3,0},{4,5},{5,6},{6,7},{7,4},{8,9},{9,10},{10,1... | collective-permute-start | bytes 1572872 | tf_op jit(solution)/shard_map/ppermute | solution.py:222
  622.8 21.3 %collective-permute-start.28 = (bf16[128,2048]{1,0:T(8,128)(2,1)S(1)}, bf16[128,2048]{1,0:T(8,128)(2,1)S(1)}, u32[]{:S(2)}, u32[]{:S(2)}) collective-permute-start(bf16[128,2048]{1,0:T(8,128)(2,1)S(1)} %add_convert_fusion.7), channel_id=1, source_target_pairs={{0,1},{1,2},{2,3},{3,0},{4,5},{5,6},{6,7},{7,4},{8,9},{9,10},{10,1... | collective-permute-start | bytes 1572872 | tf_op jit(solution)/shard_map/ppermute | solution.py:222
  634.1 17.5 %collective-permute-start.31 = (bf16[128,2048]{1,0:T(8,128)(2,1)S(1)}, bf16[128,2048]{1,0:T(8,128)(2,1)S(1)}, u32[]{:S(2)}, u32[]{:S(2)}) collective-permute-start(bf16[128,2048]{1,0:T(8,128)(2,1)S(1)} %add_convert_fusion.5), channel_id=1, source_target_pairs={{0,1},{1,2},{2,3},{3,0},{4,5},{5,6},{6,7},{7,4},{8,9},{9,10},{10,1... | collective-permute-start | bytes 1572872 | tf_op jit(solution)/shard_map/ppermute | solution.py:222
  645.3 11.9 %collective-permute-start.29 = (bf16[128,2048]{1,0:T(8,128)(2,1)S(1)}, bf16[128,2048]{1,0:T(8,128)(2,1)S(1)}, u32[]{:S(2)}, u32[]{:S(2)}) collective-permute-start(bf16[128,2048]{1,0:T(8,128)(2,1)S(1)} %add_convert_fusion.6), channel_id=1, source_target_pairs={{0,1},{1,2},{2,3},{3,0},{4,5},{5,6},{6,7},{7,4},{8,9},{9,10},{10,1... | collective-permute-start | bytes 1572872 | tf_op jit(solution)/shard_map/ppermute | solution.py:222
  652.7 16.1 %collective-permute-start.32 = (bf16[128,2048]{1,0:T(8,128)(2,1)S(1)}, bf16[128,2048]{1,0:T(8,128)(2,1)S(1)}, u32[]{:S(2)}, u32[]{:S(2)}) collective-permute-start(bf16[128,2048]{1,0:T(8,128)(2,1)S(1)} %add_convert_fusion.4), channel_id=1, source_target_pairs={{0,1},{1,2},{2,3},{3,0},{4,5},{5,6},{6,7},{7,4},{8,9},{9,10},{10,1... | collective-permute-start | bytes 1572872 | tf_op jit(solution)/shard_map/ppermute | solution.py:222
  675.4 17.0 %collective-permute-start.26 = (bf16[256,2048]{1,0:T(8,128)(2,1)}, bf16[256,2048]{1,0:T(8,128)(2,1)}, u32[]{:S(2)}, u32[]{:S(2)}) collective-permute-start(bf16[256,2048]{1,0:T(8,128)(2,1)} %add_convert_fusion), channel_id=1, source_target_pairs={{0,1},{1,2},{2,3},{3,0},{4,5},{5,6},{6,7},{7,4},{8,9},{9,10},{10,1... | collective-permute-start | bytes 3145736 | tf_op jit(solution)/shard_map/ppermute | solution.py:222
  700.4 7.6 %collective-permute-start.33 = (f32[2,256]{1,0:T(2,128)S(1)}, f32[2,256]{1,0:T(2,128)S(1)}, u32[]{:S(2)}, u32[]{:S(2)}) collective-permute-start(f32[2,256]{1,0:T(2,128)S(1)} %maximum_divide_fusion), channel_id=1, source_target_pairs={{0,1},{1,2},{2,3},{3,0},{4,5},{5,6},{6,7},{7,4},{8,9},{9,10},{10,1... | collective-permute-start | bytes 6152 | tf_op jit(solution)/shard_map/ppermute | solution.py:437
  700.5 7.5 %collective-permute-start.34 = (f32[2,256]{1,0:T(2,128)S(1)}, f32[2,256]{1,0:T(2,128)S(1)}, u32[]{:S(2)}, u32[]{:S(2)}) collective-permute-start(f32[2,256]{1,0:T(2,128)S(1)} %maximum_divide_fusion), channel_id=1, source_target_pairs={{0,2},{1,3},{2,0},{3,1},{4,6},{5,7},{6,4},{7,5},{8,10},{9,11},{10,... | collective-permute-start | bytes 6152 | tf_op jit(solution)/shard_map/ppermute | solution.py:437
  700.5 7.4 %collective-permute-start.35 = (f32[2,256]{1,0:T(2,128)S(1)}, f32[2,256]{1,0:T(2,128)S(1)}, u32[]{:S(2)}, u32[]{:S(2)}) collective-permute-start(f32[2,256]{1,0:T(2,128)S(1)} %maximum_divide_fusion), channel_id=1, source_target_pairs={{0,3},{1,0},{2,1},{3,2},{4,7},{5,4},{6,5},{7,6},{8,11},{9,8},{10,9... | collective-permute-start | bytes 6152 | tf_op jit(solution)/shard_map/ppermute | solution.py:437
  (71 other events, 518.8 us)
Sparse Core Ops, SparseCore 0:
  10.7 34.8 all-gather.5
  47.5 28.0 all-gather.9
  77.5 125.1 all-gather.7
  398.1 156.5 reduce-scatter.2
  601.1 57.0 reduce-scatter.4
